TPU v7x, 128 devices: a whole 4x4x4 slice. The times are simulated.
128 devices in a mesh: grp: 4 (over y), tile: 32 (over x, z, core).
Axes of the slice: x: 4, y: 4, z: 4, core: 2. Of those that a mesh axis runs over, the one named last changes fastest.
Arguments:
- base_rhs: float32 [1024, 16384], P('grp', 'tile'), may hold values from -6 to 6
- depth: float32 [1024, 16384], P('grp', 'tile'), may hold values from 0.25 to 2
- ssh_prev: float32 [1024, 16384], P('grp', 'tile'), may hold values from -6 to 6
- currents: float32 [2, 1024, 16384], P(None, 'grp', 'tile'), may hold values from -3 to 3
- land_blocks: int32 [128, 2048], P('grp', 'tile'), may hold values 0 or 1
- ice_thick: float32 [2, 256, 16384], P(None, 'grp', 'tile'), may hold values from 0.25 to 4
- ice_blocks: int32 [2, 32, 2048], P(None, 'grp', 'tile'), may hold values 0 or 1
- ice_vel: float32 [2, 2, 256, 16384], P(None, None, 'grp', 'tile'), may hold values from -3 to 3
- ice_stress: float32 [3, 2, 256, 16384], P(None, None, 'grp', 'tile'), may hold values from -5 to 5
- wind: float32 [2, 2, 256, 16384], P(None, None, 'grp', 'tile'), may hold values from -6 to 6
Outputs:
- ssh: float32 [1024, 16384], P('grp', 'tile')
- ice_vel_out: float32 [2, 2, 256, 16384], P(None, None, 'grp', 'tile')
- ice_stress_out: float32 [3, 2, 256, 16384], P(None, None, 'grp', 'tile')
All inputs are finite; a program needn't handle non-finite values. No bound on the sum of `land_blocks` or of `ice_blocks` on one device may be relied on, other than what follows from the above.
Results may differ from a plain program's by a relative error of at most 0.0001.
Values sent between devices are 32-bit elements; how exact they have to be, the bound alone decides.
A program may use at most 64 MiB of HBM per device.

v0:
```python
import jax
import jax.numpy as jnp
from jax import lax
from jax.sharding import Mesh
from jax.sharding import PartitionSpec as P

BS = 8
NSUB = 8
ITERS = 3
GRP_TILE = ("grp", "tile_0", "tile_1", "tile_2")
TILE = ("tile_0", "tile_1", "tile_2")


DAMP = 0.05
RELAX = 0.2
STRENGTH = 0.5
DRAG = 1.0
STEP = 0.5


def with_halo(array, sides, width):
    edges = {}
    for axis, dim in sides:
        devices, length = (lax.axis_size(axis), array.shape[dim])
        up = [(i, (i + 1) % devices) for i in range(devices - 1)]
        last = lax.slice_in_dim(array, length - width, length, axis=dim)
        first = lax.slice_in_dim(array, 0, width, axis=dim)
        edges[dim] = (
            lax.ppermute(last, axis, up),
            lax.ppermute(first, axis, [(b, a) for a, b in up]),
        )
    done = []
    for _, dim in sides:
        low, high = edges[dim]
        around = [(width, width) if d in done else (0, 0) for d in range(array.ndim)]
        array = jnp.concatenate([jnp.pad(low, around), array, jnp.pad(high, around)], axis=dim)
        done.append(dim)
    return array


def by_axis(array, axes):
    for axis in axes:
        array = lax.psum(array, axis)
    return array


def extended(array, sides, width):
    for axis, dim in sides:
        devices, length = (lax.axis_size(axis), array.shape[dim])
        up = [(i, (i + 1) % devices) for i in range(devices - 1)]
        down = [(j, i) for i, j in up]
        last = lax.slice_in_dim(array, length - width, length, axis=dim)
        first = lax.slice_in_dim(array, 0, width, axis=dim)
        before = lax.ppermute(last, axis, up)
        after = lax.ppermute(first, axis, down)
        array = jnp.concatenate([before, array, after], axis=dim)
    return array


def strain_rates(u_pad, v_pad):
    du_dx = u_pad[..., 1:, :-1] - u_pad[..., :-1, :-1]
    du_dy = u_pad[..., :-1, 1:] - u_pad[..., :-1, :-1]
    dv_dx = v_pad[..., 1:, :-1] - v_pad[..., :-1, :-1]
    dv_dy = v_pad[..., :-1, 1:] - v_pad[..., :-1, :-1]
    return (du_dx + dv_dy, du_dx - dv_dy, du_dy + dv_dx)


def relax_stress(previous, strength, div_rate, tens_rate, shear_rate):
    deformation = jnp.sqrt(
        div_rate * div_rate + tens_rate * tens_rate + shear_rate * shear_rate + 1.0
    )
    relax_scale = 1.0 / (1.0 + RELAX)
    div_part = (previous[0] + RELAX * strength * (div_rate / deformation - 1.0)) * relax_scale
    tens_part = (previous[1] + RELAX * strength * tens_rate / deformation) * relax_scale
    shear_part = (previous[2] + RELAX * strength * shear_rate / deformation) * relax_scale
    return jnp.stack([div_part, tens_part, shear_part])


def along_rows(field):
    return field[..., 1:, 1:] - field[..., :-1, 1:]


def along_cols(field):
    return field[..., 1:, 1:] - field[..., 1:, :-1]


def stress_force(stress_pad):
    force_x = 0.5 * along_rows(stress_pad[0] + stress_pad[1]) + along_cols(stress_pad[2])
    force_y = 0.5 * along_cols(stress_pad[0] - stress_pad[1]) + along_rows(stress_pad[2])
    return jnp.stack([force_x, force_y])


def momentum(velocity, force, ice_mass, ice_cover, wind, ocean_flow):
    return (
        ice_cover
        * (ice_mass * velocity + STEP * (force + wind + DRAG * ocean_flow))
        / (ice_mass + STEP * DRAG)
    )


def face_weights(depth_pad):
    centre = depth_pad[1:-1, 1:-1]
    return (
        centre * depth_pad[2:, 1:-1],
        centre * depth_pad[:-2, 1:-1],
        centre * depth_pad[1:-1, 2:],
        centre * depth_pad[1:-1, :-2],
    )


def apply_operator(field_pad, weights):
    field = field_pad[1:-1, 1:-1]
    north_weight, south_weight, east_weight, west_weight = weights
    return (
        DAMP * field
        + north_weight * (field - field_pad[2:, 1:-1])
        + south_weight * (field - field_pad[:-2, 1:-1])
        + east_weight * (field - field_pad[1:-1, 2:])
        + west_weight * (field - field_pad[1:-1, :-2])
    )


def expand(blocks):
    return jnp.repeat(jnp.repeat(blocks, BS, axis=-2), BS, axis=-1).astype(jnp.float32)


def operate(field, weights):
    field_pad = with_halo(field, (("grp", 0), (TILE, 1)), 1)
    return apply_operator(field_pad, weights)


def pair_sums(residual, precond, applied):
    return (
        by_axis(jnp.sum(residual * precond), GRP_TILE),
        by_axis(jnp.sum(precond * applied), GRP_TILE),
    )


def local_subcycle(velocity, stress, strength, ice_mass, ice_cover, wind, ocean_flow):
    vel_pad = jnp.pad(velocity, ((0, 0), (0, 0), (1, 1), (1, 1)))
    strain = strain_rates(vel_pad[0], vel_pad[1])
    stress = relax_stress(
        stress, strength, strain[0][:, 1:, 1:], strain[1][:, 1:, 1:], strain[2][:, 1:, 1:]
    )
    stress_pad = jnp.pad(stress, ((0, 0), (0, 0), (1, 0), (1, 0)))
    velocity = momentum(velocity, stress_force(stress_pad), ice_mass, ice_cover, wind, ocean_flow)
    return (velocity, stress)


def shards(
    base_rhs,
    depth,
    ssh_prev,
    currents,
    land_blocks,
    ice_thick,
    ice_blocks,
    ice_vel,
    ice_stress,
    wind,
):
    groups = lax.axis_size("grp")
    grp_index = lax.axis_index("grp")
    ocean_cols = base_rhs.shape[1]
    ice_rows = ice_thick.shape[1]
    cap_rows = ice_rows * groups
    wet_cells = expand(land_blocks)
    ice_cover = expand(ice_blocks)
    at_north = (grp_index == 0).astype(jnp.float32)
    at_south = (grp_index == groups - 1).astype(jnp.float32)
    outgoing = jnp.stack([currents * at_north, currents * at_south], axis=1)
    outgoing = outgoing.reshape(2, 2, groups, ice_rows, ocean_cols)
    incoming = lax.all_to_all(outgoing, "grp", split_axis=2, concat_axis=2, tiled=True)
    ocean_flow = jnp.sum(incoming, axis=2)
    strength = STRENGTH * ice_thick * ice_cover
    ice_mass = ice_thick * ice_cover + 1.0
    velocity = ice_vel
    stress = ice_stress
    bundle = jnp.concatenate(
        [velocity, stress, wind, ocean_flow, strength[None], ice_mass[None], ice_cover[None]],
        axis=0,
    )
    widened = extended(bundle, (("grp", 2), (TILE, 3)), NSUB)
    wide_vel = widened[0:2]
    wide_stress = widened[2:5]
    wide_wind = widened[5:7]
    wide_flow = widened[7:9]
    wide_strength = widened[9]
    wide_mass = widened[10]
    wide_cover = widened[11]
    for subcycle in range(NSUB):
        wide_vel, wide_stress = local_subcycle(
            wide_vel, wide_stress, wide_strength, wide_mass, wide_cover, wide_wind, wide_flow
        )
    velocity = wide_vel[:, :, NSUB : NSUB + ice_rows, NSUB : NSUB + ocean_cols]
    stress = wide_stress[:, :, NSUB : NSUB + ice_rows, NSUB : NSUB + ocean_cols]
    ice_drag = DRAG * ice_cover * (velocity - ocean_flow)
    empty_slot = jnp.zeros_like(ice_drag[:, 0])
    parcel = jnp.stack([ice_drag[:, 0]] + [empty_slot] * (groups - 2) + [ice_drag[:, 1]], axis=1)
    returned = lax.all_to_all(parcel, "grp", split_axis=1, concat_axis=1, tiled=True).reshape(
        2, cap_rows, ocean_cols
    )
    ocean_drag = jnp.where(
        grp_index == 0, returned, jnp.where(grp_index == groups - 1, returned, 0.0)
    )
    forcing_pad = with_halo(
        jnp.stack([ocean_drag[0], ocean_drag[1], depth * wet_cells]), (("grp", 1), (TILE, 2)), 1
    )
    spread = (
        forcing_pad[0, 1:-1, 1:-1]
        - forcing_pad[0, :-2, 1:-1]
        + (forcing_pad[1, 1:-1, 1:-1] - forcing_pad[1, 1:-1, :-2])
    )
    forcing = wet_cells * (base_rhs + spread)
    weights = face_weights(forcing_pad[2])
    diagonal = DAMP + weights[0] + weights[1] + weights[2] + weights[3]
    solution = ssh_prev
    residual = forcing - operate(solution, weights)
    precond = residual / diagonal
    applied = operate(precond, weights)
    precond_norm, curvature_sum = pair_sums(residual, precond, applied)
    step_size = precond_norm / curvature_sum
    direction = precond
    search_image = applied
    for iteration in range(ITERS):
        solution = solution + step_size * direction
        residual = residual - step_size * search_image
        if iteration + 1 < ITERS:
            precond = residual / diagonal
            applied = operate(precond, weights)
            norm_next, curvature_sum = pair_sums(residual, precond, applied)
            beta_ratio = norm_next / precond_norm
            step_size = norm_next / (curvature_sum - beta_ratio * norm_next / step_size)
            direction = precond + beta_ratio * direction
            search_image = applied + beta_ratio * search_image
            precond_norm = norm_next
    return (solution, velocity, stress)


def solution(mesh):
    finer = Mesh(
        mesh.devices.reshape(mesh.shape["grp"], 4, 4, 2), ("grp", "tile_0", "tile_1", "tile_2")
    )
    return jax.shard_map(
        shards,
        mesh=finer,
        in_specs=(
            P("grp", TILE),
            P("grp", TILE),
            P("grp", TILE),
            P(None, "grp", TILE),
            P("grp", TILE),
            P(None, "grp", TILE),
            P(None, "grp", TILE),
            P(None, None, "grp", TILE),
            P(None, None, "grp", TILE),
            P(None, None, "grp", TILE),
        ),
        out_specs=(P("grp", TILE), P(None, None, "grp", TILE), P(None, None, "grp", TILE)),
        check_vma=False,
    )
```

profile of v0, /device:TPU:1, one launch (start us, length us, event | category | flops | bytes accessed | tf_op | source)
XLA Modules:
  0.0 336.4 jit_solution(16348324338508460184)
XLA Ops:
  0.6 1.5 broadcast_multiply_fusion.1
  2.4 1.6 copy.115
  3.9 5.1 %all-to-all-start = ((f32[2,2,4,64,512]{4,3,0,1,2:T(8,128)}), f32[2,2,4,64,512]{4,3,0,1,2:T(8,128)}, u32[]{:S(2)}, u32[]{:S(2)}) async-start(f32[2,2,4,64,512]{4,3,0,1,2:T(8,128)} %copy.115), calls=%async_computation | async-start | bytes 4194304 | tf_op jit(solution)/shard_map/all_to_all | solution.py:173
  12.7 22.3 %all-to-all-done = f32[2,2,4,64,512]{4,3,0,1,2:T(8,128)} async-done(((f32[2,2,4,64,512]{4,3,0,1,2:T(8,128)}), f32[2,2,4,64,512]{4,3,0,1,2:T(8,128)}, u32[]{:S(2)}, u32[]{:S(2)}) %all-to-all-start) | async-done | bytes 2097184 | tf_op jit(solution)/shard_map/all_to_all | solution.py:173
  35.0 2.7 reduce_sum.63
  40.0 2.4 collective-permute-start
  42.4 1.3 collective-permute-start.1
  43.7 5.6 %collective-permute-done = f32[12,2,8,512]{3,2,1,0:T(8,128)S(1)} collective-permute-done((f32[12,2,8,512]{3,2,1,0:T(8,128)S(1)}, f32[12,2,8,512]{3,2,1,0:T(8,128)S(1)}, u32[]{:S(2)}, u32[]{:S(2)}) %collective-permute-start) | collective-permute-done | bytes 393248 | tf_op jit(solution)/shard_map/ppermute | solution.py:54
  49.3 3.9 %collective-permute-done.1 = f32[12,2,8,512]{3,2,1,0:T(8,128)S(1)} collective-permute-done((f32[12,2,8,512]{3,2,1,0:T(8,128)S(1)}, f32[12,2,8,512]{3,2,1,0:T(8,128)S(1)}, u32[]{:S(2)}, u32[]{:S(2)}) %collective-permute-start.1) | collective-permute-done | bytes 393248 | tf_op jit(solution)/shard_map/ppermute | solution.py:55
  53.9 1.6 pad_maximum_fusion.6
  55.6 2.1 copy.121
  57.7 6.1 %collective-permute-start.2 = (f32[12,2,80,8]{2,3,1,0:T(8,128)}, f32[12,2,80,8]{2,3,1,0:T(8,128)}, u32[]{:S(2)}, u32[]{:S(2)}) collective-permute-start(f32[12,2,80,8]{2,3,1,0:T(8,128)} %copy.121), channel_id=1, source_target_pairs={{0,1},{1,2},{2,3},{3,4},{4,5},{5,6},{6,7},{7,8},{8,9},{9,10},{10,1... | collective-permute-start | bytes 184328 | tf_op jit(solution)/shard_map/ppermute | solution.py:54
  63.8 2.1 copy.122
  65.9 1.9 collective-permute-start.3
  67.9 2.2 copy.123
  70.1 2.1 collective-permute-done.3
  72.1 2.2 copy.124
  74.3 4.3 %pad_maximum_fusion = f32[12,2,80,528]{3,2,1,0:T(8,128)S(1)} fusion(f32[12,2,80,8]{3,2,1,0:T(8,128)} %copy.124, f32[12,2,8,512]{3,2,1,0:T(8,128)} %copy-done.2, f32[12,2,64,512]{3,2,1,0:T(8,128)S(1)} %constant_dynamic-update-slice_fusion, f32[12,2,8,512]{3,2,1,0:T(8,128)S(1)} %collective-permute-done, f32[12,2,80,8]{3,2,1,0:T(8,128)} %copy.123), kind=kLoop, calls=%fused_computation | loop fusion | flops 4055040 | bytes 8110080 | tf_op jit(solution)/shard_map/concatenate | solution.py:56
  92.1 1.3 add_multiply_fusion.11
  112.4 3.6 %all-to-all-start.1 = ((f32[2,4,64,512]{3,2,0,1:T(8,128)}), f32[2,4,64,512]{3,2,0,1:T(8,128)S(1)}, u32[]{:S(2)}, u32[]{:S(2)}) async-start(f32[2,4,64,512]{3,2,0,1:T(8,128)} %pad_maximum_fusion.3), calls=%async_computation.1 | async-start | bytes 2097152 | tf_op jit(solution)/shard_map/all_to_all | solution.py:200
  116.3 1.9 collective-permute-start.10
  118.3 2.0 copy.138
  121.4 7.6 %all-to-all-done.1 = f32[2,4,64,512]{3,2,0,1:T(8,128)S(1)} async-done(((f32[2,4,64,512]{3,2,0,1:T(8,128)}), f32[2,4,64,512]{3,2,0,1:T(8,128)S(1)}, u32[]{:S(2)}, u32[]{:S(2)}) %all-to-all-start.1) | async-done | bytes 1048608 | tf_op jit(solution)/shard_map/all_to_all | solution.py:200
  130.2 2.5 copy.137
  132.7 1.3 select_select_fusion
  134.0 1.4 fusion.42
  135.4 1.4 copy.139
  136.9 2.2 collective-permute-start.4
  139.1 1.4 copy.141
  140.5 1.3 collective-permute-start.6
  141.8 4.4 %collective-permute-start.5 = (f32[3,256,1]{1,2,0:T(1,128)S(1)}, f32[3,256,1]{1,2,0:T(1,128)S(1)}, u32[]{:S(2)}, u32[]{:S(2)}) collective-permute-start(f32[3,256,1]{1,2,0:T(1,128)S(1)} %get-tuple-element.96), channel_id=1, source_target_pairs={{0,1},{1,2},{2,3},{3,4},{4,5},{5,6},{6,7},{7,8},{8,9},{9,10},{10,1... | collective-permute-start | bytes 9224 | tf_op jit(solution)/shard_map/ppermute | solution.py:29
  146.1 1.9 collective-permute-start.7
  151.5 3.6 %collective-permute-start.11 = (f32[256,1]{0,1:T(1,128)S(1)}, f32[256,1]{0,1:T(1,128)S(1)}, u32[]{:S(2)}, u32[]{:S(2)}) collective-permute-start(f32[256,1]{0,1:T(1,128)S(1)} %get-tuple-element.170), channel_id=1, source_target_pairs={{0,1},{1,2},{2,3},{3,4},{4,5},{5,6},{6,7},{7,8},{8,9},{9,10},{10,1... | collective-permute-start | bytes 3080 | tf_op jit(solution)/shard_map/ppermute | solution.py:29
  157.8 5.6 %collective-permute-start.9 = (f32[1,512]{0,1:T(8,128)}, f32[1,512]{0,1:T(8,128)}, u32[]{:S(2)}, u32[]{:S(2)}) collective-permute-start(f32[1,512]{0,1:T(8,128)} %copy.149), channel_id=1, source_target_pairs={{0,32},{32,64},{64,96},{1,33},{33,65},{65,97},{2,34},{34,66},{66,9... | collective-permute-start | bytes 6152 | tf_op jit(solution)/shard_map/ppermute | solution.py:29
  164.6 1.5 fusion.40
  166.9 1.4 collective-permute-done.9
  168.3 3.4 fusion.196
  171.8 1.3 collective-permute-start.12
  173.1 4.5 %collective-permute-start.13 = (f32[1,512]{0,1:T(8,128)S(1)}, f32[1,512]{0,1:T(8,128)S(1)}, u32[]{:S(2)}, u32[]{:S(2)}) collective-permute-start(f32[1,512]{0,1:T(8,128)S(1)} %get-tuple-element.165), channel_id=1, source_target_pairs={{0,32},{32,64},{64,96},{1,33},{33,65},{65,97},{2,34},{34,66},{66,9... | collective-permute-start | bytes 6152 | tf_op jit(solution)/shard_map/ppermute | solution.py:29
  177.6 2.1 collective-permute-start.14
  179.7 3.7 %collective-permute-start.15 = (f32[256,1]{0,1:T(1,128)S(1)}, f32[256,1]{0,1:T(1,128)S(1)}, u32[]{:S(2)}, u32[]{:S(2)}) collective-permute-start(f32[256,1]{0,1:T(1,128)S(1)} %get-tuple-element.164), channel_id=1, source_target_pairs={{0,1},{1,2},{2,3},{3,4},{4,5},{5,6},{6,7},{7,8},{8,9},{9,10},{10,1... | collective-permute-start | bytes 3080 | tf_op jit(solution)/shard_map/ppermute | solution.py:29
  185.5 9.8 %all-reduce.34 = (f32[]{:T(128)}, f32[]{:T(128)}) all-reduce(f32[]{:T(128)} %get-tuple-element.20, f32[]{:T(128)} %get-tuple-element.19), channel_id=1, replica_groups=mesh['grp'=4,'tile_0'=4,'tile_1'=4,'tile_2'=2] {'grp'}, use_global_device_ids=true, to_apply=%region_2.3 | all-reduce | flops 2 | bytes 16 | tf_op jit(solution)/shard_map/psum | solution.py:43
  195.3 10.2 %all-reduce.31 = (f32[]{:T(128)}, f32[]{:T(128)}) all-reduce(f32[]{:T(128)} %get-tuple-element.37, f32[]{:T(128)} %get-tuple-element.38), channel_id=1, replica_groups=mesh['grp'=4,'tile_0'=4,'tile_1'=4,'tile_2'=2] {'tile_0'}, use_global_device_ids=true, to_apply=%region_3.4 | all-reduce | flops 2 | bytes 16 | tf_op jit(solution)/shard_map/psum | solution.py:43
  205.5 9.1 %all-reduce.28 = (f32[]{:T(128)}, f32[]{:T(128)}) all-reduce(f32[]{:T(128)} %get-tuple-element.31, f32[]{:T(128)} %get-tuple-element.32), channel_id=1, replica_groups=mesh['grp'=4,'tile_0'=4,'tile_1'=4,'tile_2'=2] {'tile_1'}, use_global_device_ids=true, to_apply=%region_4.5 | all-reduce | flops 2 | bytes 16 | tf_op jit(solution)/shard_map/psum | solution.py:43
  214.6 10.6 %all-reduce.37 = (f32[]{:T(128)}, f32[]{:T(128)}) all-reduce(f32[]{:T(128)} %get-tuple-element.25, f32[]{:T(128)} %get-tuple-element.26), channel_id=1, replica_groups=mesh['grp'=4,'tile_0'=4,'tile_1'=4,'tile_2'=2] {'tile_2'}, use_global_device_ids=true, to_apply=%region_5.6 | all-reduce | flops 2 | bytes 16 | tf_op jit(solution)/shard_map/psum | solution.py:43
  227.9 1.3 collective-permute-start.16
  229.2 4.0 %collective-permute-start.17 = (f32[1,512]{0,1:T(8,128)S(1)}, f32[1,512]{0,1:T(8,128)S(1)}, u32[]{:S(2)}, u32[]{:S(2)}) collective-permute-start(f32[1,512]{0,1:T(8,128)S(1)} %get-tuple-element.161), channel_id=1, source_target_pairs={{0,32},{32,64},{64,96},{1,33},{33,65},{65,97},{2,34},{34,66},{66,9... | collective-permute-start | bytes 6152 | tf_op jit(solution)/shard_map/ppermute | solution.py:29
  233.2 2.8 collective-permute-start.18
  236.0 3.5 %collective-permute-start.19 = (f32[256,1]{0,1:T(1,128)S(1)}, f32[256,1]{0,1:T(1,128)S(1)}, u32[]{:S(2)}, u32[]{:S(2)}) collective-permute-start(f32[256,1]{0,1:T(1,128)S(1)} %get-tuple-element.160), channel_id=1, source_target_pairs={{0,1},{1,2},{2,3},{3,4},{4,5},{5,6},{6,7},{7,8},{8,9},{9,10},{10,1... | collective-permute-start | bytes 3080 | tf_op jit(solution)/shard_map/ppermute | solution.py:29
  240.3 2.1 multiply_reduce_fusion.1
  242.4 7.5 %all-reduce.33 = (f32[]{:T(128)}, f32[]{:T(128)}) all-reduce(f32[]{:T(128)} %get-tuple-element.18, f32[]{:T(128)} %get-tuple-element.17), channel_id=1, replica_groups=mesh['grp'=4,'tile_0'=4,'tile_1'=4,'tile_2'=2] {'grp'}, use_global_device_ids=true, to_apply=%region_12.13 | all-reduce | flops 2 | bytes 16 | tf_op jit(solution)/shard_map/psum | solution.py:43
  249.9 7.4 %all-reduce.30 = (f32[]{:T(128)}, f32[]{:T(128)}) all-reduce(f32[]{:T(128)} %get-tuple-element.35, f32[]{:T(128)} %get-tuple-element.36), channel_id=1, replica_groups=mesh['grp'=4,'tile_0'=4,'tile_1'=4,'tile_2'=2] {'tile_0'}, use_global_device_ids=true, to_apply=%region_13.14 | all-reduce | flops 2 | bytes 16 | tf_op jit(solution)/shard_map/psum | solution.py:43
  257.3 9.2 %all-reduce.27 = (f32[]{:T(128)}, f32[]{:T(128)}) all-reduce(f32[]{:T(128)} %get-tuple-element.29, f32[]{:T(128)} %get-tuple-element.30), channel_id=1, replica_groups=mesh['grp'=4,'tile_0'=4,'tile_1'=4,'tile_2'=2] {'tile_1'}, use_global_device_ids=true, to_apply=%region_14.15 | all-reduce | flops 2 | bytes 16 | tf_op jit(solution)/shard_map/psum | solution.py:43
  266.5 10.5 %all-reduce.36 = (f32[]{:T(128)}, f32[]{:T(128)}) all-reduce(f32[]{:T(128)} %get-tuple-element.23, f32[]{:T(128)} %get-tuple-element.24), channel_id=1, replica_groups=mesh['grp'=4,'tile_0'=4,'tile_1'=4,'tile_2'=2] {'tile_2'}, use_global_device_ids=true, to_apply=%region_15.16 | all-reduce | flops 2 | bytes 16 | tf_op jit(solution)/shard_map/psum | solution.py:43
  281.5 1.3 fusion.193
  283.0 1.4 collective-permute-start.20
  284.5 4.0 %collective-permute-start.21 = (f32[1,512]{0,1:T(8,128)S(1)}, f32[1,512]{0,1:T(8,128)S(1)}, u32[]{:S(2)}, u32[]{:S(2)}) collective-permute-start(f32[1,512]{0,1:T(8,128)S(1)} %get-tuple-element.157), channel_id=1, source_target_pairs={{0,32},{32,64},{64,96},{1,33},{33,65},{65,97},{2,34},{34,66},{66,9... | collective-permute-start | bytes 6152 | tf_op jit(solution)/shard_map/ppermute | solution.py:29
  288.5 2.8 collective-permute-start.22
  291.3 3.5 %collective-permute-start.23 = (f32[256,1]{0,1:T(1,128)S(1)}, f32[256,1]{0,1:T(1,128)S(1)}, u32[]{:S(2)}, u32[]{:S(2)}) collective-permute-start(f32[256,1]{0,1:T(1,128)S(1)} %get-tuple-element.156), channel_id=1, source_target_pairs={{0,1},{1,2},{2,3},{3,4},{4,5},{5,6},{6,7},{7,8},{8,9},{9,10},{10,1... | collective-permute-start | bytes 3080 | tf_op jit(solution)/shard_map/ppermute | solution.py:29
  296.9 1.3 fusion.50
  298.2 7.2 %all-reduce.32 = (f32[]{:T(128)}, f32[]{:T(128)}) all-reduce(f32[]{:T(128)} %get-tuple-element.16, f32[]{:T(128)} %get-tuple-element.15), channel_id=1, replica_groups=mesh['grp'=4,'tile_0'=4,'tile_1'=4,'tile_2'=2] {'grp'}, use_global_device_ids=true, to_apply=%region_22.23 | all-reduce | flops 2 | bytes 16 | tf_op jit(solution)/shard_map/psum | solution.py:43
  305.4 6.7 %all-reduce.29 = (f32[]{:T(128)}, f32[]{:T(128)}) all-reduce(f32[]{:T(128)} %get-tuple-element.33, f32[]{:T(128)} %get-tuple-element.34), channel_id=1, replica_groups=mesh['grp'=4,'tile_0'=4,'tile_1'=4,'tile_2'=2] {'tile_0'}, use_global_device_ids=true, to_apply=%region_23.24 | all-reduce | flops 2 | bytes 16 | tf_op jit(solution)/shard_map/psum | solution.py:43
  312.1 9.8 %all-reduce.26 = (f32[]{:T(128)}, f32[]{:T(128)}) all-reduce(f32[]{:T(128)} %get-tuple-element.27, f32[]{:T(128)} %get-tuple-element.28), channel_id=1, replica_groups=mesh['grp'=4,'tile_0'=4,'tile_1'=4,'tile_2'=2] {'tile_1'}, use_global_device_ids=true, to_apply=%region_24.25 | all-reduce | flops 2 | bytes 16 | tf_op jit(solution)/shard_map/psum | solution.py:43
  321.9 9.2 %all-reduce.35 = (f32[]{:T(128)}, f32[]{:T(128)}) all-reduce(f32[]{:T(128)} %get-tuple-element.21, f32[]{:T(128)} %get-tuple-element.22), channel_id=1, replica_groups=mesh['grp'=4,'tile_0'=4,'tile_1'=4,'tile_2'=2] {'tile_2'}, use_global_device_ids=true, to_apply=%region_25.26 | all-reduce | flops 2 | bytes 16 | tf_op jit(solution)/shard_map/psum | solution.py:43
  (214 shorter events, 57.0 us)
Async XLA Ops:
  3.9 5.1 %copy-start.35 = (s32[2,8,64]{2,1,0:T(8,128)S(1)}, s32[2,8,64]{2,1,0:T(8,128)}, u32[]{:S(2)}) copy-start(s32[2,8,64]{2,1,0:T(8,128)} %param.16) | copy-start | bytes 12292
  3.9 31.1 %all-to-all-start = ((f32[2,2,4,64,512]{4,3,0,1,2:T(8,128)}), f32[2,2,4,64,512]{4,3,0,1,2:T(8,128)}, u32[]{:S(2)}, u32[]{:S(2)}) async-start(f32[2,2,4,64,512]{4,3,0,1,2:T(8,128)} %copy.115), calls=%async_computation | async-start | bytes 4194304 | tf_op jit(solution)/shard_map/all_to_all | solution.py:173
  9.4 30.4 %copy-start.24 = (f32[2,64,512]{2,1,0:T(8,128)}, f32[2,64,512]{2,1,0:T(8,128)S(1)}, u32[]{:S(2)}) copy-start(f32[2,64,512]{2,1,0:T(8,128)S(1)} %copy.114) | copy-start | bytes 786436
  10.3 2.3 copy-start.31
  37.7 2.1 copy-start.28
  37.7 2.2 copy-start.29
  40.0 9.4 %collective-permute-start = (f32[12,2,8,512]{3,2,1,0:T(8,128)S(1)}, f32[12,2,8,512]{3,2,1,0:T(8,128)S(1)}, u32[]{:S(2)}, u32[]{:S(2)}) collective-permute-start(f32[12,2,8,512]{3,2,1,0:T(8,128)S(1)} %get-tuple-element.93), channel_id=1, source_target_pairs={{0,32},{32,64},{64,96},{1,33},{33,65},{65,97},{2,34},{34,66},{66,9... | collective-permute-start | bytes 1179656 | tf_op jit(solution)/shard_map/ppermute | solution.py:54
  42.4 10.8 %collective-permute-start.1 = (f32[12,2,8,512]{3,2,1,0:T(8,128)S(1)}, f32[12,2,8,512]{3,2,1,0:T(8,128)S(1)}, u32[]{:S(2)}, u32[]{:S(2)}) collective-permute-start(f32[12,2,8,512]{3,2,1,0:T(8,128)S(1)} %get-tuple-element.94), channel_id=1, source_target_pairs={{32,0},{64,32},{96,64},{33,1},{65,33},{97,65},{34,2},{66,34},{98,6... | collective-permute-start | bytes 1179656 | tf_op jit(solution)/shard_map/ppermute | solution.py:55
  53.2 0.7 copy-start.2
  57.7 10.2 %collective-permute-start.2 = (f32[12,2,80,8]{2,3,1,0:T(8,128)}, f32[12,2,80,8]{2,3,1,0:T(8,128)}, u32[]{:S(2)}, u32[]{:S(2)}) collective-permute-start(f32[12,2,80,8]{2,3,1,0:T(8,128)} %copy.121), channel_id=1, source_target_pairs={{0,1},{1,2},{2,3},{3,4},{4,5},{5,6},{6,7},{7,8},{8,9},{9,10},{10,1... | collective-permute-start | bytes 184328 | tf_op jit(solution)/shard_map/ppermute | solution.py:54
  65.9 6.2 %collective-permute-start.3 = (f32[12,2,80,8]{2,3,1,0:T(8,128)}, f32[12,2,80,8]{2,3,1,0:T(8,128)}, u32[]{:S(2)}, u32[]{:S(2)}) collective-permute-start(f32[12,2,80,8]{2,3,1,0:T(8,128)} %copy.122), channel_id=1, source_target_pairs={{1,0},{2,1},{3,2},{4,3},{5,4},{6,5},{7,6},{8,7},{9,8},{10,9},{11,1... | collective-permute-start | bytes 184328 | tf_op jit(solution)/shard_map/ppermute | solution.py:55
  79.0 1.2 copy-start
  79.0 1.5 copy-start.1
  79.0 1.6 copy-start.3
  109.0 1.0 copy-start.23
  109.0 1.1 copy-start.25
  112.4 3.7 %copy-start.30 = (f32[256,512]{1,0:T(8,128)S(1)}, f32[256,512]{1,0:T(8,128)}, u32[]{:S(2)}) copy-start(f32[256,512]{1,0:T(8,128)} %param.12) | copy-start | bytes 1572868
  112.4 5.8 %copy-start.34 = (s32[32,64]{1,0:T(8,128)S(1)}, s32[32,64]{1,0:T(8,128)}, u32[]{:S(2)}) copy-start(s32[32,64]{1,0:T(8,128)} %param.14) | copy-start | bytes 24580
  112.4 16.7 %all-to-all-start.1 = ((f32[2,4,64,512]{3,2,0,1:T(8,128)}), f32[2,4,64,512]{3,2,0,1:T(8,128)S(1)}, u32[]{:S(2)}, u32[]{:S(2)}) async-start(f32[2,4,64,512]{3,2,0,1:T(8,128)} %pad_maximum_fusion.3), calls=%async_computation.1 | async-start | bytes 2097152 | tf_op jit(solution)/shard_map/all_to_all | solution.py:200
  116.2 14.0 %copy-start.20 = (f32[256,512]{0,1:T(8,128)}, f32[256,512]{0,1:T(8,128)S(1)}, u32[]{:S(2)}) copy-start(f32[256,512]{0,1:T(8,128)S(1)} %copy.157) | copy-start | bytes 1572868
  116.3 49.9 %collective-permute-start.10 = (f32[256,1]{0,1:T(1,128)S(1)}, f32[256,1]{0,1:T(1,128)S(1)}, u32[]{:S(2)}, u32[]{:S(2)}) collective-permute-start(f32[256,1]{0,1:T(1,128)S(1)} %get-tuple-element.169), channel_id=1, source_target_pairs={{1,0},{2,1},{3,2},{4,3},{5,4},{6,5},{7,6},{8,7},{9,8},{10,9},{11,1... | collective-permute-start | bytes 3080 | tf_op jit(solution)/shard_map/ppermute | solution.py:30
  135.4 15.1 %copy-start.32 = (f32[256,512]{1,0:T(8,128)S(1)}, f32[256,512]{1,0:T(8,128)}, u32[]{:S(2)}) copy-start(f32[256,512]{1,0:T(8,128)} %param.10) | copy-start | bytes 1572868
  136.9 18.4 %collective-permute-start.4 = (f32[3,1,512]{2,1,0:T(1,128)S(1)}, f32[3,1,512]{2,1,0:T(1,128)S(1)}, u32[]{:S(2)}, u32[]{:S(2)}) collective-permute-start(f32[3,1,512]{2,1,0:T(1,128)S(1)} %copy.139), channel_id=1, source_target_pairs={{0,32},{32,64},{64,96},{1,33},{33,65},{65,97},{2,34},{34,66},{66,9... | collective-permute-start | bytes 18440 | tf_op jit(solution)/shard_map/ppermute | solution.py:29
  140.5 17.3 %collective-permute-start.6 = (f32[3,1,512]{2,1,0:T(1,128)S(1)}, f32[3,1,512]{2,1,0:T(1,128)S(1)}, u32[]{:S(2)}, u32[]{:S(2)}) collective-permute-start(f32[3,1,512]{2,1,0:T(1,128)S(1)} %copy.141), channel_id=1, source_target_pairs={{32,0},{64,32},{96,64},{33,1},{65,33},{97,65},{34,2},{66,34},{98,6... | collective-permute-start | bytes 18440 | tf_op jit(solution)/shard_map/ppermute | solution.py:30
  141.8 9.8 %collective-permute-start.5 = (f32[3,256,1]{1,2,0:T(1,128)S(1)}, f32[3,256,1]{1,2,0:T(1,128)S(1)}, u32[]{:S(2)}, u32[]{:S(2)}) collective-permute-start(f32[3,256,1]{1,2,0:T(1,128)S(1)} %get-tuple-element.96), channel_id=1, source_target_pairs={{0,1},{1,2},{2,3},{3,4},{4,5},{5,6},{6,7},{7,8},{8,9},{9,10},{10,1... | collective-permute-start | bytes 9224 | tf_op jit(solution)/shard_map/ppermute | solution.py:29
  146.1 18.4 %collective-permute-start.7 = (f32[3,256,1]{1,2,0:T(1,128)S(1)}, f32[3,256,1]{1,2,0:T(1,128)S(1)}, u32[]{:S(2)}, u32[]{:S(2)}) collective-permute-start(f32[3,256,1]{1,2,0:T(1,128)S(1)} %get-tuple-element.95), channel_id=1, source_target_pairs={{1,0},{2,1},{3,2},{4,3},{5,4},{6,5},{7,6},{8,7},{9,8},{10,9},{11,1... | collective-permute-start | bytes 9224 | tf_op jit(solution)/shard_map/ppermute | solution.py:30
  151.5 14.6 %collective-permute-start.11 = (f32[256,1]{0,1:T(1,128)S(1)}, f32[256,1]{0,1:T(1,128)S(1)}, u32[]{:S(2)}, u32[]{:S(2)}) collective-permute-start(f32[256,1]{0,1:T(1,128)S(1)} %get-tuple-element.170), channel_id=1, source_target_pairs={{0,1},{1,2},{2,3},{3,4},{4,5},{5,6},{6,7},{7,8},{8,9},{9,10},{10,1... | collective-permute-start | bytes 3080 | tf_op jit(solution)/shard_map/ppermute | solution.py:29
  155.3 10.9 %collective-permute-start.8 = (f32[1,512]{0,1:T(8,128)}, f32[1,512]{0,1:T(8,128)S(1)}, u32[]{:S(2)}, u32[]{:S(2)}) collective-permute-start(f32[1,512]{0,1:T(8,128)} %copy.146), channel_id=1, source_target_pairs={{32,0},{64,32},{96,64},{33,1},{65,33},{97,65},{34,2},{66,34},{98,6... | collective-permute-start | bytes 6152 | tf_op jit(solution)/shard_map/ppermute | solution.py:30
  157.8 10.5 %collective-permute-start.9 = (f32[1,512]{0,1:T(8,128)}, f32[1,512]{0,1:T(8,128)}, u32[]{:S(2)}, u32[]{:S(2)}) collective-permute-start(f32[1,512]{0,1:T(8,128)} %copy.149), channel_id=1, source_target_pairs={{0,32},{32,64},{64,96},{1,33},{33,65},{65,97},{2,34},{34,66},{66,9... | collective-permute-start | bytes 6152 | tf_op jit(solution)/shard_map/ppermute | solution.py:29
  164.5 3.8 %copy-start.18 = (f32[3,1,512]{1,2,0:T(8,128)S(1)}, f32[3,1,512]{1,2,0:T(8,128)}, u32[]{:S(2)}) copy-start(f32[3,1,512]{1,2,0:T(8,128)} %copy.140) | copy-start | bytes 18436
  164.5 3.8 %copy-start.19 = (f32[3,1,512]{1,2,0:T(8,128)S(1)}, f32[3,1,512]{1,2,0:T(8,128)}, u32[]{:S(2)}) copy-start(f32[3,1,512]{1,2,0:T(8,128)} %copy.143) | copy-start | bytes 18436
  164.5 3.8 %copy-start.21 = (f32[256,512]{0,1:T(8,128)S(1)}, f32[256,512]{0,1:T(8,128)}, u32[]{:S(2)}) copy-start(f32[256,512]{0,1:T(8,128)} %copy-done.20) | copy-start | bytes 1572868
  164.5 3.8 %copy-start.27 = (f32[256,512]{0,1:T(8,128)S(1)}, f32[256,512]{0,1:T(8,128)}, u32[]{:S(2)}) copy-start(f32[256,512]{0,1:T(8,128)} %copy.144) | copy-start | bytes 1572868
  166.1 0.7 copy-start.33
  171.7 13.8 %copy-start.4 = (f32[256,512]{0,1:T(8,128)}, f32[256,512]{0,1:T(8,128)S(1)}, u32[]{:S(2)}) copy-start(f32[256,512]{0,1:T(8,128)S(1)} %get-tuple-element.49) | copy-start | bytes 1572868
  171.7 13.8 %copy-start.6 = (f32[256,512]{0,1:T(8,128)}, f32[256,512]{0,1:T(8,128)S(1)}, u32[]{:S(2)}) copy-start(f32[256,512]{0,1:T(8,128)S(1)} %get-tuple-element.52) | copy-start | bytes 1572868
  171.7 13.8 %copy-start.9 = (f32[256,512]{0,1:T(8,128)}, f32[256,512]{0,1:T(8,128)S(1)}, u32[]{:S(2)}) copy-start(f32[256,512]{0,1:T(8,128)S(1)} %get-tuple-element.53) | copy-start | bytes 1572868
  171.7 13.8 %copy-start.12 = (f32[256,512]{0,1:T(8,128)}, f32[256,512]{0,1:T(8,128)S(1)}, u32[]{:S(2)}) copy-start(f32[256,512]{0,1:T(8,128)S(1)} %get-tuple-element.54) | copy-start | bytes 1572868
  171.7 13.8 %copy-start.15 = (f32[256,512]{0,1:T(8,128)}, f32[256,512]{0,1:T(8,128)S(1)}, u32[]{:S(2)}) copy-start(f32[256,512]{0,1:T(8,128)S(1)} %get-tuple-element.55) | copy-start | bytes 1572868
  171.8 12.4 %collective-permute-start.12 = (f32[1,512]{0,1:T(8,128)S(1)}, f32[1,512]{0,1:T(8,128)S(1)}, u32[]{:S(2)}, u32[]{:S(2)}) collective-permute-start(f32[1,512]{0,1:T(8,128)S(1)} %get-tuple-element.166), channel_id=1, source_target_pairs={{32,0},{64,32},{96,64},{33,1},{65,33},{97,65},{34,2},{66,34},{98,6... | collective-permute-start | bytes 6152 | tf_op jit(solution)/shard_map/ppermute | solution.py:30
  173.1 11.1 %collective-permute-start.13 = (f32[1,512]{0,1:T(8,128)S(1)}, f32[1,512]{0,1:T(8,128)S(1)}, u32[]{:S(2)}, u32[]{:S(2)}) collective-permute-start(f32[1,512]{0,1:T(8,128)S(1)} %get-tuple-element.165), channel_id=1, source_target_pairs={{0,32},{32,64},{64,96},{1,33},{33,65},{65,97},{2,34},{34,66},{66,9... | collective-permute-start | bytes 6152 | tf_op jit(solution)/shard_map/ppermute | solution.py:29
  177.6 5.9 %collective-permute-start.14 = (f32[256,1]{0,1:T(1,128)S(1)}, f32[256,1]{0,1:T(1,128)S(1)}, u32[]{:S(2)}, u32[]{:S(2)}) collective-permute-start(f32[256,1]{0,1:T(1,128)S(1)} %get-tuple-element.163), channel_id=1, source_target_pairs={{1,0},{2,1},{3,2},{4,3},{5,4},{6,5},{7,6},{8,7},{9,8},{10,9},{11,1... | collective-permute-start | bytes 3080 | tf_op jit(solution)/shard_map/ppermute | solution.py:30
  179.7 4.5 %collective-permute-start.15 = (f32[256,1]{0,1:T(1,128)S(1)}, f32[256,1]{0,1:T(1,128)S(1)}, u32[]{:S(2)}, u32[]{:S(2)}) collective-permute-start(f32[256,1]{0,1:T(1,128)S(1)} %get-tuple-element.164), channel_id=1, source_target_pairs={{0,1},{1,2},{2,3},{3,4},{4,5},{5,6},{6,7},{7,8},{8,9},{9,10},{10,1... | collective-permute-start | bytes 3080 | tf_op jit(solution)/shard_map/ppermute | solution.py:29
  226.4 13.9 %copy-start.7 = (f32[256,512]{0,1:T(8,128)S(1)}, f32[256,512]{0,1:T(8,128)}, u32[]{:S(2)}) copy-start(f32[256,512]{0,1:T(8,128)} %copy-done.6) | copy-start | bytes 1572868
  226.4 13.9 %copy-start.10 = (f32[256,512]{0,1:T(8,128)S(1)}, f32[256,512]{0,1:T(8,128)}, u32[]{:S(2)}) copy-start(f32[256,512]{0,1:T(8,128)} %copy-done.9) | copy-start | bytes 1572868
  226.4 13.9 %copy-start.13 = (f32[256,512]{0,1:T(8,128)S(1)}, f32[256,512]{0,1:T(8,128)}, u32[]{:S(2)}) copy-start(f32[256,512]{0,1:T(8,128)} %copy-done.12) | copy-start | bytes 1572868
  226.5 13.9 %copy-start.16 = (f32[256,512]{0,1:T(8,128)S(1)}, f32[256,512]{0,1:T(8,128)}, u32[]{:S(2)}) copy-start(f32[256,512]{0,1:T(8,128)} %copy-done.15) | copy-start | bytes 1572868
  227.9 12.4 %collective-permute-start.16 = (f32[1,512]{0,1:T(8,128)S(1)}, f32[1,512]{0,1:T(8,128)S(1)}, u32[]{:S(2)}, u32[]{:S(2)}) collective-permute-start(f32[1,512]{0,1:T(8,128)S(1)} %get-tuple-element.162), channel_id=1, source_target_pairs={{32,0},{64,32},{96,64},{33,1},{65,33},{97,65},{34,2},{66,34},{98,6... | collective-permute-start | bytes 6152 | tf_op jit(solution)/shard_map/ppermute | solution.py:30
  229.2 11.1 %collective-permute-start.17 = (f32[1,512]{0,1:T(8,128)S(1)}, f32[1,512]{0,1:T(8,128)S(1)}, u32[]{:S(2)}, u32[]{:S(2)}) collective-permute-start(f32[1,512]{0,1:T(8,128)S(1)} %get-tuple-element.161), channel_id=1, source_target_pairs={{0,32},{32,64},{64,96},{1,33},{33,65},{65,97},{2,34},{34,66},{66,9... | collective-permute-start | bytes 6152 | tf_op jit(solution)/shard_map/ppermute | solution.py:29
  233.2 6.4 %collective-permute-start.18 = (f32[256,1]{0,1:T(1,128)S(1)}, f32[256,1]{0,1:T(1,128)S(1)}, u32[]{:S(2)}, u32[]{:S(2)}) collective-permute-start(f32[256,1]{0,1:T(1,128)S(1)} %get-tuple-element.159), channel_id=1, source_target_pairs={{1,0},{2,1},{3,2},{4,3},{5,4},{6,5},{7,6},{8,7},{9,8},{10,9},{11,1... | collective-permute-start | bytes 3080 | tf_op jit(solution)/shard_map/ppermute | solution.py:30
  236.0 4.2 %collective-permute-start.19 = (f32[256,1]{0,1:T(1,128)S(1)}, f32[256,1]{0,1:T(1,128)S(1)}, u32[]{:S(2)}, u32[]{:S(2)}) collective-permute-start(f32[256,1]{0,1:T(1,128)S(1)} %get-tuple-element.160), channel_id=1, source_target_pairs={{0,1},{1,2},{2,3},{3,4},{4,5},{5,6},{6,7},{7,8},{8,9},{9,10},{10,1... | collective-permute-start | bytes 3080 | tf_op jit(solution)/shard_map/ppermute | solution.py:29
  282.9 13.2 %copy-start.26 = (f32[2,2,64,512]{3,2,0,1:T(8,128)S(1)}, f32[2,2,64,512]{3,2,0,1:T(8,128)}, u32[]{:S(2)}) copy-start(f32[2,2,64,512]{3,2,0,1:T(8,128)} %get-tuple-element.57) | copy-start | bytes 1572868
  283.0 13.9 %copy-start.8 = (f32[256,512]{0,1:T(8,128)S(1)}, f32[256,512]{0,1:T(8,128)}, u32[]{:S(2)}) copy-start(f32[256,512]{0,1:T(8,128)} %copy-done.6) | copy-start | bytes 1572868
  283.0 13.9 %copy-start.11 = (f32[256,512]{0,1:T(8,128)S(1)}, f32[256,512]{0,1:T(8,128)}, u32[]{:S(2)}) copy-start(f32[256,512]{0,1:T(8,128)} %copy-done.9) | copy-start | bytes 1572868
  283.0 13.9 %copy-start.14 = (f32[256,512]{0,1:T(8,128)S(1)}, f32[256,512]{0,1:T(8,128)}, u32[]{:S(2)}) copy-start(f32[256,512]{0,1:T(8,128)} %copy-done.12) | copy-start | bytes 1572868
  283.0 13.9 %copy-start.17 = (f32[256,512]{0,1:T(8,128)S(1)}, f32[256,512]{0,1:T(8,128)}, u32[]{:S(2)}) copy-start(f32[256,512]{0,1:T(8,128)} %copy-done.15) | copy-start | bytes 1572868
  283.0 13.8 %collective-permute-start.20 = (f32[1,512]{0,1:T(8,128)S(1)}, f32[1,512]{0,1:T(8,128)S(1)}, u32[]{:S(2)}, u32[]{:S(2)}) collective-permute-start(f32[1,512]{0,1:T(8,128)S(1)} %get-tuple-element.158), channel_id=1, source_target_pairs={{32,0},{64,32},{96,64},{33,1},{65,33},{97,65},{34,2},{66,34},{98,6... | collective-permute-start | bytes 6152 | tf_op jit(solution)/shard_map/ppermute | solution.py:30
  284.5 12.4 %collective-permute-start.21 = (f32[1,512]{0,1:T(8,128)S(1)}, f32[1,512]{0,1:T(8,128)S(1)}, u32[]{:S(2)}, u32[]{:S(2)}) collective-permute-start(f32[1,512]{0,1:T(8,128)S(1)} %get-tuple-element.157), channel_id=1, source_target_pairs={{0,32},{32,64},{64,96},{1,33},{33,65},{65,97},{2,34},{34,66},{66,9... | collective-permute-start | bytes 6152 | tf_op jit(solution)/shard_map/ppermute | solution.py:29
  288.5 8.3 %collective-permute-start.22 = (f32[256,1]{0,1:T(1,128)S(1)}, f32[256,1]{0,1:T(1,128)S(1)}, u32[]{:S(2)}, u32[]{:S(2)}) collective-permute-start(f32[256,1]{0,1:T(1,128)S(1)} %get-tuple-element.155), channel_id=1, source_target_pairs={{1,0},{2,1},{3,2},{4,3},{5,4},{6,5},{7,6},{8,7},{9,8},{10,9},{11,1... | collective-permute-start | bytes 3080 | tf_op jit(solution)/shard_map/ppermute | solution.py:30
  291.3 5.5 %collective-permute-start.23 = (f32[256,1]{0,1:T(1,128)S(1)}, f32[256,1]{0,1:T(1,128)S(1)}, u32[]{:S(2)}, u32[]{:S(2)}) collective-permute-start(f32[256,1]{0,1:T(1,128)S(1)} %get-tuple-element.156), channel_id=1, source_target_pairs={{0,1},{1,2},{2,3},{3,4},{4,5},{5,6},{6,7},{7,8},{8,9},{9,10},{10,1... | collective-permute-start | bytes 3080 | tf_op jit(solution)/shard_map/ppermute | solution.py:29
  296.9 38.1 %copy-start.5 = (f32[256,512]{0,1:T(8,128)S(1)}, f32[256,512]{0,1:T(8,128)}, u32[]{:S(2)}) copy-start(f32[256,512]{0,1:T(8,128)} %copy-done.4) | copy-start | bytes 1572868
  296.9 38.1 %copy-start.22 = (f32[256,512]{0,1:T(8,128)S(1)}, f32[256,512]{0,1:T(8,128)}, u32[]{:S(2)}) copy-start(f32[256,512]{0,1:T(8,128)} %copy-done.20) | copy-start | bytes 1572868
where the time goes:
time: 342 us; the launch traced here: 336 us
  blocking collectives  107 us (31%)
  starting transfers between devices  77.7 us (23%)
  other arithmetic  56.1 us (16%)
  waiting for transfers between devices  44.4 us (13%)
  local copies, waits for them, and re-layouts  39.4 us (12%)
  between operations  11.6 us (3%)
    psum x12, blocking collectives, by_axis(): array = lax.psum(array, axis)  107 us
    ppermute x10, starting transfers between devices, with_halo(): lax.ppermute(last, axis, up)  39 us
    all_to_all x1, waiting for transfers between devices, shards(): lax.all_to_all(outgoing, 'grp', split_axis=2, concat_axis=2, tiled=True)  22.3 us
    ppermute x10, starting transfers between devices, with_halo(): lax.ppermute(first, axis, [(b, a) for a, b in up])  18.2 us
    unnamed x81, local copies, waits for them, and re-layouts  12.2 us
    ppermute x2, starting transfers between devices, extended(): before = lax.ppermute(last, axis, up)  8.51 us
    all_to_all x1, waiting for transfers between devices, shards(): lax.all_to_all(parcel, 'grp', split_axis=1, concat_axis=1, tiled=True)  7.65 us
    mul x7, other arithmetic, relax_stress(): (previous[0] + RELAX * strength * (div_rate / deformation - 1.0)) * relax...  6.91 us
  transfers between devices with their start and end apart: 26, of which 8 were waited for; matrix products, arithmetic and copies ran while one was open for 9% of the time, Pallas kernels for 0%

commit v1 on v0

v1 whole, which is shorter than its diff:
```python
import functools

import jax
import jax.numpy as jnp
from jax import lax
from jax.experimental import pallas as pl
from jax.experimental.pallas import tpu as pltpu
from jax.sharding import PartitionSpec as P

BS = 8
NSUB = 8
DAMP = 0.05
RELAX = 0.2
STRENGTH = 0.5
DRAG = 1.0
STEP = 0.5
G = 4
LT = 4
NT = LT + 1
IR = 64
OR = 256
IH = IR + 32
OH = OR + 32
F32 = jnp.float32
MESH = pl.DeviceIdType.MESH
DUMMY = 4096

R_CL, R_CR, R_IL, R_IR, R_OL, R_OR = 0, 1, 2, 3, 4, 5
R_IU, R_ID, R_F = 6, 8, 10
R_OU, R_OD, R_RS, R_RH, R_1, R_2 = 12, 13, 14, 18, 19, 20
R_BI, R_BO = 21, 30
N_R = 39
S_CL, S_CR, S_L, S_R, S_U, S_D, S_F, S_RS, S_1, S_2 = 0, 1, 2, 3, 4, 5, 6, 7, 9, 10
S_RH = 11
S_BI, S_BO = 12, 21
N_S = 30
L_BLK, L_ICE, L_FL, L_OC, L_OUT, L_OUTS = 0, 1, 2, 3, 4, 5
N_L = 6


def east(tiles, lane):
    turned = [pltpu.roll(x, 127, 1) for x in tiles]
    return [jnp.where(lane == 127, turned[(j + 1) % NT], turned[j]) for j in range(NT)]


def west(tiles, lane):
    turned = [pltpu.roll(x, 1, 1) for x in tiles]
    return [jnp.where(lane == 0, turned[(j - 1) % NT], turned[j]) for j in range(NT)]


def kernel(
    T,
    base, depth, ssh, cur, land, thick, iblk, ivel, istr, wind,
    o_ssh, o_vel, o_str,
    V, S, W, TH, FL, CV, C1, C2, EV, ES, EW, ETH, EO,
    LV, LS, LW, LTH, LC, LO,
    B, D, X, Z, Y0, Y1, Y2, H, WID, DG, WET, V1, V2,
    BI, BO, PKO, PKI, SPB, XB, RSP, RX, RH, RXH, L1, L2, OUT, DUM,
    rs, ss, ls,
):
    g = lax.axis_index("grp")
    t = lax.axis_index("tile")
    has_l, has_r, has_u, has_d = t > 0, t < T - 1, g > 0, g < G - 1
    lane = lax.broadcasted_iota(jnp.int32, (8, 128), 1)
    sub = lax.broadcasted_iota(jnp.int32, (8, 128), 0)
    zero = jnp.zeros((8, 128), F32)
    first_cap = g // 2
    owner_cap = jnp.where(g == 0, 0, 1)
    is_owner = jnp.logical_or(g == 0, g == G - 1)

    def wait_rows(sem, rows):
        pltpu.make_async_copy(DUM.at[pl.ds(0, rows)], DUM.at[pl.ds(0, rows)], sem).wait()

    def send(src, dst, s, r, dev):
        pltpu.make_async_remote_copy(
            src_ref=src, dst_ref=dst, send_sem=ss.at[s], recv_sem=rs.at[r],
            device_id=dev, device_id_type=MESH,
        ).start()

    def local(src, dst, s):
        pltpu.make_async_copy(src, dst, ls.at[s]).start()

    def cols(j):
        return pl.ds(128 * j, 128)

    nbrs = []
    for dy in (-1, 0, 1):
        for dx in (-1, 0, 1):
            if dy == 0 and dx == 0:
                continue
            cond = None
            for need, there in ((dy < 0, has_u), (dy > 0, has_d), (dx < 0, has_l), (dx > 0, has_r)):
                if need:
                    cond = there if cond is None else jnp.logical_and(cond, there)
            nbrs.append((dy, dx, cond))

    local(iblk, BI.at[1, 1], L_BLK)
    local(land, BO.at[1, 1], L_BLK)
    for j in range(LT):
        local(ivel.at[:, :, :, cols(j)], V.at[:, :, j, pl.ds(16, IR), :], L_ICE)
        local(istr.at[:, :, :, cols(j)], S.at[:, :, j, pl.ds(16, IR), :], L_ICE)
        local(wind.at[:, :, :, cols(j)], W.at[:, :, j, pl.ds(16, IR), :], L_ICE)
        local(thick.at[:, :, cols(j)], TH.at[:, j, pl.ds(16, IR), :], L_ICE)
        local(base.at[:, cols(j)], B.at[j, pl.ds(16, OR), :], L_OC)
        local(depth.at[:, cols(j)], D.at[j, pl.ds(16, OR), :], L_OC)
        local(ssh.at[:, cols(j)], X.at[j, pl.ds(16, OR), :], L_OC)

    barrier = pltpu.get_barrier_semaphore()
    core = lax.rem(t, 2)
    for dy, dx, cond in nbrs:
        @pl.when(cond)
        def _(dy=dy, dx=dx):
            pl.semaphore_signal(barrier, inc=1, device_id=(g + dy, t + dx), device_id_type=MESH)
    peers1 = []
    for dg in range(G):
        for dc in range(2):
            if dg or dc:
                peers1.append((lax.rem(g + dg, G), t - core + lax.rem(core + dc, 2)))
    M2 = T // 2
    mine2 = t // 2
    peers2 = [(g, 2 * lax.rem(mine2 + k, M2) + core) for k in range(1, M2)]
    for dev in peers1 + peers2:
        pl.semaphore_signal(barrier, inc=1, device_id=dev, device_id_type=MESH)
    high = 1 + jnp.minimum(g, 1) + jnp.minimum(G - 1 - g, 1)
    wide = 1 + jnp.minimum(t, 1) + jnp.minimum(T - 1 - t, 1)
    pl.semaphore_wait(barrier, high * wide - 1 + len(peers1) + len(peers2))

    left, right, up, down = (g, t - 1), (g, t + 1), (g - 1, t), (g + 1, t)

    @pl.when(jnp.logical_and(is_owner, has_l))
    def _():
        send(cur.at[:, :, cols(0)], LC.at[1], S_CL, R_CR, left)

    @pl.when(jnp.logical_and(is_owner, has_r))
    def _():
        send(cur.at[:, :, cols(LT - 1)], LC.at[0], S_CR, R_CL, right)

    def flow_rows(d):
        lo, hi = max(IR * d - 8, 0), min(IR * d + IR + 8, OR)
        return lo, hi - lo, 16 + lo - IR * d

    dests = {0: (1, 2, 3), G - 1: (2, 1, 0)}

    def send_flow(c, d):
        lo, n, at = flow_rows(d)
        for j in range(LT):
            send(cur.at[:, pl.ds(lo, n), cols(j)], FL.at[:, c, j, pl.ds(at, n), :],
                 S_F, R_F + c, (d, t))

    def halo_ice(dev, c, src, dst, s, r):
        for j in range(LT):
            send(ivel.at[:, c, pl.ds(src, 8), cols(j)], V.at[:, c, j, pl.ds(dst, 8), :], s, r, dev)
            send(istr.at[:, c, pl.ds(src, 8), cols(j)], S.at[:, c, j, pl.ds(dst, 8), :], s, r, dev)
            send(wind.at[:, c, pl.ds(src, 8), cols(j)], W.at[:, c, j, pl.ds(dst, 8), :], s, r, dev)
            send(thick.at[c, pl.ds(src, 8), cols(j)], TH.at[c, j, pl.ds(dst, 8), :], s, r, dev)

    for own, c in ((0, 0), (G - 1, 1)):
        @pl.when(g == own)
        def _(own=own, c=c):
            send_flow(c, dests[own][0])
            lo, n, at = flow_rows(own)
            for j in range(LT):
                local(cur.at[:, pl.ds(lo, n), cols(j)], FL.at[:, c, j, pl.ds(at, n), :], L_FL)

    for turn in range(2):
        for dev, cond, src, dst, s, r in (
            (up, has_u, 0, IR + 16, S_U, R_ID),
            (down, has_d, IR - 8, 8, S_D, R_IU),
        ):
            @pl.when(cond)
            def _(dev=dev, src=src, dst=dst, s=s, r=r):
                if turn == 0:
                    at = 0 if s == S_U else OR - 8
                    to = OR + 16 if s == S_U else 8
                    ro = R_OD if s == S_U else R_OU
                    for j in range(LT):
                        send(base.at[pl.ds(at, 8), cols(j)], B.at[j, pl.ds(to, 8), :], s, ro, dev)
                        send(depth.at[pl.ds(at, 8), cols(j)], D.at[j, pl.ds(to, 8), :], s, ro, dev)
                        send(ssh.at[pl.ds(at, 8), cols(j)], X.at[j, pl.ds(to, 8), :], s, ro, dev)
                there = dev[0] // 2
                c = there if turn == 0 else 1 - there
                halo_ice(dev, c, src, dst, s, r + c)
        if turn == 0:
            for own, c in ((0, 0), (G - 1, 1)):
                @pl.when(g == own)
                def _(own=own, c=c):
                    for d in dests[own][1:]:
                        send_flow(c, d)

    for dy, dx, cond in nbrs:
        k = 3 * (1 - dy) + (1 - dx)
        @pl.when(cond)
        def _(dy=dy, dx=dx, k=k):
            dev = (g + dy, t + dx)
            send(iblk, BI.at[1 - dy, 1 - dx], S_BI + k, R_BI + k, dev)
            rows = pl.ds(0, OR // BS) if dy == 0 else pl.ds(0 if dy < 0 else OR // BS - 8, 8)
            send(land.at[rows], BO.at[1 - dy, 1 - dx, rows], S_BO + k, R_BO + k, dev)

    for dev, cond, side, at, s, ri, ro in (
        (left, has_l, 1, 0, S_L, R_IR, R_OR),
        (right, has_r, 0, LT - 1, S_R, R_IL, R_OL),
    ):
        @pl.when(cond)
        def _(dev=dev, side=side, at=at, s=s, ri=ri, ro=ro):
            send(ivel.at[:, :, :, cols(at)], LV.at[side], s, ri, dev)
            send(istr.at[:, :, :, cols(at)], LS.at[side], s, ri, dev)
            send(wind.at[:, :, :, cols(at)], LW.at[side], s, ri, dev)
            send(thick.at[:, :, cols(at)], LTH.at[side], s, ri, dev)
            send(base.at[:, cols(at)], LO.at[0, side], s, ro, dev)
            send(depth.at[:, cols(at)], LO.at[1, side], s, ro, dev)
            send(ssh.at[:, cols(at)], LO.at[2, side], s, ro, dev)

    def fill(ref, idx):
        ref[idx] = jnp.zeros(ref.at[idx].shape, ref.dtype)

    for cond, row, orow, by in ((g == 0, 8, 8, 0), (g == G - 1, IR + 16, OR + 16, 2)):
        @pl.when(cond)
        def _(row=row, orow=orow, by=by):
            for c in range(2):
                for j in range(NT):
                    for k in range(3):
                        S[k, c, j, pl.ds(row, 8), :] = zero
                    for k in range(2):
                        V[k, c, j, pl.ds(row, 8), :] = zero
                        W[k, c, j, pl.ds(row, 8), :] = zero
                        FL[k, c, j, pl.ds(row, 8), :] = zero
                    TH[c, j, pl.ds(row, 8), :] = zero
            for j in range(NT):
                B[j, pl.ds(orow, 8), :] = zero
                D[j, pl.ds(orow, 8), :] = zero
                X[j, pl.ds(orow, 8), :] = zero
            for x in range(3):
                for c in range(2):
                    BI[by, x, c] = jnp.zeros((8, 64), jnp.int32)
                BO[by, x] = jnp.zeros((32, 64), jnp.int32)

    for cond, side, bx in ((t == 0, 0, 0), (t == T - 1, 1, 2)):
        @pl.when(cond)
        def _(side=side, bx=bx):
            def body(i, carry):
                r = pl.ds(pl.multiple_of(8 * i, 8), 8)
                for c in range(2):
                    for k in range(3):
                        LS[side, k, c, r, :] = zero
                    for k in range(2):
                        LV[side, k, c, r, :] = zero
                        LW[side, k, c, r, :] = zero
                    LTH[side, c, r, :] = zero
                return carry
            lax.fori_loop(0, IR // 8, body, 0)

            def body2(i, carry):
                r = pl.ds(pl.multiple_of(8 * i, 8), 8)
                for k in range(2):
                    LC[side, k, r, :] = zero
                for k in range(3):
                    LO[k, side, r, :] = zero
                return carry
            lax.fori_loop(0, OR // 8, body2, 0)
            for y in range(3):
                for c in range(2):
                    BI[y, bx, c] = jnp.zeros((8, 64), jnp.int32)
                BO[y, bx] = jnp.zeros((32, 64), jnp.int32)

    for own, c in ((0, 0), (G - 1, 1)):
        @pl.when(g == own)
        def _(own=own, c=c):
            @pl.when(has_l)
            def _():
                wait_rows(rs.at[R_CL], 2 * OR)

            @pl.when(has_r)
            def _():
                wait_rows(rs.at[R_CR], 2 * OR)

            def merged(k, q):
                r = pl.ds(8 * q, 8)
                return jnp.where(lane < 64, LC[1, k, r, :], LC[0, k, r, :])

            for k in range(2):
                for s in range(10):
                    q = 8 * own - 1 + s
                    if 0 <= q < OR // 8:
                        FL[k, c, LT, pl.ds(8 + 8 * s, 8), :] = merged(k, q)
            for at, d in enumerate(dests[own]):
                packs = [zero] * 5
                for k in range(2):
                    for s in range(10):
                        q = 8 * d - 1 + s
                        if 0 <= q < OR // 8:
                            m = 10 * k + s
                            slot = m % 4
                            moved = pltpu.roll(merged(k, q), (32 * slot + 16) % 128, 1)
                            packs[m // 4] = jnp.where(lane // 32 == slot, moved, packs[m // 4])
                for v in range(5):
                    PKO[at, v] = packs[v]
                send(PKO.at[at], PKI.at[c], S_F, R_F + c, (d, t))

    wait_rows(ls.at[L_ICE], 8 * 2 * IR * LT)

    @pl.when(has_l)
    def _():
        wait_rows(rs.at[R_IL], 8 * 2 * IR)

    @pl.when(has_r)
    def _():
        wait_rows(rs.at[R_IR], 8 * 2 * IR)

    for c in range(2):
        def merge_ice(i, carry, c=c):
            r = pl.ds(pl.multiple_of(8 * i, 8), 8)
            w = pl.ds(pl.multiple_of(8 * i + 16, 8), 8)
            for k in range(2):
                V[k, c, LT, w, :] = jnp.where(lane < 64, LV[1, k, c, r, :], LV[0, k, c, r, :])
                W[k, c, LT, w, :] = jnp.where(lane < 64, LW[1, k, c, r, :], LW[0, k, c, r, :])
            for k in range(3):
                S[k, c, LT, w, :] = jnp.where(lane < 64, LS[1, k, c, r, :], LS[0, k, c, r, :])
            TH[c, LT, w, :] = jnp.where(lane < 64, LTH[1, c, r, :], LTH[0, c, r, :])
            return carry
        lax.fori_loop(0, IR // 8, merge_ice, 0)

    for e, dev, cond, src, dst, s, r in (
        (0, up, has_u, 16, IR + 16, S_U, R_ID),
        (1, down, has_d, IR + 8, 8, S_D, R_IU),
    ):
        @pl.when(cond)
        def _(e=e, dev=dev, src=src, dst=dst, s=s, r=r):
            a, b = pl.ds(src, 8), pl.ds(dst, 8)
            for c in range(2):
                for k in range(3):
                    ES[e, k, c] = S[k, c, LT, a, :]
                for k in range(2):
                    EV[e, k, c] = V[k, c, LT, a, :]
                    EW[e, k, c] = W[k, c, LT, a, :]
                ETH[e, c] = TH[c, LT, a, :]
            for turn in range(2):
                there = dev[0] // 2
                c = there if turn == 0 else 1 - there
                send(EV.at[e, :, c], V.at[:, c, LT, b, :], s, r + c, dev)
                send(ES.at[e, :, c], S.at[:, c, LT, b, :], s, r + c, dev)
                send(EW.at[e, :, c], W.at[:, c, LT, b, :], s, r + c, dev)
                send(ETH.at[e, c], TH.at[c, LT, b, :], s, r + c, dev)

    wait_rows(ls.at[L_OC], 3 * OR * LT)

    @pl.when(has_l)
    def _():
        wait_rows(rs.at[R_OL], 3 * OR)

    @pl.when(has_r)
    def _():
        wait_rows(rs.at[R_OR], 3 * OR)

    def merge_ocean(i, carry):
        r = pl.ds(pl.multiple_of(8 * i, 8), 8)
        w = pl.ds(pl.multiple_of(8 * i + 16, 8), 8)
        for k, ref in enumerate((B, D, X)):
            ref[LT, w, :] = jnp.where(lane < 64, LO[k, 1, r, :], LO[k, 0, r, :])
        return carry
    lax.fori_loop(0, OR // 8, merge_ocean, 0)
    for e, dev, cond, src, dst, s, r in (
        (0, up, has_u, 16, OR + 16, S_U, R_OD),
        (1, down, has_d, OR + 8, 8, S_D, R_OU),
    ):
        @pl.when(cond)
        def _(e=e, dev=dev, src=src, dst=dst, s=s, r=r):
            for k, ref in enumerate((B, D, X)):
                EO[e, k] = ref[LT, pl.ds(src, 8), :]
            for k, ref in enumerate((B, D, X)):
                send(EO.at[e, k], ref.at[LT, pl.ds(dst, 8), :], s, r, dev)

    pltpu.make_async_copy(iblk, BI.at[1, 1], ls.at[L_BLK]).wait()
    pltpu.make_async_copy(land, BO.at[1, 1], ls.at[L_BLK]).wait()
    for dy, dx, cond in nbrs:
        k = 3 * (1 + dy) + (1 + dx)
        @pl.when(cond)
        def _(dy=dy, dx=dx, k=k):
            dev = (g + dy, t + dx)
            pltpu.make_async_remote_copy(
                src_ref=iblk, dst_ref=BI.at[1 + dy, 1 + dx], send_sem=ss.at[S_BI + k],
                recv_sem=rs.at[R_BI + k], device_id=dev, device_id_type=MESH).wait_recv()
            rows = pl.ds(0, OR // BS) if dy == 0 else pl.ds(OR // BS - 8 if dy < 0 else 0, 8)
            pltpu.make_async_remote_copy(
                src_ref=land.at[rows], dst_ref=BO.at[1 + dy, 1 + dx, rows], send_sem=ss.at[S_BO + k],
                recv_sem=rs.at[R_BO + k], device_id=dev, device_id_type=MESH).wait_recv()

    def selection(width, first, start):
        block = lax.broadcasted_iota(jnp.int32, (64, width), 0)
        at = lax.broadcasted_iota(jnp.int32, (64, width), 1)
        hit = block == at // BS + first
        if start is not None:
            hit = jnp.logical_and(hit, (at < 64) if start == 0 else (at >= 64))
        return hit.astype(F32)

    sel_c = selection(128 * LT, 0, None)
    sel_r = selection(128, 0, 0)
    sel_l = selection(128, 48, 1)

    def spread_rows(refs):
        lft, mid, rgt = (ref.astype(F32) for ref in refs)
        wide = jnp.dot(mid, sel_c, preferred_element_type=F32)
        last = jnp.dot(rgt, sel_r, preferred_element_type=F32) + jnp.dot(
            lft, sel_l, preferred_element_type=F32)
        return wide, last

    def paint(ref, row, parts, b):
        wide, last = parts
        for j in range(LT):
            ref[j, pl.ds(row, 8), :] = jnp.broadcast_to(wide[b:b + 1, 128 * j:128 * j + 128], (8, 128))
        ref[LT, pl.ds(row, 8), :] = jnp.broadcast_to(last[b:b + 1, :], (8, 128))

    for c in range(2):
        cov = CV.at[c]
        paint(cov, 8, spread_rows([BI[0, x, c] for x in range(3)]), 7)
        mid = spread_rows([BI[1, x, c] for x in range(3)])
        for b in range(8):
            paint(cov, 16 + 8 * b, mid, b)
        paint(cov, IR + 16, spread_rows([BI[2, x, c] for x in range(3)]), 0)
    paint(WET, 8, spread_rows([BO[0, x, 24:32] for x in range(3)]), 7)
    for q in range(4):
        mid = spread_rows([BO[1, x, 8 * q:8 * q + 8] for x in range(3)])
        for b in range(8):
            paint(WET, 16 + 64 * q + 8 * b, mid, b)
    paint(WET, OR + 16, spread_rows([BO[2, x, 0:8] for x in range(3)]), 0)

    def cap(c):
        @pl.when(has_u)
        def _():
            wait_rows(rs.at[R_IU + c], 8 * 8 * NT)

        @pl.when(has_d)
        def _():
            wait_rows(rs.at[R_ID + c], 8 * 8 * NT)

        mine = jnp.logical_and(is_owner, c == owner_cap)
        at_end = jnp.logical_or(jnp.logical_and(c == 0, g == G - 1), jnp.logical_and(c == 1, g == 0))

        @pl.when(mine)
        def _():
            wait_rows(ls.at[L_FL], 2 * (IR + 8) * LT)

        @pl.when(jnp.logical_not(mine))
        def _():
            @pl.when(at_end)
            def _():
                wait_rows(rs.at[R_F + c], 2 * (IR + 8) * LT + 40)

            @pl.when(jnp.logical_not(at_end))
            def _():
                wait_rows(rs.at[R_F + c], 2 * (IR + 16) * LT + 40)

            for k in range(2):
                for s in range(10):
                    m = 10 * k + s
                    FL[k, c, LT, pl.ds(8 + 8 * s, 8), :] = pltpu.roll(
                        PKI[c, m // 4], (128 - (32 * (m % 4) + 16)) % 128, 1)

        def prepare(i, carry):
            r = pl.ds(pl.multiple_of(8 * i + 8, 8), 8)
            for j in range(NT):
                cov = CV[c, j, r, :]
                thc = TH[c, j, r, :] * cov
                scale = cov / (thc + (1.0 + STEP * DRAG))
                C1[c, j, r, :] = scale * (thc + 1.0)
                C2[c, j, r, :] = scale * STEP
                TH[c, j, r, :] = thc * (RELAX * STRENGTH / (1.0 + RELAX))
                for k in range(2):
                    W[k, c, j, r, :] = W[k, c, j, r, :] + FL[k, c, j, r, :] * DRAG
            return carry
        lax.fori_loop(0, IR // 8 + 2, prepare, 0)

        keep = 1.0 / (1.0 + RELAX)

        def group(r):
            rr = pl.ds(r, 8)
            u = [V[0, c, j, rr, :] for j in range(NT)]
            v = [V[1, c, j, rr, :] for j in range(NT)]
            ue, ve = east(u, lane), east(v, lane)
            s0, s1, s2 = [], [], []
            for j in range(NT):
                dux = V[0, c, j, pl.ds(r + 1, 8), :] - u[j]
                dvx = V[1, c, j, pl.ds(r + 1, 8), :] - v[j]
                duy, dvy = ue[j] - u[j], ve[j] - v[j]
                ed, et, es = dux + dvy, dux - dvy, duy + dvx
                inv = lax.rsqrt(ed * ed + et * et + es * es + 1.0)
                a = TH[c, j, rr, :]
                ai = a * inv
                s0.append(S[0, c, j, rr, :] * keep + (ed * ai - a))
                s1.append(S[1, c, j, rr, :] * keep + et * ai)
                s2.append(S[2, c, j, rr, :] * keep + es * ai)
                S[0, c, j, rr, :] = s0[j]
                S[1, c, j, rr, :] = s1[j]
                S[2, c, j, rr, :] = s2[j]
            dif = [s0[j] - s1[j] for j in range(NT)]
            dw, sw = west(dif, lane), west(s2, lane)
            above = pl.ds(r - 1, 8)
            for j in range(NT):
                tot_up = S[0, c, j, above, :] + S[1, c, j, above, :]
                f0 = 0.5 * ((s0[j] + s1[j]) - tot_up) + (s2[j] - sw[j])
                f1 = 0.5 * (dif[j] - dw[j]) + (s2[j] - S[2, c, j, above, :])
                c1, c2 = C1[c, j, rr, :], C2[c, j, rr, :]
                V[0, c, j, rr, :] = c1 * u[j] + c2 * (f0 + W[0, c, j, rr, :])
                V[1, c, j, rr, :] = c1 * v[j] + c2 * (f1 + W[1, c, j, rr, :])

        def subcycle(n, carry):
            for i in range(IR // 8 + 2):
                group(8 + 8 * i)
            return carry
        lax.fori_loop(0, NSUB, subcycle, 0)

        for j in range(LT):
            local(V.at[:, c, j, pl.ds(16, IR), :], o_vel.at[:, c, :, cols(j)], L_OUT)
            local(S.at[:, c, j, pl.ds(16, IR), :], o_str.at[:, c, :, cols(j)], L_OUT)

        prev = [zero] * NT
        pack = zero
        for i in range(IR // 8):
            rr = pl.ds(16 + 8 * i, 8)
            p0, p1 = [], []
            for j in range(NT):
                cov = CV[c, j, rr, :] * DRAG
                p0.append(cov * (V[0, c, j, rr, :] - FL[0, c, j, rr, :]))
                p1.append(cov * (V[1, c, j, rr, :] - FL[1, c, j, rr, :]))
            pw = west(p1, lane)
            for j in range(NT):
                turned = pltpu.roll(p0[j], 1, 0)
                above = jnp.where(sub == 0, prev[j], turned)
                prev[j] = turned
                sp = (p0[j] - above) + (p1[j] - pw[j])
                if j < LT:
                    SPB[c, j, pl.ds(8 * i, 8), :] = sp
                else:
                    pack = jnp.where(lane // 16 == i, pltpu.roll(sp, 16 * i + 8, 1), pack)
        XB[c, 0] = pack
        extra = zero
        for j in range(NT):
            extra = jnp.where(sub == j, -jnp.broadcast_to(prev[j][0:1, :], (8, 128)), extra)
        XB[c, 1] = extra

        @pl.when(mine)
        def _():
            for j in range(LT):
                for i in range(IR // 8):
                    RSP[g, j, pl.ds(8 * i, 8), :] = SPB[c, j, pl.ds(8 * i, 8), :]
            RX[g, 0] = XB[c, 0]
            RX[g, 1] = XB[c, 1]

        @pl.when(jnp.logical_not(mine))
        def _():
            dev = (c * (G - 1), t)
            send(SPB.at[c], RSP.at[g], S_RS + c, R_RS + g, dev)
            send(XB.at[c], RX.at[g], S_RS + c, R_RS + g, dev)

        @pl.when(at_end)
        def _():
            at = jnp.where(c == 0, IR - 8, 0)
            dev = (1 + c, t)
            send(SPB.at[c, :, pl.ds(pl.multiple_of(at, 8), 8), :], RH, S_RH, R_RH, dev)
            send(XB.at[c], RXH, S_RH, R_RH, dev)

    def caps(turn, carry):
        cap(jnp.where(turn == 0, first_cap, 1 - first_cap))
        return carry

    def ocean_rows(body, carry, unroll=2):
        def step(i, cc):
            for m in range(unroll):
                cc = body(pl.multiple_of(8 * (unroll * i + m) + 16, 8), cc)
            return cc
        return lax.fori_loop(0, OR // 8 // unroll, step, carry)

    def shifted_sum(ref, r):
        rr = pl.ds(r, 8)
        mid = [ref[j, rr, :] for j in range(NT)]
        e, w = east(mid, lane), west(mid, lane)
        return mid, [
            (ref[j, pl.ds(r + 1, 8), :] + ref[j, pl.ds(r - 1, 8), :]) + (e[j] + w[j])
            for j in range(NT)
        ]

    def ocean_prepare():
        @pl.when(has_u)
        def _():
            wait_rows(rs.at[R_OU], 24 * NT)

        @pl.when(has_d)
        def _():
            wait_rows(rs.at[R_OD], 24 * NT)

        def first(r, carry):
            rr = pl.ds(r, 8)
            for j in range(NT):
                gg = D[j, rr, :] * WET[j, rr, :]
                D[j, rr, :] = gg
                Y0[j, rr, :] = gg * X[j, rr, :]
            return carry

        def second(r, carry):
            rr = pl.ds(r, 8)
            gs, gn = shifted_sum(D, r)
            _, xn = shifted_sum(Y0, r)
            for j in range(NT):
                diag = gs[j] * gn[j] + DAMP
                inv = 1.0 / diag
                wid = WET[j, rr, :] * inv
                h = gs[j] * inv
                DG[j, rr, :] = diag
                WID[j, rr, :] = wid
                H[j, rr, :] = h
                Z[j, rr, :] = wid * B[j, rr, :] + h * xn[j] - X[j, rr, :]
            return carry
        for body in (first, second):
            body(8, 0)
            ocean_rows(body, 0)
            body(OR + 16, 0)

    def both(turn, carry):
        @pl.when(turn == 1)
        def _():
            ocean_prepare()
        return caps(turn, carry)
    lax.fori_loop(0, 2, both, 0)

    @pl.when(is_owner)
    def _():
        for d in range(G):
            @pl.when(g != d)
            def _(d=d):
                wait_rows(rs.at[R_RS + d], LT * IR + 16)
        for d in range(G):
            for i in range(IR // 8):
                rr = pl.ds(16 + IR * d + 8 * i, 8)
                for j in range(NT):
                    if j < LT:
                        sp = RSP[d, j, pl.ds(8 * i, 8), :]
                    else:
                        sp = pltpu.roll(RX[d, 0], 128 - (16 * i + 8), 1)
                    if i == 0 and d > 0:
                        more = jnp.broadcast_to(RX[d - 1, 1][j:j + 1, :], (8, 128))
                        sp = sp + jnp.where(sub == 0, more, 0.0)
                    Z[j, rr, :] = Z[j, rr, :] + WID[j, rr, :] * sp

    @pl.when(g == 0)
    def _():
        rr = pl.ds(OR + 16, 8)
        for j in range(NT):
            more = jnp.broadcast_to(RX[G - 1, 1][j:j + 1, :], (8, 128))
            Z[j, rr, :] = Z[j, rr, :] + WID[j, rr, :] * jnp.where(sub == 0, more, 0.0)

    @pl.when(jnp.logical_not(is_owner))
    def _():
        wait_rows(rs.at[R_RH], LT * 8 + 16)

        @pl.when(g == 1)
        def _():
            rr = pl.ds(16, 8)
            for j in range(NT):
                more = jnp.broadcast_to(RXH[1][j:j + 1, :], (8, 128))
                Z[j, rr, :] = Z[j, rr, :] + WID[j, rr, :] * jnp.where(sub == 0, more, 0.0)
        for at, row, i in ((1, 8, 7), (2, OR + 16, 0)):
            @pl.when(g == at)
            def _(row=row, i=i):
                rr = pl.ds(row, 8)
                for j in range(NT):
                    sp = RH[j] if j < LT else pltpu.roll(RXH[0], 128 - (16 * i + 8), 1)
                    Z[j, rr, :] = Z[j, rr, :] + WID[j, rr, :] * sp

    def krylov0(r, acc):
        rr = pl.ds(r, 8)
        for j in range(NT):
            z = Z[j, rr, :]
            Y0[j, rr, :] = D[j, rr, :] * z
            if j < LT and acc is not None:
                acc = acc + DG[j, rr, :] * z * z
        return acc

    def krylov(src, dst, vec, r, acc):
        rr = pl.ds(r, 8)
        y, n = shifted_sum(src, r)
        if acc is not None:
            odd, even = acc
        for j in range(NT):
            v = H[j, rr, :] * n[j]
            out = D[j, rr, :] * v
            vec[j, rr, :] = v
            dst[j, rr, :] = out
            if j < LT and acc is not None:
                odd = odd + y[j] * n[j]
                even = even + out * n[j]
        return None if acc is None else (odd, even)

    def last(r, acc):
        y, n = shifted_sum(Y2, r)
        for j in range(LT):
            acc = acc + y[j] * n[j]
        return acc

    krylov0(8, None)
    krylov0(OR + 16, None)
    moments = [ocean_rows(krylov0, zero)]
    for src, dst, vec in ((Y0, Y1, V1), (Y1, Y2, V2)):
        step = functools.partial(krylov, src, dst, vec)
        step(8, None)
        step(OR + 16, None)
        moments += list(ocean_rows(step, (zero, zero)))
    moments.append(ocean_rows(last, zero))

    tile = zero
    for k, m in enumerate(moments):
        tile = jnp.where(sub == k, jnp.sum(m, axis=0, keepdims=True), tile)
    slot1 = 2 * g + core
    L1[slot1] = tile
    for dev in peers1:
        send(L1.at[slot1], L1.at[slot1], S_1, R_1, dev)
    wait_rows(rs.at[R_1], 8 * len(peers1))
    tile = L1[0]
    for k in range(1, 8):
        tile = tile + L1[k]
    L2[mine2] = tile
    for dev in peers2:
        send(L2.at[mine2], L2.at[mine2], S_2, R_2, dev)
    wait_rows(rs.at[R_2], 8 * len(peers2))
    tile = L2[0]
    for k in range(1, M2):
        tile = tile + L2[k]
    total = jnp.sum(tile, axis=1, keepdims=True)
    mu = [total[k:k + 1, :] for k in range(6)]
    nu = [mu[k] - mu[k + 1] for k in range(5)]

    a0 = mu[0] / nu[0]
    z10, z11 = 1.0 - a0, a0
    rz1 = z11 * (z10 * mu[1] + z11 * mu[2])
    b0 = rz1 / mu[0]
    p10, p11 = z10 + b0, z11
    a1 = rz1 / (p11 * (p10 * nu[1] + p11 * nu[2]))
    z20, z21, z22 = z10 - a1 * p10, z11 - a1 * (p11 - p10), a1 * p11
    rz2 = z22 * (z20 * mu[2] + z21 * mu[3] + z22 * mu[4])
    b1 = rz2 / rz1
    p20, p21, p22 = z20 + b1 * p10, z21 + b1 * p11, z22
    a2 = rz2 / (p22 * (p20 * nu[2] + p21 * nu[3] + p22 * nu[4]))
    k0 = jnp.broadcast_to(a0 + a1 * p10 + a2 * p20, (8, 128))
    k1 = jnp.broadcast_to(a1 * p11 + a2 * p21, (8, 128))
    k2 = jnp.broadcast_to(a2 * p22, (8, 128))

    def finish(r, carry):
        rr = pl.ds(r, 8)
        for j in range(LT):
            OUT[j, pl.ds(pl.multiple_of(r - 16, 8), 8), :] = X[j, rr, :] + (
                k0 * Z[j, rr, :] + (k1 * V1[j, rr, :] + k2 * V2[j, rr, :]))
        return carry
    ocean_rows(finish, 0)
    for j in range(LT):
        local(OUT.at[j], o_ssh.at[:, cols(j)], L_OUTS)
    wait_rows(ls.at[L_OUTS], OR * LT)
    wait_rows(ls.at[L_OUT], 5 * 2 * IR * LT)

    for s, cond in ((S_CL, jnp.logical_and(is_owner, has_l)), (S_CR, jnp.logical_and(is_owner, has_r))):
        @pl.when(cond)
        def _(s=s):
            wait_rows(ss.at[s], 2 * OR)
    for s, cond in ((S_L, has_l), (S_R, has_r)):
        @pl.when(cond)
        def _(s=s):
            wait_rows(ss.at[s], 8 * 2 * IR + 3 * OR)
    for s, cond in ((S_U, has_u), (S_D, has_d)):
        @pl.when(cond)
        def _(s=s):
            wait_rows(ss.at[s], (8 * 2 + 3) * 8 * NT)

    @pl.when(is_owner)
    def _():
        wait_rows(ss.at[S_F], 2 * LT * (2 * (IR + 16) + IR + 8) + 3 * 40)
    for c in range(2):
        mine = jnp.logical_and(is_owner, c == owner_cap)

        @pl.when(jnp.logical_not(mine))
        def _(c=c):
            wait_rows(ss.at[S_RS + c], LT * IR + 16)

    @pl.when(is_owner)
    def _():
        wait_rows(ss.at[S_RH], LT * 8 + 16)
    wait_rows(ss.at[S_1], 8 * len(peers1))
    wait_rows(ss.at[S_2], 8 * len(peers2))
    for dy, dx, cond in nbrs:
        k = 3 * (1 - dy) + (1 - dx)
        @pl.when(cond)
        def _(dy=dy, dx=dx, k=k):
            dev = (g + dy, t + dx)
            pltpu.make_async_remote_copy(
                src_ref=iblk, dst_ref=BI.at[1 - dy, 1 - dx], send_sem=ss.at[S_BI + k],
                recv_sem=rs.at[R_BI + k], device_id=dev, device_id_type=MESH).wait_send()
            rows = pl.ds(0, OR // BS) if dy == 0 else pl.ds(0 if dy < 0 else OR // BS - 8, 8)
            pltpu.make_async_remote_copy(
                src_ref=land.at[rows], dst_ref=BO.at[1 - dy, 1 - dx, rows], send_sem=ss.at[S_BO + k],
                recv_sem=rs.at[R_BO + k], device_id=dev, device_id_type=MESH).wait_send()


def shards(T, *args):
    ice = (2, NT, IH, 128)
    ocean = (NT, OH, 128)
    vm = lambda *s: pltpu.VMEM(s, F32)
    scratch = [
        vm(2, *ice), vm(3, *ice), vm(2, *ice), vm(*ice), vm(2, *ice), vm(*ice), vm(*ice), vm(*ice),
        vm(2, 2, 2, 8, 128), vm(2, 3, 2, 8, 128), vm(2, 2, 2, 8, 128), vm(2, 2, 8, 128), vm(2, 3, 8, 128),
        vm(2, 2, 2, IR, 128), vm(2, 3, 2, IR, 128), vm(2, 2, 2, IR, 128), vm(2, 2, IR, 128),
        vm(2, 2, OR, 128), vm(3, 2, OR, 128),
        *[vm(*ocean) for _ in range(13)],
        pltpu.VMEM((3, 3, 2, 8, 64), jnp.int32), pltpu.VMEM((3, 3, 32, 64), jnp.int32),
        vm(3, 5, 8, 128), vm(2, 5, 8, 128), vm(2, LT, IR, 128), vm(2, 2, 8, 128),
        vm(G, LT, IR, 128), vm(G, 2, 8, 128), vm(LT, 8, 128), vm(2, 8, 128),
        vm(8, 8, 128), vm(T // 2, 8, 128), vm(LT, OR, 128), vm(DUMMY, 128),
        pltpu.SemaphoreType.DMA((N_R,)), pltpu.SemaphoreType.DMA((N_S,)), pltpu.SemaphoreType.DMA((N_L,)),
    ]
    hbm = pl.BlockSpec(memory_space=pltpu.HBM)
    return pl.pallas_call(
        functools.partial(kernel, T),
        out_shape=(
            jax.ShapeDtypeStruct((OR, 128 * LT), F32),
            jax.ShapeDtypeStruct((2, 2, IR, 128 * LT), F32),
            jax.ShapeDtypeStruct((3, 2, IR, 128 * LT), F32),
        ),
        in_specs=[hbm] * 10,
        out_specs=(hbm, hbm, hbm),
        scratch_shapes=scratch,
        compiler_params=pltpu.CompilerParams(
            collective_id=0, has_side_effects=True, vmem_limit_bytes=60 * 1024 * 1024),
    )(*args)


def solution(mesh):
    return jax.shard_map(
        functools.partial(shards, mesh.shape["tile"]),
        mesh=mesh,
        in_specs=(
            P("grp", "tile"),
            P("grp", "tile"),
            P("grp", "tile"),
            P(None, "grp", "tile"),
            P("grp", "tile"),
            P(None, "grp", "tile"),
            P(None, "grp", "tile"),
            P(None, None, "grp", "tile"),
            P(None, None, "grp", "tile"),
            P(None, None, "grp", "tile"),
        ),
        out_specs=(P("grp", "tile"), P(None, None, "grp", "tile"), P(None, None, "grp", "tile")),
        check_vma=False,
    )
```

time: 342 us -> 72.3 us (0.21); the launches traced: 336 us -> 72.1 us
  blocking collectives: 107 us -> 0 us
  starting transfers between devices: 77.7 us -> 0 us
  Pallas kernels: 0 us -> 66.8 us
  other arithmetic: 56.1 us -> 0 us
  waiting for transfers between devices: 44.4 us -> 0 us
  local copies, waits for them, and re-layouts: 39.4 us -> 4.69 us
  between operations: 11.6 us -> 0.65 us
    psum x12 -> x0, blocking collectives: 107 us -> none  [by_axis(): array = lax.psum(array, axis)]
    ppermute x24 -> x0, starting transfers between devices: 68.9 us -> none  [the longest x10 39 us: with_halo(): lax.ppermute(last, axis, up)]
    pallas_call x0 -> x1, Pallas kernels: none -> 66.8 us  [shards(): pl.pallas_call(functools.partial(kernel, T), out_shape=(jax.ShapeDtypeStr...]
    all_to_all x2 -> x0, waiting for transfers between devices: 29.9 us -> none  [the longest x1 22.3 us: shards(): lax.all_to_all(outgoing, 'grp', split_axis=2, concat_axis=2, tiled=True)]
    ppermute x24 -> x0, waiting for transfers between devices: 14.4 us -> none  [the longest x2 5.93 us: extended(): after = lax.ppermute(first, axis, down)]
    another operation x23 -> x0, other arithmetic: 13.3 us -> none  [the longest x8 5.06 us: stress_force(): return jnp.stack([force_x, force_y])]
    mul x18 -> x0, other arithmetic: 12.9 us -> none  [the longest x7 6.91 us: relax_stress(): (previous[0] + RELAX * strength * (div_rate / deformation - 1.0)) * relax...]
    slice x19 -> x0, local copies, waits for them, and re-layouts: 11.4 us -> none  [the longest x6 3.43 us: with_halo(): last = lax.slice_in_dim(array, length - width, length, axis=dim)]
  transfers between devices with their start and end apart: 26 -> 0, of which waited for: 8 -> 0; matrix products, arithmetic and copies ran while one was open for 9% -> 0% of each run, Pallas kernels for 0% -> 0%
where the time goes in v1:
time: 72.3 us; the launch traced here: 72.1 us
  Pallas kernels  66.8 us (92%)
  local copies, waits for them, and re-layouts  4.69 us (6%)
    pallas_call x1, Pallas kernels, shards(): pl.pallas_call(functools.partial(kernel, T), out_shape=(jax.ShapeDtypeStr...  66.8 us
    unnamed x5, local copies, waits for them, and re-layouts  4.69 us

profile of v1, /device:TPU:1, one launch (start us, length us, event | category | flops | bytes accessed | tf_op | source)
XLA Modules:
  0.0 72.1 jit_solution(1378464288882276472)
XLA Ops:
  0.6 66.8 %shard_map.121 = (f32[256,512]{1,0:T(8,128)}, f32[2,2,64,512]{3,2,1,0:T(8,128)}, f32[3,2,64,512]{3,2,1,0:T(8,128)}) custom-call(f32[256,512]{1,0:T(8,128)} %base.1, f32[256,512]{1,0:T(8,128)} %depth.1, f32[256,512]{1,0:T(8,128)} %ssh.1, f32[2,256,512]{2,1,0:T(8,128)} %cur.1, s32[32,64]{1,0:T(8,128)} %land.1, f32[2,64,512]{2,1,0:T(8,128)} %thick.1, ...), custom_call_target="tpu_custom_call" | custom-call | tf_op jit(solution)/shard_map/pallas_call | solution.py:816
  67.4 0.0 copy-start
  67.4 1.9 %copy.16 = f32[256,512]{1,0:T(8,128)} copy(f32[256,512]{1,0:T(8,128)} %get-tuple-element.6) | data formatting | bytes 1048576
  69.4 1.9 %copy.17 = f32[2,2,64,512]{3,2,1,0:T(8,128)} copy(f32[2,2,64,512]{3,2,1,0:T(8,128)} %get-tuple-element.7) | data formatting | bytes 1048576
  71.2 0.0 copy-done
  71.2 0.9 %copy.18 = f32[3,2,64,512]{3,2,1,0:T(8,128)} copy(f32[3,2,64,512]{3,2,1,0:T(8,128)S(1)} %copy-done) | data formatting | bytes 1572864
Async XLA Ops:
  67.4 3.8 %copy-start = (f32[3,2,64,512]{3,2,1,0:T(8,128)S(1)}, f32[3,2,64,512]{3,2,1,0:T(8,128)}, u32[]{:S(2)}) copy-start(f32[3,2,64,512]{3,2,1,0:T(8,128)} %get-tuple-element.8) | copy-start | bytes 2359300

commit v2 on v1

--- a/solution.py
+++ b/solution.py
@@ -25,17 +25,17 @@
 MESH = pl.DeviceIdType.MESH
 DUMMY = 4096
 
-R_CL, R_CR, R_IL, R_IR, R_OL, R_OR = 0, 1, 2, 3, 4, 5
-R_IU, R_ID, R_F = 6, 8, 10
-R_OU, R_OD, R_RS, R_RH, R_1, R_2 = 12, 13, 14, 18, 19, 20
-R_BI, R_BO = 21, 30
-N_R = 39
-S_CL, S_CR, S_L, S_R, S_U, S_D, S_F, S_RS, S_1, S_2 = 0, 1, 2, 3, 4, 5, 6, 7, 9, 10
+R_PL, R_PR, R_IL, R_IR, R_OL, R_OR = 41, 43, 4, 5, 6, 7
+R_IU, R_ID, R_F = 8, 10, 12
+R_OU, R_OD, R_RS, R_RH, R_1, R_2 = 14, 15, 16, 20, 21, 22
+R_BI, R_BO = 23, 32
+N_R = 45
+S_FL, S_FR, S_L, S_R, S_U, S_D, S_F, S_RS, S_1, S_2 = 0, 1, 2, 3, 4, 5, 6, 7, 9, 10
 S_RH = 11
 S_BI, S_BO = 12, 21
 N_S = 30
-L_BLK, L_ICE, L_FL, L_OC, L_OUT, L_OUTS = 0, 1, 2, 3, 4, 5
-N_L = 6
+L_BLK, L_ICE, L_FL, L_OC, L_OUT, L_OUTS, L_ED = 0, 1, 2, 3, 4, 5, 6
+N_L = 7
 
 
 def east(tiles, lane):
@@ -46,16 +46,29 @@
 def west(tiles, lane):
     turned = [pltpu.roll(x, 1, 1) for x in tiles]
     return [jnp.where(lane == 0, turned[(j - 1) % NT], turned[j]) for j in range(NT)]
+
+
+class Phases:
+    def __init__(self):
+        self.open = None
+
+    def __call__(self, name):
+        if self.open is not None:
+            self.open.__exit__(None, None, None)
+        self.open = None
+        if name:
+            self.open = jax.named_scope(name)
+            self.open.__enter__()
 
 
 def kernel(
     T,
     base, depth, ssh, cur, land, thick, iblk, ivel, istr, wind,
     o_ssh, o_vel, o_str,
-    V, S, W, TH, FL, CV, C1, C2, EV, ES, EW, ETH, EO,
-    LV, LS, LW, LTH, LC, LO,
+    V, S, W, TH, FL, CV, C1, C2,
+    PI, LI, PC, LC, PF, LF, PH, LH, PHO, LHO, CE,
     B, D, X, Z, Y0, Y1, Y2, H, WID, DG, WET, V1, V2,
-    BI, BO, PKO, PKI, SPB, XB, RSP, RX, RH, RXH, L1, L2, OUT, DUM,
+    BI, BO, SPB, XB, RSP, RX, RH, RXH, L1, L2, OUT, DUM,
     rs, ss, ls,
 ):
     g = lax.axis_index("grp")
@@ -94,6 +107,8 @@
                     cond = there if cond is None else jnp.logical_and(cond, there)
             nbrs.append((dy, dx, cond))
 
+    phase = Phases()
+    phase("loads")
     local(iblk, BI.at[1, 1], L_BLK)
     local(land, BO.at[1, 1], L_BLK)
     for j in range(LT):
@@ -105,114 +120,35 @@
         local(depth.at[:, cols(j)], D.at[j, pl.ds(16, OR), :], L_OC)
         local(ssh.at[:, cols(j)], X.at[j, pl.ds(16, OR), :], L_OC)
 
+    @pl.when(is_owner)
+    def _():
+        local(cur.at[:, :, cols(0)], CE.at[0], L_ED)
+        local(cur.at[:, :, cols(LT - 1)], CE.at[1], L_ED)
+
+    phase("signal")
     barrier = pltpu.get_barrier_semaphore()
     core = lax.rem(t, 2)
-    for dy, dx, cond in nbrs:
-        @pl.when(cond)
-        def _(dy=dy, dx=dx):
-            pl.semaphore_signal(barrier, inc=1, device_id=(g + dy, t + dx), device_id_type=MESH)
+    M2 = T // 2
+    mine2 = t // 2
     peers1 = []
     for dg in range(G):
         for dc in range(2):
             if dg or dc:
                 peers1.append((lax.rem(g + dg, G), t - core + lax.rem(core + dc, 2)))
-    M2 = T // 2
-    mine2 = t // 2
     peers2 = [(g, 2 * lax.rem(mine2 + k, M2) + core) for k in range(1, M2)]
-    for dev in peers1 + peers2:
+    for dg in range(G):
+        for dx, cond in ((-1, has_l), (0, None), (1, has_r)):
+            dev = (lax.rem(g + dg, G), t + dx)
+            if cond is not None:
+                @pl.when(cond)
+                def _(dev=dev):
+                    pl.semaphore_signal(barrier, inc=1, device_id=dev, device_id_type=MESH)
+            elif dg:
+                pl.semaphore_signal(barrier, inc=1, device_id=dev, device_id_type=MESH)
+    for dev in peers2:
         pl.semaphore_signal(barrier, inc=1, device_id=dev, device_id_type=MESH)
-    high = 1 + jnp.minimum(g, 1) + jnp.minimum(G - 1 - g, 1)
-    wide = 1 + jnp.minimum(t, 1) + jnp.minimum(T - 1 - t, 1)
-    pl.semaphore_wait(barrier, high * wide - 1 + len(peers1) + len(peers2))
-
-    left, right, up, down = (g, t - 1), (g, t + 1), (g - 1, t), (g + 1, t)
-
-    @pl.when(jnp.logical_and(is_owner, has_l))
-    def _():
-        send(cur.at[:, :, cols(0)], LC.at[1], S_CL, R_CR, left)
-
-    @pl.when(jnp.logical_and(is_owner, has_r))
-    def _():
-        send(cur.at[:, :, cols(LT - 1)], LC.at[0], S_CR, R_CL, right)
-
-    def flow_rows(d):
-        lo, hi = max(IR * d - 8, 0), min(IR * d + IR + 8, OR)
-        return lo, hi - lo, 16 + lo - IR * d
-
-    dests = {0: (1, 2, 3), G - 1: (2, 1, 0)}
-
-    def send_flow(c, d):
-        lo, n, at = flow_rows(d)
-        for j in range(LT):
-            send(cur.at[:, pl.ds(lo, n), cols(j)], FL.at[:, c, j, pl.ds(at, n), :],
-                 S_F, R_F + c, (d, t))
-
-    def halo_ice(dev, c, src, dst, s, r):
-        for j in range(LT):
-            send(ivel.at[:, c, pl.ds(src, 8), cols(j)], V.at[:, c, j, pl.ds(dst, 8), :], s, r, dev)
-            send(istr.at[:, c, pl.ds(src, 8), cols(j)], S.at[:, c, j, pl.ds(dst, 8), :], s, r, dev)
-            send(wind.at[:, c, pl.ds(src, 8), cols(j)], W.at[:, c, j, pl.ds(dst, 8), :], s, r, dev)
-            send(thick.at[c, pl.ds(src, 8), cols(j)], TH.at[c, j, pl.ds(dst, 8), :], s, r, dev)
-
-    for own, c in ((0, 0), (G - 1, 1)):
-        @pl.when(g == own)
-        def _(own=own, c=c):
-            send_flow(c, dests[own][0])
-            lo, n, at = flow_rows(own)
-            for j in range(LT):
-                local(cur.at[:, pl.ds(lo, n), cols(j)], FL.at[:, c, j, pl.ds(at, n), :], L_FL)
-
-    for turn in range(2):
-        for dev, cond, src, dst, s, r in (
-            (up, has_u, 0, IR + 16, S_U, R_ID),
-            (down, has_d, IR - 8, 8, S_D, R_IU),
-        ):
-            @pl.when(cond)
-            def _(dev=dev, src=src, dst=dst, s=s, r=r):
-                if turn == 0:
-                    at = 0 if s == S_U else OR - 8
-                    to = OR + 16 if s == S_U else 8
-                    ro = R_OD if s == S_U else R_OU
-                    for j in range(LT):
-                        send(base.at[pl.ds(at, 8), cols(j)], B.at[j, pl.ds(to, 8), :], s, ro, dev)
-                        send(depth.at[pl.ds(at, 8), cols(j)], D.at[j, pl.ds(to, 8), :], s, ro, dev)
-                        send(ssh.at[pl.ds(at, 8), cols(j)], X.at[j, pl.ds(to, 8), :], s, ro, dev)
-                there = dev[0] // 2
-                c = there if turn == 0 else 1 - there
-                halo_ice(dev, c, src, dst, s, r + c)
-        if turn == 0:
-            for own, c in ((0, 0), (G - 1, 1)):
-                @pl.when(g == own)
-                def _(own=own, c=c):
-                    for d in dests[own][1:]:
-                        send_flow(c, d)
-
-    for dy, dx, cond in nbrs:
-        k = 3 * (1 - dy) + (1 - dx)
-        @pl.when(cond)
-        def _(dy=dy, dx=dx, k=k):
-            dev = (g + dy, t + dx)
-            send(iblk, BI.at[1 - dy, 1 - dx], S_BI + k, R_BI + k, dev)
-            rows = pl.ds(0, OR // BS) if dy == 0 else pl.ds(0 if dy < 0 else OR // BS - 8, 8)
-            send(land.at[rows], BO.at[1 - dy, 1 - dx, rows], S_BO + k, R_BO + k, dev)
-
-    for dev, cond, side, at, s, ri, ro in (
-        (left, has_l, 1, 0, S_L, R_IR, R_OR),
-        (right, has_r, 0, LT - 1, S_R, R_IL, R_OL),
-    ):
-        @pl.when(cond)
-        def _(dev=dev, side=side, at=at, s=s, ri=ri, ro=ro):
-            send(ivel.at[:, :, :, cols(at)], LV.at[side], s, ri, dev)
-            send(istr.at[:, :, :, cols(at)], LS.at[side], s, ri, dev)
-            send(wind.at[:, :, :, cols(at)], LW.at[side], s, ri, dev)
-            send(thick.at[:, :, cols(at)], LTH.at[side], s, ri, dev)
-            send(base.at[:, cols(at)], LO.at[0, side], s, ro, dev)
-            send(depth.at[:, cols(at)], LO.at[1, side], s, ro, dev)
-            send(ssh.at[:, cols(at)], LO.at[2, side], s, ro, dev)
-
-    def fill(ref, idx):
-        ref[idx] = jnp.zeros(ref.at[idx].shape, ref.dtype)
-
+
+    phase("zeros")
     for cond, row, orow, by in ((g == 0, 8, 8, 0), (g == G - 1, IR + 16, OR + 16, 2)):
         @pl.when(cond)
         def _(row=row, orow=orow, by=by):
@@ -237,138 +173,220 @@
     for cond, side, bx in ((t == 0, 0, 0), (t == T - 1, 1, 2)):
         @pl.when(cond)
         def _(side=side, bx=bx):
-            def body(i, carry):
-                r = pl.ds(pl.multiple_of(8 * i, 8), 8)
-                for c in range(2):
-                    for k in range(3):
-                        LS[side, k, c, r, :] = zero
-                    for k in range(2):
-                        LV[side, k, c, r, :] = zero
-                        LW[side, k, c, r, :] = zero
-                    LTH[side, c, r, :] = zero
-                return carry
-            lax.fori_loop(0, IR // 8, body, 0)
-
-            def body2(i, carry):
-                r = pl.ds(pl.multiple_of(8 * i, 8), 8)
-                for k in range(2):
-                    LC[side, k, r, :] = zero
-                for k in range(3):
-                    LO[k, side, r, :] = zero
-                return carry
-            lax.fori_loop(0, OR // 8, body2, 0)
+            for c in range(2):
+                for k in range(8):
+                    LI[side, c, k] = zero
+                for v in range(3):
+                    LF[side, c, v] = zero
+            for k in range(3):
+                for v in range(4):
+                    LC[side, k, v] = zero
             for y in range(3):
                 for c in range(2):
                     BI[y, bx, c] = jnp.zeros((8, 64), jnp.int32)
                 BO[y, bx] = jnp.zeros((32, 64), jnp.int32)
 
+    phase("pack")
+    slot_of = lane // 16
+
+    def put(pack, e, at, x):
+        moved = pltpu.roll(x, 16 * at, 1) if at else x
+        return jnp.where(slot_of == (at - e) % 8, moved, pack)
+
+    def take(from_right, from_left, at):
+        both = jnp.where(slot_of == at, from_right, from_left)
+        return pltpu.roll(both, 128 - 16 * at, 1) if at else both
+
+    wait_rows(ls.at[L_ICE], 8 * 2 * IR * LT)
+
+    def ice_get(k, c, j, r):
+        if k < 2:
+            return V[k, c, j, pl.ds(r, 8), :]
+        if k < 5:
+            return S[k - 2, c, j, pl.ds(r, 8), :]
+        return W[k - 5, c, j, pl.ds(r, 8), :] if k < 7 else TH[c, j, pl.ds(r, 8), :]
+
+    def ice_set(k, c, j, r, x):
+        if k < 2:
+            V[k, c, j, pl.ds(r, 8), :] = x
+        elif k < 5:
+            S[k - 2, c, j, pl.ds(r, 8), :] = x
+        elif k < 7:
+            W[k - 5, c, j, pl.ds(r, 8), :] = x
+        else:
+            TH[c, j, pl.ds(r, 8), :] = x
+
+    for e, j in ((0, 0), (1, LT - 1)):
+        for c in range(2):
+            for k in range(8):
+                pack = zero
+                for i in range(IR // 8):
+                    pack = put(pack, e, i, ice_get(k, c, j, 16 + 8 * i))
+                PI[e, c, k] = pack
+
+    for own in (0, G - 1):
+        @pl.when(g == own)
+        def _(own=own):
+            wait_rows(ls.at[L_ED], 2 * 2 * OR)
+            for e in range(2):
+                for d in range(G):
+                    packs = [zero] * 3
+                    for k in range(2):
+                        for s in range(10):
+                            q = 8 * d - 1 + s
+                            if 0 <= q < OR // 8:
+                                m = 10 * k + s
+                                packs[m // 8] = put(packs[m // 8], e, m % 8, CE[e, k, pl.ds(8 * q, 8), :])
+                    for v in range(3):
+                        PF[e, d, v] = packs[v]
+
+    wait_rows(ls.at[L_OC], 3 * OR * LT)
+    for e, j in ((0, 0), (1, LT - 1)):
+        for k, ref in enumerate((B, D, X)):
+            for v in range(4):
+                pack = zero
+                for i in range(8):
+                    pack = put(pack, e, i, ref[j, pl.ds(16 + 64 * v + 8 * i, 8), :])
+                PC[e, k, v] = pack
+
+    phase("barrier")
+    wide = 1 + jnp.minimum(t, 1) + jnp.minimum(T - 1 - t, 1)
+    pl.semaphore_wait(barrier, G * wide - 1 + len(peers2))
+
+    phase("sends")
+    left, right, up, down = (g, t - 1), (g, t + 1), (g - 1, t), (g + 1, t)
+    for dy, dx, cond in nbrs:
+        k = 3 * (1 - dy) + (1 - dx)
+        @pl.when(cond)
+        def _(dy=dy, dx=dx, k=k):
+            dev = (g + dy, t + dx)
+            send(iblk, BI.at[1 - dy, 1 - dx], S_BI + k, R_BI + k, dev)
+            rows = pl.ds(0, OR // BS) if dy == 0 else pl.ds(0 if dy < 0 else OR // BS - 8, 8)
+            send(land.at[rows], BO.at[1 - dy, 1 - dx, rows], S_BO + k, R_BO + k, dev)
+
+    for e, dev, cond, s, ri, ro in ((0, left, has_l, S_L, R_IR, R_OR), (1, right, has_r, S_R, R_IL, R_OL)):
+        @pl.when(cond)
+        def _(e=e, dev=dev, s=s, ri=ri, ro=ro):
+            send(PI.at[e], LI.at[1 - e], s, ri, dev)
+            send(PC.at[e], LC.at[1 - e], s, ro, dev)
+
+    def flow_rows(d):
+        lo, hi = max(IR * d - 8, 0), min(IR * d + IR + 8, OR)
+        return lo, hi - lo, 16 + lo - IR * d
+
+    dests = {0: (1, 2, 3), G - 1: (2, 1, 0)}
+
+    def send_flow(c, d):
+        lo, n, at = flow_rows(d)
+        for j in range(LT):
+            send(cur.at[:, pl.ds(lo, n), cols(j)], FL.at[:, c, j, pl.ds(at, n), :],
+                 S_F, R_F + c, (d, t))
+
+    def halo_ice(dev, c, src, dst, s, r):
+        for j in range(LT):
+            send(ivel.at[:, c, pl.ds(src, 8), cols(j)], V.at[:, c, j, pl.ds(dst, 8), :], s, r, dev)
+            send(istr.at[:, c, pl.ds(src, 8), cols(j)], S.at[:, c, j, pl.ds(dst, 8), :], s, r, dev)
+            send(wind.at[:, c, pl.ds(src, 8), cols(j)], W.at[:, c, j, pl.ds(dst, 8), :], s, r, dev)
+            send(thick.at[c, pl.ds(src, 8), cols(j)], TH.at[c, j, pl.ds(dst, 8), :], s, r, dev)
+
+    def halo_turn(turn):
+        for dev, cond, src, dst, s, r in (
+            (up, has_u, 0, IR + 16, S_U, R_ID),
+            (down, has_d, IR - 8, 8, S_D, R_IU),
+        ):
+            @pl.when(cond)
+            def _(dev=dev, src=src, dst=dst, s=s, r=r):
+                there = dev[0] // 2
+                c = there if turn == 0 else 1 - there
+                halo_ice(dev, c, src, dst, s, r + c)
+
     for own, c in ((0, 0), (G - 1, 1)):
         @pl.when(g == own)
         def _(own=own, c=c):
-            @pl.when(has_l)
-            def _():
-                wait_rows(rs.at[R_CL], 2 * OR)
-
-            @pl.when(has_r)
-            def _():
-                wait_rows(rs.at[R_CR], 2 * OR)
-
-            def merged(k, q):
-                r = pl.ds(8 * q, 8)
-                return jnp.where(lane < 64, LC[1, k, r, :], LC[0, k, r, :])
-
-            for k in range(2):
-                for s in range(10):
-                    q = 8 * own - 1 + s
-                    if 0 <= q < OR // 8:
-                        FL[k, c, LT, pl.ds(8 + 8 * s, 8), :] = merged(k, q)
-            for at, d in enumerate(dests[own]):
-                packs = [zero] * 5
-                for k in range(2):
-                    for s in range(10):
-                        q = 8 * d - 1 + s
-                        if 0 <= q < OR // 8:
-                            m = 10 * k + s
-                            slot = m % 4
-                            moved = pltpu.roll(merged(k, q), (32 * slot + 16) % 128, 1)
-                            packs[m // 4] = jnp.where(lane // 32 == slot, moved, packs[m // 4])
-                for v in range(5):
-                    PKO[at, v] = packs[v]
-                send(PKO.at[at], PKI.at[c], S_F, R_F + c, (d, t))
-
-    wait_rows(ls.at[L_ICE], 8 * 2 * IR * LT)
-
+            for e, dx, cond, s, r in ((0, -1, has_l, S_FL, R_PR), (1, 1, has_r, S_FR, R_PL)):
+                @pl.when(cond)
+                def _(e=e, dx=dx, s=s, r=r):
+                    for dg in range(G):
+                        d = dg if own == 0 else G - 1 - dg
+                        dev = (g + dg if own == 0 else g - dg, t + dx)
+                        send(PF.at[e, d], LF.at[1 - e, c], s, r + c, dev)
+            send_flow(c, dests[own][0])
+            lo, n, at = flow_rows(own)
+            for j in range(LT):
+                local(cur.at[:, pl.ds(lo, n), cols(j)], FL.at[:, c, j, pl.ds(at, n), :], L_FL)
+    halo_turn(0)
+
+    phase("mergeice")
     @pl.when(has_l)
     def _():
-        wait_rows(rs.at[R_IL], 8 * 2 * IR)
+        wait_rows(rs.at[R_IL], 2 * 8 * 8)
 
     @pl.when(has_r)
     def _():
-        wait_rows(rs.at[R_IR], 8 * 2 * IR)
-
+        wait_rows(rs.at[R_IR], 2 * 8 * 8)
+
+    quarter = lane // 32
     for c in range(2):
-        def merge_ice(i, carry, c=c):
-            r = pl.ds(pl.multiple_of(8 * i, 8), 8)
-            w = pl.ds(pl.multiple_of(8 * i + 16, 8), 8)
-            for k in range(2):
-                V[k, c, LT, w, :] = jnp.where(lane < 64, LV[1, k, c, r, :], LV[0, k, c, r, :])
-                W[k, c, LT, w, :] = jnp.where(lane < 64, LW[1, k, c, r, :], LW[0, k, c, r, :])
-            for k in range(3):
-                S[k, c, LT, w, :] = jnp.where(lane < 64, LS[1, k, c, r, :], LS[0, k, c, r, :])
-            TH[c, LT, w, :] = jnp.where(lane < 64, LTH[1, c, r, :], LTH[0, c, r, :])
-            return carry
-        lax.fori_loop(0, IR // 8, merge_ice, 0)
-
-    for e, dev, cond, src, dst, s, r in (
-        (0, up, has_u, 16, IR + 16, S_U, R_ID),
-        (1, down, has_d, IR + 8, 8, S_D, R_IU),
+        ends = [[zero, zero], [zero, zero]]
+        for k in range(8):
+            for i in range(IR // 8):
+                x = take(LI[1, c, k], LI[0, c, k], i)
+                ice_set(k, c, LT, 16 + 8 * i, x)
+                for e, at in ((0, 0), (1, IR // 8 - 1)):
+                    if i == at:
+                        moved = pltpu.roll(x, (32 * (k % 4) + 16) % 128, 1)
+                        ends[e][k // 4] = jnp.where(quarter == k % 4, moved, ends[e][k // 4])
+        for e in range(2):
+            for v in range(2):
+                PH[e, c, v] = ends[e][v]
+    for e, dev, cond, s, r in ((0, up, has_u, S_U, R_ID), (1, down, has_d, S_D, R_IU)):
+        @pl.when(cond)
+        def _(e=e, dev=dev, s=s, r=r):
+            for c in range(2):
+                send(PH.at[e, c], LH.at[1 - e, c], s, r + c, dev)
+
+    for own, c in ((0, 0), (G - 1, 1)):
+        @pl.when(g == own)
+        def _(own=own, c=c):
+            for d in dests[own][1:]:
+                send_flow(c, d)
+    halo_turn(1)
+    for dev, cond, at, to, s, r in (
+        (up, has_u, 0, OR + 16, S_U, R_OD),
+        (down, has_d, OR - 8, 8, S_D, R_OU),
     ):
         @pl.when(cond)
-        def _(e=e, dev=dev, src=src, dst=dst, s=s, r=r):
-            a, b = pl.ds(src, 8), pl.ds(dst, 8)
-            for c in range(2):
-                for k in range(3):
-                    ES[e, k, c] = S[k, c, LT, a, :]
-                for k in range(2):
-                    EV[e, k, c] = V[k, c, LT, a, :]
-                    EW[e, k, c] = W[k, c, LT, a, :]
-                ETH[e, c] = TH[c, LT, a, :]
-            for turn in range(2):
-                there = dev[0] // 2
-                c = there if turn == 0 else 1 - there
-                send(EV.at[e, :, c], V.at[:, c, LT, b, :], s, r + c, dev)
-                send(ES.at[e, :, c], S.at[:, c, LT, b, :], s, r + c, dev)
-                send(EW.at[e, :, c], W.at[:, c, LT, b, :], s, r + c, dev)
-                send(ETH.at[e, c], TH.at[c, LT, b, :], s, r + c, dev)
-
-    wait_rows(ls.at[L_OC], 3 * OR * LT)
-
+        def _(dev=dev, at=at, to=to, s=s, r=r):
+            for j in range(LT):
+                send(base.at[pl.ds(at, 8), cols(j)], B.at[j, pl.ds(to, 8), :], s, r, dev)
+                send(depth.at[pl.ds(at, 8), cols(j)], D.at[j, pl.ds(to, 8), :], s, r, dev)
+                send(ssh.at[pl.ds(at, 8), cols(j)], X.at[j, pl.ds(to, 8), :], s, r, dev)
+
+    phase("mergeoc")
     @pl.when(has_l)
     def _():
-        wait_rows(rs.at[R_OL], 3 * OR)
+        wait_rows(rs.at[R_OL], 3 * 4 * 8)
 
     @pl.when(has_r)
     def _():
-        wait_rows(rs.at[R_OR], 3 * OR)
-
-    def merge_ocean(i, carry):
-        r = pl.ds(pl.multiple_of(8 * i, 8), 8)
-        w = pl.ds(pl.multiple_of(8 * i + 16, 8), 8)
-        for k, ref in enumerate((B, D, X)):
-            ref[LT, w, :] = jnp.where(lane < 64, LO[k, 1, r, :], LO[k, 0, r, :])
-        return carry
-    lax.fori_loop(0, OR // 8, merge_ocean, 0)
-    for e, dev, cond, src, dst, s, r in (
-        (0, up, has_u, 16, OR + 16, S_U, R_OD),
-        (1, down, has_d, OR + 8, 8, S_D, R_OU),
-    ):
-        @pl.when(cond)
-        def _(e=e, dev=dev, src=src, dst=dst, s=s, r=r):
-            for k, ref in enumerate((B, D, X)):
-                EO[e, k] = ref[LT, pl.ds(src, 8), :]
-            for k, ref in enumerate((B, D, X)):
-                send(EO.at[e, k], ref.at[LT, pl.ds(dst, 8), :], s, r, dev)
-
+        wait_rows(rs.at[R_OR], 3 * 4 * 8)
+
+    ends = [zero, zero]
+    for k, ref in enumerate((B, D, X)):
+        for q in range(OR // 8):
+            x = take(LC[1, k, q // 8], LC[0, k, q // 8], q % 8)
+            ref[LT, pl.ds(16 + 8 * q, 8), :] = x
+            for e, at in ((0, 0), (1, OR // 8 - 1)):
+                if q == at:
+                    moved = pltpu.roll(x, 32 * k + 16, 1)
+                    ends[e] = jnp.where(quarter == k, moved, ends[e])
+    for e, dev, cond, s, r in ((0, up, has_u, S_U, R_OD), (1, down, has_d, S_D, R_OU)):
+        PHO[e] = ends[e]
+        @pl.when(cond)
+        def _(e=e, dev=dev, s=s, r=r):
+            send(PHO.at[e], LHO.at[1 - e], s, r, dev)
+
+    phase("masks")
     pltpu.make_async_copy(iblk, BI.at[1, 1], ls.at[L_BLK]).wait()
     pltpu.make_async_copy(land, BO.at[1, 1], ls.at[L_BLK]).wait()
     for dy, dx, cond in nbrs:
@@ -423,14 +441,31 @@
             paint(WET, 16 + 64 * q + 8 * b, mid, b)
     paint(WET, OR + 16, spread_rows([BO[2, x, 0:8] for x in range(3)]), 0)
 
+    phase("")
     def cap(c):
-        @pl.when(has_u)
+        phase = Phases()
+        phase("capwait")
+
+        for e, cond, r, row in ((0, has_u, R_IU, 8), (1, has_d, R_ID, IR + 16)):
+            @pl.when(cond)
+            def _(e=e, r=r, row=row):
+                wait_rows(rs.at[r + c], 8 * 8 * LT + 16)
+                for k in range(8):
+                    x = pltpu.roll(LH[e, c, k // 4], (128 - 32 * (k % 4) - 16) % 128, 1)
+                    ice_set(k, c, LT, row, x)
+
+        @pl.when(has_l)
         def _():
-            wait_rows(rs.at[R_IU + c], 8 * 8 * NT)
-
-        @pl.when(has_d)
+            wait_rows(rs.at[R_PL + c], 24)
+
+        @pl.when(has_r)
         def _():
-            wait_rows(rs.at[R_ID + c], 8 * 8 * NT)
+            wait_rows(rs.at[R_PR + c], 24)
+
+        for k in range(2):
+            for s in range(10):
+                m = 10 * k + s
+                FL[k, c, LT, pl.ds(8 + 8 * s, 8), :] = take(LF[1, c, m // 8], LF[0, c, m // 8], m % 8)
 
         mine = jnp.logical_and(is_owner, c == owner_cap)
         at_end = jnp.logical_or(jnp.logical_and(c == 0, g == G - 1), jnp.logical_and(c == 1, g == 0))
@@ -443,18 +478,13 @@
         def _():
             @pl.when(at_end)
             def _():
-                wait_rows(rs.at[R_F + c], 2 * (IR + 8) * LT + 40)
+                wait_rows(rs.at[R_F + c], 2 * (IR + 8) * LT)
 
             @pl.when(jnp.logical_not(at_end))
             def _():
-                wait_rows(rs.at[R_F + c], 2 * (IR + 16) * LT + 40)
-
-            for k in range(2):
-                for s in range(10):
-                    m = 10 * k + s
-                    FL[k, c, LT, pl.ds(8 + 8 * s, 8), :] = pltpu.roll(
-                        PKI[c, m // 4], (128 - (32 * (m % 4) + 16)) % 128, 1)
-
+                wait_rows(rs.at[R_F + c], 2 * (IR + 16) * LT)
+
+        phase("prepare")
         def prepare(i, carry):
             r = pl.ds(pl.multiple_of(8 * i + 8, 8), 8)
             for j in range(NT):
@@ -469,6 +499,7 @@
             return carry
         lax.fori_loop(0, IR // 8 + 2, prepare, 0)
 
+        phase("subcycles")
         keep = 1.0 / (1.0 + RELAX)
 
         def group(r):
@@ -508,6 +539,7 @@
             return carry
         lax.fori_loop(0, NSUB, subcycle, 0)
 
+        phase("diverge")
         for j in range(LT):
             local(V.at[:, c, j, pl.ds(16, IR), :], o_vel.at[:, c, :, cols(j)], L_OUT)
             local(S.at[:, c, j, pl.ds(16, IR), :], o_str.at[:, c, :, cols(j)], L_OUT)
@@ -557,6 +589,7 @@
             dev = (1 + c, t)
             send(SPB.at[c, :, pl.ds(pl.multiple_of(at, 8), 8), :], RH, S_RH, R_RH, dev)
             send(XB.at[c], RXH, S_RH, R_RH, dev)
+        phase(None)
 
     def caps(turn, carry):
         cap(jnp.where(turn == 0, first_cap, 1 - first_cap))
@@ -579,14 +612,17 @@
         ]
 
     def ocean_prepare():
-        @pl.when(has_u)
-        def _():
-            wait_rows(rs.at[R_OU], 24 * NT)
-
-        @pl.when(has_d)
-        def _():
-            wait_rows(rs.at[R_OD], 24 * NT)
-
+        phase = Phases()
+        phase("oceanwait")
+
+        for e, cond, r, row in ((0, has_u, R_OU, 8), (1, has_d, R_OD, OR + 16)):
+            @pl.when(cond)
+            def _(e=e, r=r, row=row):
+                wait_rows(rs.at[r], 24 * LT + 8)
+                for k, ref in enumerate((B, D, X)):
+                    ref[LT, pl.ds(row, 8), :] = pltpu.roll(LHO[e], 128 - 32 * k - 16, 1)
+
+        phase("oceanprep")
         def first(r, carry):
             rr = pl.ds(r, 8)
             for j in range(NT):
@@ -613,14 +649,12 @@
             body(8, 0)
             ocean_rows(body, 0)
             body(OR + 16, 0)
-
-    def both(turn, carry):
-        @pl.when(turn == 1)
-        def _():
-            ocean_prepare()
-        return caps(turn, carry)
-    lax.fori_loop(0, 2, both, 0)
-
+        phase(None)
+
+    lax.fori_loop(0, 2, caps, 0)
+    ocean_prepare()
+
+    phase("arrive")
     @pl.when(is_owner)
     def _():
         for d in range(G):
@@ -665,6 +699,7 @@
                     sp = RH[j] if j < LT else pltpu.roll(RXH[0], 128 - (16 * i + 8), 1)
                     Z[j, rr, :] = Z[j, rr, :] + WID[j, rr, :] * sp
 
+    phase("krylov")
     def krylov0(r, acc):
         rr = pl.ds(r, 8)
         for j in range(NT):
@@ -705,6 +740,7 @@
         moments += list(ocean_rows(step, (zero, zero)))
     moments.append(ocean_rows(last, zero))
 
+    phase("red1")
     tile = zero
     for k, m in enumerate(moments):
         tile = jnp.where(sub == k, jnp.sum(m, axis=0, keepdims=True), tile)
@@ -716,6 +752,7 @@
     tile = L1[0]
     for k in range(1, 8):
         tile = tile + L1[k]
+    phase("red2")
     L2[mine2] = tile
     for dev in peers2:
         send(L2.at[mine2], L2.at[mine2], S_2, R_2, dev)
@@ -723,6 +760,7 @@
     tile = L2[0]
     for k in range(1, M2):
         tile = tile + L2[k]
+    phase("coef")
     total = jnp.sum(tile, axis=1, keepdims=True)
     mu = [total[k:k + 1, :] for k in range(6)]
     nu = [mu[k] - mu[k + 1] for k in range(5)]
@@ -742,6 +780,7 @@
     k1 = jnp.broadcast_to(a1 * p11 + a2 * p21, (8, 128))
     k2 = jnp.broadcast_to(a2 * p22, (8, 128))
 
+    phase("finish")
     def finish(r, carry):
         rr = pl.ds(r, 8)
         for j in range(LT):
@@ -751,25 +790,27 @@
     ocean_rows(finish, 0)
     for j in range(LT):
         local(OUT.at[j], o_ssh.at[:, cols(j)], L_OUTS)
+    phase("outwait")
     wait_rows(ls.at[L_OUTS], OR * LT)
     wait_rows(ls.at[L_OUT], 5 * 2 * IR * LT)
 
-    for s, cond in ((S_CL, jnp.logical_and(is_owner, has_l)), (S_CR, jnp.logical_and(is_owner, has_r))):
+    phase("sentwait")
+    for s, cond in ((S_FL, jnp.logical_and(is_owner, has_l)), (S_FR, jnp.logical_and(is_owner, has_r))):
         @pl.when(cond)
         def _(s=s):
-            wait_rows(ss.at[s], 2 * OR)
+            wait_rows(ss.at[s], G * 24)
     for s, cond in ((S_L, has_l), (S_R, has_r)):
         @pl.when(cond)
         def _(s=s):
-            wait_rows(ss.at[s], 8 * 2 * IR + 3 * OR)
+            wait_rows(ss.at[s], 2 * 8 * 8 + 3 * 4 * 8)
     for s, cond in ((S_U, has_u), (S_D, has_d)):
         @pl.when(cond)
         def _(s=s):
-            wait_rows(ss.at[s], (8 * 2 + 3) * 8 * NT)
+            wait_rows(ss.at[s], (8 * 2 + 3) * 8 * LT + 2 * 16 + 8)
 
     @pl.when(is_owner)
     def _():
-        wait_rows(ss.at[S_F], 2 * LT * (2 * (IR + 16) + IR + 8) + 3 * 40)
+        wait_rows(ss.at[S_F], 2 * LT * (2 * (IR + 16) + IR + 8))
     for c in range(2):
         mine = jnp.logical_and(is_owner, c == owner_cap)
 
@@ -794,6 +835,7 @@
             pltpu.make_async_remote_copy(
                 src_ref=land.at[rows], dst_ref=BO.at[1 - dy, 1 - dx, rows], send_sem=ss.at[S_BO + k],
                 recv_sem=rs.at[R_BO + k], device_id=dev, device_id_type=MESH).wait_send()
+    phase(None)
 
 
 def shards(T, *args):
@@ -802,12 +844,12 @@
     vm = lambda *s: pltpu.VMEM(s, F32)
     scratch = [
         vm(2, *ice), vm(3, *ice), vm(2, *ice), vm(*ice), vm(2, *ice), vm(*ice), vm(*ice), vm(*ice),
-        vm(2, 2, 2, 8, 128), vm(2, 3, 2, 8, 128), vm(2, 2, 2, 8, 128), vm(2, 2, 8, 128), vm(2, 3, 8, 128),
-        vm(2, 2, 2, IR, 128), vm(2, 3, 2, IR, 128), vm(2, 2, 2, IR, 128), vm(2, 2, IR, 128),
-        vm(2, 2, OR, 128), vm(3, 2, OR, 128),
+        vm(2, 2, 8, 8, 128), vm(2, 2, 8, 8, 128), vm(2, 3, 4, 8, 128), vm(2, 3, 4, 8, 128),
+        vm(2, G, 3, 8, 128), vm(2, 2, 3, 8, 128), vm(2, 2, 2, 8, 128), vm(2, 2, 2, 8, 128),
+        vm(2, 8, 128), vm(2, 8, 128), vm(2, 2, OR, 128),
         *[vm(*ocean) for _ in range(13)],
         pltpu.VMEM((3, 3, 2, 8, 64), jnp.int32), pltpu.VMEM((3, 3, 32, 64), jnp.int32),
-        vm(3, 5, 8, 128), vm(2, 5, 8, 128), vm(2, LT, IR, 128), vm(2, 2, 8, 128),
+        vm(2, LT, IR, 128), vm(2, 2, 8, 128),
         vm(G, LT, IR, 128), vm(G, 2, 8, 128), vm(LT, 8, 128), vm(2, 8, 128),
         vm(8, 8, 128), vm(T // 2, 8, 128), vm(LT, OR, 128), vm(DUMMY, 128),
         pltpu.SemaphoreType.DMA((N_R,)), pltpu.SemaphoreType.DMA((N_S,)), pltpu.SemaphoreType.DMA((N_L,)),

time: 72.3 us -> 63.9 us (0.88)
  Pallas kernels: 66.8 us -> 58.3 us
    pallas_call x1, Pallas kernels: 66.8 us -> 58.3 us  [shards(): pl.pallas_call(functools.partial(kernel, T), out_shape=(jax.ShapeDtypeStr...]
where the time goes in v2:
time: 63.9 us; the launch traced here: 63.7 us
  Pallas kernels  58.3 us (91%)
  local copies, waits for them, and re-layouts  4.69 us (7%)
  between operations  0.65 us (1%)
    pallas_call x1, Pallas kernels, shards(): pl.pallas_call(functools.partial(kernel, T), out_shape=(jax.ShapeDtypeStr...  58.3 us
    unnamed x5, local copies, waits for them, and re-layouts  4.69 us

profile of v2, /device:TPU:1, one launch (start us, length us, event | category | flops | bytes accessed | tf_op | source)
XLA Modules:
  0.0 63.7 jit_solution(4454296098458353467)
XLA Ops:
  0.6 58.3 %shard_map.121 = (f32[256,512]{1,0:T(8,128)}, f32[2,2,64,512]{3,2,1,0:T(8,128)}, f32[3,2,64,512]{3,2,1,0:T(8,128)}) custom-call(f32[256,512]{1,0:T(8,128)} %base.1, f32[256,512]{1,0:T(8,128)} %depth.1, f32[256,512]{1,0:T(8,128)} %ssh.1, f32[2,256,512]{2,1,0:T(8,128)} %cur.1, s32[32,64]{1,0:T(8,128)} %land.1, f32[2,64,512]{2,1,0:T(8,128)} %thick.1, ...), custom_call_target="tpu_custom_call" | custom-call | tf_op jit(solution)/shard_map/pallas_call | solution.py:858
  59.0 0.0 copy-start
  59.0 1.9 %copy.16 = f32[256,512]{1,0:T(8,128)} copy(f32[256,512]{1,0:T(8,128)} %get-tuple-element.6) | data formatting | bytes 1048576
  60.9 1.9 %copy.17 = f32[2,2,64,512]{3,2,1,0:T(8,128)} copy(f32[2,2,64,512]{3,2,1,0:T(8,128)} %get-tuple-element.7) | data formatting | bytes 1048576
  62.8 0.0 copy-done
  62.8 0.9 %copy.18 = f32[3,2,64,512]{3,2,1,0:T(8,128)} copy(f32[3,2,64,512]{3,2,1,0:T(8,128)S(1)} %copy-done) | data formatting | bytes 1572864
Async XLA Ops:
  59.0 3.8 %copy-start = (f32[3,2,64,512]{3,2,1,0:T(8,128)S(1)}, f32[3,2,64,512]{3,2,1,0:T(8,128)}, u32[]{:S(2)}) copy-start(f32[3,2,64,512]{3,2,1,0:T(8,128)} %get-tuple-element.8) | copy-start | bytes 2359300

commit v3 on v2

--- a/solution.py
+++ b/solution.py
@@ -19,21 +19,21 @@
 NT = LT + 1
 IR = 64
 OR = 256
-IH = IR + 32
-OH = OR + 32
+IH = IR + 40
+OH = OR + 40
 F32 = jnp.float32
 MESH = pl.DeviceIdType.MESH
 DUMMY = 4096
 
-R_PL, R_PR, R_IL, R_IR, R_OL, R_OR = 41, 43, 4, 5, 6, 7
+R_PL, R_PR, R_FU, R_FD, R_IL, R_IR, R_OL, R_OR = 41, 43, 45, 47, 4, 5, 6, 7
 R_IU, R_ID, R_F = 8, 10, 12
 R_OU, R_OD, R_RS, R_RH, R_1, R_2 = 14, 15, 16, 20, 21, 22
 R_BI, R_BO = 23, 32
-N_R = 45
+N_R = 49
 S_FL, S_FR, S_L, S_R, S_U, S_D, S_F, S_RS, S_1, S_2 = 0, 1, 2, 3, 4, 5, 6, 7, 9, 10
-S_RH = 11
+S_RH, S_FW = 11, 30
 S_BI, S_BO = 12, 21
-N_S = 30
+N_S = 31
 L_BLK, L_ICE, L_FL, L_OC, L_OUT, L_OUTS, L_ED = 0, 1, 2, 3, 4, 5, 6
 N_L = 7
 
@@ -64,11 +64,11 @@
 def kernel(
     T,
     base, depth, ssh, cur, land, thick, iblk, ivel, istr, wind,
-    o_ssh, o_vel, o_str,
-    V, S, W, TH, FL, CV, C1, C2,
-    PI, LI, PC, LC, PF, LF, PH, LH, PHO, LHO, CE,
+    V, S, OUT,
+    W, TH, FL, CV, C1, C2,
+    PI, LI, PC, LC, PF, LF, PH, LH, PHO, LHO, CE, FE,
     B, D, X, Z, Y0, Y1, Y2, H, WID, DG, WET, V1, V2,
-    BI, BO, SPB, XB, RSP, RX, RH, RXH, L1, L2, OUT, DUM,
+    BI, BO, SPB, XB, RSP, RX, RH, RXH, L1, L2, MOM, DUM,
     rs, ss, ls,
 ):
     g = lax.axis_index("grp")
@@ -107,24 +107,19 @@
                     cond = there if cond is None else jnp.logical_and(cond, there)
             nbrs.append((dy, dx, cond))
 
+    def top_summed(c, d):
+        return (c == 0 and d in (1, 2)) or (c == 1 and d == 1)
+
+    def bottom_summed(c, d):
+        return (c == 1 and d in (1, 2)) or (c == 0 and d == 2)
+
+    def top_is_summed(c):
+        return jnp.logical_or(g == 1, jnp.logical_and(g == 2, c == 0))
+
+    def bottom_is_summed(c):
+        return jnp.logical_or(g == 2, jnp.logical_and(g == 1, c == 1))
+
     phase = Phases()
-    phase("loads")
-    local(iblk, BI.at[1, 1], L_BLK)
-    local(land, BO.at[1, 1], L_BLK)
-    for j in range(LT):
-        local(ivel.at[:, :, :, cols(j)], V.at[:, :, j, pl.ds(16, IR), :], L_ICE)
-        local(istr.at[:, :, :, cols(j)], S.at[:, :, j, pl.ds(16, IR), :], L_ICE)
-        local(wind.at[:, :, :, cols(j)], W.at[:, :, j, pl.ds(16, IR), :], L_ICE)
-        local(thick.at[:, :, cols(j)], TH.at[:, j, pl.ds(16, IR), :], L_ICE)
-        local(base.at[:, cols(j)], B.at[j, pl.ds(16, OR), :], L_OC)
-        local(depth.at[:, cols(j)], D.at[j, pl.ds(16, OR), :], L_OC)
-        local(ssh.at[:, cols(j)], X.at[j, pl.ds(16, OR), :], L_OC)
-
-    @pl.when(is_owner)
-    def _():
-        local(cur.at[:, :, cols(0)], CE.at[0], L_ED)
-        local(cur.at[:, :, cols(LT - 1)], CE.at[1], L_ED)
-
     phase("signal")
     barrier = pltpu.get_barrier_semaphore()
     core = lax.rem(t, 2)
@@ -148,6 +143,88 @@
     for dev in peers2:
         pl.semaphore_signal(barrier, inc=1, device_id=dev, device_id_type=MESH)
 
+    phase("loads")
+    local(iblk, BI.at[1, 1], L_BLK)
+    local(land, BO.at[1, 1], L_BLK)
+    for j in range(LT):
+        local(ivel.at[:, :, :, cols(j)], V.at[:, :, j, pl.ds(16, IR), :], L_ICE)
+        local(istr.at[:, :, :, cols(j)], S.at[:, :, j, pl.ds(16, IR), :], L_ICE)
+        local(wind.at[:, :, :, cols(j)], W.at[:, :, j, pl.ds(16, IR), :], L_ICE)
+        local(thick.at[:, :, cols(j)], TH.at[:, j, pl.ds(16, IR), :], L_ICE)
+        local(base.at[:, cols(j)], B.at[j, pl.ds(16, OR), :], L_OC)
+        local(depth.at[:, cols(j)], D.at[j, pl.ds(16, OR), :], L_OC)
+        local(ssh.at[:, cols(j)], X.at[j, pl.ds(16, OR), :], L_OC)
+
+    @pl.when(is_owner)
+    def _():
+        local(cur.at[:, :, cols(0)], CE.at[0], L_ED)
+        local(cur.at[:, :, cols(LT - 1)], CE.at[1], L_ED)
+
+    phase("barrier")
+    wide = 1 + jnp.minimum(t, 1) + jnp.minimum(T - 1 - t, 1)
+    pl.semaphore_wait(barrier, G * wide - 1 + len(peers2))
+
+    phase("sends")
+    left, right, up, down = (g, t - 1), (g, t + 1), (g - 1, t), (g + 1, t)
+    for dy, dx, cond in nbrs:
+        k = 3 * (1 - dy) + (1 - dx)
+        @pl.when(cond)
+        def _(dy=dy, dx=dx, k=k):
+            dev = (g + dy, t + dx)
+            send(iblk, BI.at[1 - dy, 1 - dx], S_BI + k, R_BI + k, dev)
+            rows = pl.ds(0, OR // BS) if dy == 0 else pl.ds(0 if dy < 0 else OR // BS - 8, 8)
+            send(land.at[rows], BO.at[1 - dy, 1 - dx, rows], S_BO + k, R_BO + k, dev)
+
+    def flow_rows(c, d):
+        lo = IR * d if d == 0 or top_summed(c, d) else IR * d - 8
+        hi = IR * d + IR if d == G - 1 or bottom_summed(c, d) else IR * d + IR + 8
+        return lo, hi - lo, 16 + lo - IR * d
+
+    dests = {0: (1, 3, 2), G - 1: (2, 0, 1)}
+
+    def send_flow(c, d):
+        lo, n, at = flow_rows(c, d)
+        for j in range(LT):
+            send(cur.at[:, pl.ds(lo, n), cols(j)], FL.at[:, c, j, pl.ds(at, n), :],
+                 S_F, R_F + c, (d, t))
+
+    def halo_ice(dev, c, src, dst, s, r):
+        there = dev[0]
+        if s == S_D:
+            summed = jnp.logical_or(there == 1, jnp.logical_and(there == 2, c == 0))
+        else:
+            summed = jnp.logical_or(there == 2, jnp.logical_and(there == 1, c == 1))
+
+        @pl.when(jnp.logical_not(summed))
+        def _():
+            for j in range(LT):
+                send(wind.at[:, c, pl.ds(src, 8), cols(j)], W.at[:, c, j, pl.ds(dst, 8), :], s, r, dev)
+        for j in range(LT):
+            send(ivel.at[:, c, pl.ds(src, 8), cols(j)], V.at[:, c, j, pl.ds(dst, 8), :], s, r, dev)
+            send(istr.at[:, c, pl.ds(src, 8), cols(j)], S.at[:, c, j, pl.ds(dst, 8), :], s, r, dev)
+            send(thick.at[c, pl.ds(src, 8), cols(j)], TH.at[c, j, pl.ds(dst, 8), :], s, r, dev)
+
+    def halo_turn(turn):
+        for dev, cond, src, dst, s, r in (
+            (up, has_u, 0, IR + 16, S_U, R_ID),
+            (down, has_d, IR - 8, 8, S_D, R_IU),
+        ):
+            @pl.when(cond)
+            def _(dev=dev, src=src, dst=dst, s=s, r=r):
+                there = dev[0] // 2
+                c = there if turn == 0 else 1 - there
+                halo_ice(dev, c, src, dst, s, r + c)
+
+    for own, c in ((0, 0), (G - 1, 1)):
+        @pl.when(g == own)
+        def _(own=own, c=c):
+            send_flow(c, dests[own][0])
+            send_flow(c, dests[own][1])
+            lo, n, at = flow_rows(c, own)
+            for j in range(LT):
+                local(cur.at[:, pl.ds(lo, n), cols(j)], FL.at[:, c, j, pl.ds(at, n), :], L_FL)
+    halo_turn(0)
+
     phase("zeros")
     for cond, row, orow, by in ((g == 0, 8, 8, 0), (g == G - 1, IR + 16, OR + 16, 2)):
         @pl.when(cond)
@@ -170,6 +247,16 @@
                     BI[by, x, c] = jnp.zeros((8, 64), jnp.int32)
                 BO[by, x] = jnp.zeros((32, 64), jnp.int32)
 
+    for d in (1, 2):
+        @pl.when(g == d)
+        def _(d=d):
+            for c in range(2):
+                for here, row in ((top_summed(c, d), 8), (bottom_summed(c, d), IR + 16)):
+                    if here:
+                        for k in range(2):
+                            for j in range(LT):
+                                FL[k, c, j, pl.ds(row, 8), :] = zero
+
     for cond, side, bx in ((t == 0, 0, 0), (t == T - 1, 1, 2)):
         @pl.when(cond)
         def _(side=side, bx=bx):
@@ -249,56 +336,11 @@
                     pack = put(pack, e, i, ref[j, pl.ds(16 + 64 * v + 8 * i, 8), :])
                 PC[e, k, v] = pack
 
-    phase("barrier")
-    wide = 1 + jnp.minimum(t, 1) + jnp.minimum(T - 1 - t, 1)
-    pl.semaphore_wait(barrier, G * wide - 1 + len(peers2))
-
-    phase("sends")
-    left, right, up, down = (g, t - 1), (g, t + 1), (g - 1, t), (g + 1, t)
-    for dy, dx, cond in nbrs:
-        k = 3 * (1 - dy) + (1 - dx)
-        @pl.when(cond)
-        def _(dy=dy, dx=dx, k=k):
-            dev = (g + dy, t + dx)
-            send(iblk, BI.at[1 - dy, 1 - dx], S_BI + k, R_BI + k, dev)
-            rows = pl.ds(0, OR // BS) if dy == 0 else pl.ds(0 if dy < 0 else OR // BS - 8, 8)
-            send(land.at[rows], BO.at[1 - dy, 1 - dx, rows], S_BO + k, R_BO + k, dev)
-
     for e, dev, cond, s, ri, ro in ((0, left, has_l, S_L, R_IR, R_OR), (1, right, has_r, S_R, R_IL, R_OL)):
         @pl.when(cond)
         def _(e=e, dev=dev, s=s, ri=ri, ro=ro):
             send(PI.at[e], LI.at[1 - e], s, ri, dev)
             send(PC.at[e], LC.at[1 - e], s, ro, dev)
-
-    def flow_rows(d):
-        lo, hi = max(IR * d - 8, 0), min(IR * d + IR + 8, OR)
-        return lo, hi - lo, 16 + lo - IR * d
-
-    dests = {0: (1, 2, 3), G - 1: (2, 1, 0)}
-
-    def send_flow(c, d):
-        lo, n, at = flow_rows(d)
-        for j in range(LT):
-            send(cur.at[:, pl.ds(lo, n), cols(j)], FL.at[:, c, j, pl.ds(at, n), :],
-                 S_F, R_F + c, (d, t))
-
-    def halo_ice(dev, c, src, dst, s, r):
-        for j in range(LT):
-            send(ivel.at[:, c, pl.ds(src, 8), cols(j)], V.at[:, c, j, pl.ds(dst, 8), :], s, r, dev)
-            send(istr.at[:, c, pl.ds(src, 8), cols(j)], S.at[:, c, j, pl.ds(dst, 8), :], s, r, dev)
-            send(wind.at[:, c, pl.ds(src, 8), cols(j)], W.at[:, c, j, pl.ds(dst, 8), :], s, r, dev)
-            send(thick.at[c, pl.ds(src, 8), cols(j)], TH.at[c, j, pl.ds(dst, 8), :], s, r, dev)
-
-    def halo_turn(turn):
-        for dev, cond, src, dst, s, r in (
-            (up, has_u, 0, IR + 16, S_U, R_ID),
-            (down, has_d, IR - 8, 8, S_D, R_IU),
-        ):
-            @pl.when(cond)
-            def _(dev=dev, src=src, dst=dst, s=s, r=r):
-                there = dev[0] // 2
-                c = there if turn == 0 else 1 - there
-                halo_ice(dev, c, src, dst, s, r + c)
 
     for own, c in ((0, 0), (G - 1, 1)):
         @pl.when(g == own)
@@ -310,11 +352,6 @@
                         d = dg if own == 0 else G - 1 - dg
                         dev = (g + dg if own == 0 else g - dg, t + dx)
                         send(PF.at[e, d], LF.at[1 - e, c], s, r + c, dev)
-            send_flow(c, dests[own][0])
-            lo, n, at = flow_rows(own)
-            for j in range(LT):
-                local(cur.at[:, pl.ds(lo, n), cols(j)], FL.at[:, c, j, pl.ds(at, n), :], L_FL)
-    halo_turn(0)
 
     phase("mergeice")
     @pl.when(has_l)
@@ -345,11 +382,21 @@
             for c in range(2):
                 send(PH.at[e, c], LH.at[1 - e, c], s, r + c, dev)
 
+    for own, c, row, to, dev, r in (
+        (0, 0, IR + 8, 8, down, R_FU), (G - 1, 1, 16, IR + 16, up, R_FD + 1)):
+        @pl.when(g == own)
+        def _(c=c, row=row, to=to, dev=dev, r=r):
+            wait_rows(ls.at[L_FL], 2 * (IR + 8) * LT)
+            for k in range(2):
+                for j in range(LT):
+                    FE[k, j] = W[k, c, j, pl.ds(row, 8), :] + FL[k, c, j, pl.ds(row, 8), :] * DRAG
+            for j in range(LT):
+                send(FE.at[:, j], W.at[:, c, j, pl.ds(to, 8), :], S_FW, r, dev)
+
     for own, c in ((0, 0), (G - 1, 1)):
         @pl.when(g == own)
         def _(own=own, c=c):
-            for d in dests[own][1:]:
-                send_flow(c, d)
+            send_flow(c, dests[own][2])
     halo_turn(1)
     for dev, cond, at, to, s, r in (
         (up, has_u, 0, OR + 16, S_U, R_OD),
@@ -442,14 +489,28 @@
     paint(WET, OR + 16, spread_rows([BO[2, x, 0:8] for x in range(3)]), 0)
 
     phase("")
+    def pass_on(c, row, to, dev, r):
+        for j in range(LT):
+            send(W.at[:, c, j, pl.ds(row, 8), :], W.at[:, c, j, pl.ds(to, 8), :], S_FW, r + c, dev)
+
     def cap(c):
         phase = Phases()
         phase("capwait")
 
-        for e, cond, r, row in ((0, has_u, R_IU, 8), (1, has_d, R_ID, IR + 16)):
+        for e, cond, r, row, rf, summed in (
+            (0, has_u, R_IU, 8, R_FU, top_is_summed(c)),
+            (1, has_d, R_ID, IR + 16, R_FD, bottom_is_summed(c)),
+        ):
             @pl.when(cond)
-            def _(e=e, r=r, row=row):
-                wait_rows(rs.at[r + c], 8 * 8 * LT + 16)
+            def _(e=e, r=r, row=row, rf=rf, summed=summed):
+                @pl.when(summed)
+                def _():
+                    wait_rows(rs.at[rf + c], 2 * 8 * LT)
+                    wait_rows(rs.at[r + c], 6 * 8 * LT + 16)
+
+                @pl.when(jnp.logical_not(summed))
+                def _():
+                    wait_rows(rs.at[r + c], 8 * 8 * LT + 16)
                 for k in range(8):
                     x = pltpu.roll(LH[e, c, k // 4], (128 - 32 * (k % 4) - 16) % 128, 1)
                     ice_set(k, c, LT, row, x)
@@ -470,19 +531,17 @@
         mine = jnp.logical_and(is_owner, c == owner_cap)
         at_end = jnp.logical_or(jnp.logical_and(c == 0, g == G - 1), jnp.logical_and(c == 1, g == 0))
 
-        @pl.when(mine)
-        def _():
-            wait_rows(ls.at[L_FL], 2 * (IR + 8) * LT)
-
         @pl.when(jnp.logical_not(mine))
         def _():
-            @pl.when(at_end)
+            both = jnp.logical_and(top_is_summed(c), bottom_is_summed(c))
+
+            @pl.when(both)
+            def _():
+                wait_rows(rs.at[R_F + c], 2 * IR * LT)
+
+            @pl.when(jnp.logical_not(both))
             def _():
                 wait_rows(rs.at[R_F + c], 2 * (IR + 8) * LT)
-
-            @pl.when(jnp.logical_not(at_end))
-            def _():
-                wait_rows(rs.at[R_F + c], 2 * (IR + 16) * LT)
 
         phase("prepare")
         def prepare(i, carry):
@@ -498,6 +557,22 @@
                     W[k, c, j, r, :] = W[k, c, j, r, :] + FL[k, c, j, r, :] * DRAG
             return carry
         lax.fori_loop(0, IR // 8 + 2, prepare, 0)
+
+        @pl.when(jnp.logical_and(c == 0, g == 1))
+        def _():
+            pass_on(0, IR + 8, 8, down, R_FU)
+
+        @pl.when(jnp.logical_and(c == 0, g == G - 1))
+        def _():
+            pass_on(0, 16, IR + 16, up, R_FD)
+
+        @pl.when(jnp.logical_and(c == 1, g == 0))
+        def _():
+            pass_on(1, IR + 8, 8, down, R_FU)
+
+        @pl.when(jnp.logical_and(c == 1, g == 2))
+        def _():
+            pass_on(1, 16, IR + 16, up, R_FD)
 
         phase("subcycles")
         keep = 1.0 / (1.0 + RELAX)
@@ -534,16 +609,13 @@
                 V[1, c, j, rr, :] = c1 * v[j] + c2 * (f1 + W[1, c, j, rr, :])
 
         def subcycle(n, carry):
-            for i in range(IR // 8 + 2):
-                group(8 + 8 * i)
+            for _ in range(2):
+                for i in range(IR // 8 + 2):
+                    group(8 + 8 * i)
             return carry
-        lax.fori_loop(0, NSUB, subcycle, 0)
+        lax.fori_loop(0, NSUB // 2, subcycle, 0)
 
         phase("diverge")
-        for j in range(LT):
-            local(V.at[:, c, j, pl.ds(16, IR), :], o_vel.at[:, c, :, cols(j)], L_OUT)
-            local(S.at[:, c, j, pl.ds(16, IR), :], o_str.at[:, c, :, cols(j)], L_OUT)
-
         prev = [zero] * NT
         pack = zero
         for i in range(IR // 8):
@@ -595,7 +667,7 @@
         cap(jnp.where(turn == 0, first_cap, 1 - first_cap))
         return carry
 
-    def ocean_rows(body, carry, unroll=2):
+    def ocean_rows(body, carry, unroll=4):
         def step(i, cc):
             for m in range(unroll):
                 cc = body(pl.multiple_of(8 * (unroll * i + m) + 16, 8), cc)
@@ -655,31 +727,39 @@
     ocean_prepare()
 
     phase("arrive")
-    @pl.when(is_owner)
-    def _():
-        for d in range(G):
-            @pl.when(g != d)
-            def _(d=d):
-                wait_rows(rs.at[R_RS + d], LT * IR + 16)
-        for d in range(G):
-            for i in range(IR // 8):
-                rr = pl.ds(16 + IR * d + 8 * i, 8)
-                for j in range(NT):
-                    if j < LT:
-                        sp = RSP[d, j, pl.ds(8 * i, 8), :]
-                    else:
-                        sp = pltpu.roll(RX[d, 0], 128 - (16 * i + 8), 1)
-                    if i == 0 and d > 0:
-                        more = jnp.broadcast_to(RX[d - 1, 1][j:j + 1, :], (8, 128))
-                        sp = sp + jnp.where(sub == 0, more, 0.0)
-                    Z[j, rr, :] = Z[j, rr, :] + WID[j, rr, :] * sp
-
-    @pl.when(g == 0)
-    def _():
-        rr = pl.ds(OR + 16, 8)
+    late_block = {0: 2, G - 1: 1}
+
+    def add_block(d, more_from):
+        for i in range(IR // 8):
+            rr = pl.ds(16 + IR * d + 8 * i, 8)
+            for j in range(NT):
+                if j < LT:
+                    sp = RSP[d, j, pl.ds(8 * i, 8), :]
+                else:
+                    sp = pltpu.roll(RX[d, 0], 128 - (16 * i + 8), 1)
+                if i == 0 and more_from is not None:
+                    sp = sp + below_block(more_from, j)
+                Z[j, rr, :] = Z[j, rr, :] + WID[j, rr, :] * sp
+
+    def below_block(d, j):
+        return jnp.where(sub == 0, jnp.broadcast_to(RX[d, 1][j:j + 1, :], (8, 128)), 0.0)
+
+    def add_below(d):
+        rr = pl.ds(16 + IR * (d + 1), 8)
         for j in range(NT):
-            more = jnp.broadcast_to(RX[G - 1, 1][j:j + 1, :], (8, 128))
-            Z[j, rr, :] = Z[j, rr, :] + WID[j, rr, :] * jnp.where(sub == 0, more, 0.0)
+            Z[j, rr, :] = Z[j, rr, :] + WID[j, rr, :] * below_block(d, j)
+
+    for own, last_in in late_block.items():
+        @pl.when(g == own)
+        def _(own=own, last_in=last_in):
+            rest = [d for d in range(G) if d != last_in]
+            for d in rest:
+                if d != own:
+                    wait_rows(rs.at[R_RS + d], LT * IR + 16)
+            for d in rest:
+                add_block(d, d - 1 if d - 1 in rest else None)
+            if own == 0:
+                add_below(G - 1)
 
     @pl.when(jnp.logical_not(is_owner))
     def _():
@@ -706,40 +786,77 @@
             z = Z[j, rr, :]
             Y0[j, rr, :] = D[j, rr, :] * z
             if j < LT and acc is not None:
-                acc = acc + DG[j, rr, :] * z * z
+                acc = (acc[0] + DG[j, rr, :] * z * z,)
         return acc
 
     def krylov(src, dst, vec, r, acc):
         rr = pl.ds(r, 8)
         y, n = shifted_sum(src, r)
-        if acc is not None:
-            odd, even = acc
         for j in range(NT):
             v = H[j, rr, :] * n[j]
             out = D[j, rr, :] * v
             vec[j, rr, :] = v
             dst[j, rr, :] = out
             if j < LT and acc is not None:
-                odd = odd + y[j] * n[j]
-                even = even + out * n[j]
-        return None if acc is None else (odd, even)
-
-    def last(r, acc):
+                acc = (acc[0] + y[j] * n[j], acc[1] + out * n[j])
+        return acc
+
+    def krylov3(r, acc):
+        if acc is None:
+            return None
         y, n = shifted_sum(Y2, r)
         for j in range(LT):
-            acc = acc + y[j] * n[j]
+            acc = (acc[0] + y[j] * n[j],)
         return acc
 
-    krylov0(8, None)
-    krylov0(OR + 16, None)
-    moments = [ocean_rows(krylov0, zero)]
-    for src, dst, vec in ((Y0, Y1, V1), (Y1, Y2, V2)):
-        step = functools.partial(krylov, src, dst, vec)
-        step(8, None)
-        step(OR + 16, None)
-        moments += list(ocean_rows(step, (zero, zero)))
-    moments.append(ocean_rows(last, zero))
-
+    sweeps = (
+        (krylov0, (0,)),
+        (functools.partial(krylov, Y0, Y1, V1), (1, 2)),
+        (functools.partial(krylov, Y1, Y2, V2), (3, 4)),
+        (krylov3, (5,)),
+    )
+    start = jnp.where(g == 0, 13, jnp.where(g == G - 1, 5, 17))
+    end = jnp.where(g == 0, 29, jnp.where(g == G - 1, 21, 17))
+
+    def row_of(group):
+        return pl.multiple_of(8 * group + 8, 8)
+
+    for body, into in sweeps:
+        body(8, None)
+        body(OR + 16, None)
+        body(row_of(start), None)
+        body(row_of(end - 1), None)
+
+        def four(i, acc, first, body=body):
+            for m in range(4):
+                acc = body(row_of(first + 4 * i + m), acc)
+            return acc
+        acc = (zero,) * len(into)
+        acc = lax.fori_loop(0, (start - 1) // 4, functools.partial(four, first=1), acc)
+        acc = lax.fori_loop(0, (33 - end) // 4, functools.partial(four, first=end), acc)
+        for k, m in zip(into, acc):
+            MOM[k] = m
+
+    phase("late")
+    for own, last_in in late_block.items():
+        @pl.when(g == own)
+        def _(own=own, last_in=last_in):
+            wait_rows(rs.at[R_RS + last_in], LT * IR + 16)
+            add_block(last_in, last_in - 1)
+            add_below(last_in)
+
+    phase("krylate")
+
+    @pl.when(is_owner)
+    def _():
+        for body, into in sweeps:
+            acc = (zero,) * len(into)
+            for m in range(16):
+                acc = body(row_of(start + m), acc)
+            for k, m in zip(into, acc):
+                MOM[k] = MOM[k] + m
+
+    moments = [MOM[k] for k in range(6)]
     phase("red1")
     tile = zero
     for k, m in enumerate(moments):
@@ -788,12 +905,6 @@
                 k0 * Z[j, rr, :] + (k1 * V1[j, rr, :] + k2 * V2[j, rr, :]))
         return carry
     ocean_rows(finish, 0)
-    for j in range(LT):
-        local(OUT.at[j], o_ssh.at[:, cols(j)], L_OUTS)
-    phase("outwait")
-    wait_rows(ls.at[L_OUTS], OR * LT)
-    wait_rows(ls.at[L_OUT], 5 * 2 * IR * LT)
-
     phase("sentwait")
     for s, cond in ((S_FL, jnp.logical_and(is_owner, has_l)), (S_FR, jnp.logical_and(is_owner, has_r))):
         @pl.when(cond)
@@ -803,14 +914,20 @@
         @pl.when(cond)
         def _(s=s):
             wait_rows(ss.at[s], 2 * 8 * 8 + 3 * 4 * 8)
-    for s, cond in ((S_U, has_u), (S_D, has_d)):
-        @pl.when(cond)
-        def _(s=s):
-            wait_rows(ss.at[s], (8 * 2 + 3) * 8 * LT + 2 * 16 + 8)
-
-    @pl.when(is_owner)
-    def _():
-        wait_rows(ss.at[S_F], 2 * LT * (2 * (IR + 16) + IR + 8))
+    for at in range(G):
+        @pl.when(g == at)
+        def _(at=at):
+            full = (8 * 2 + 3) * 8 * LT + 2 * 16 + 8
+            if at > 0:
+                less = sum(bottom_summed(c, at - 1) for c in range(2))
+                wait_rows(ss.at[S_U], full - less * 2 * 8 * LT)
+            if at < G - 1:
+                less = sum(top_summed(c, at + 1) for c in range(2))
+                wait_rows(ss.at[S_D], full - less * 2 * 8 * LT)
+            if at in (0, G - 1):
+                c = 0 if at == 0 else 1
+                wait_rows(ss.at[S_F], 2 * LT * sum(flow_rows(c, d)[1] for d in dests[at]))
+            wait_rows(ss.at[S_FW], (2 if at in (0, G - 1) else 1) * 2 * 8 * LT)
     for c in range(2):
         mine = jnp.logical_and(is_owner, c == owner_cap)
 
@@ -843,31 +960,55 @@
     ocean = (NT, OH, 128)
     vm = lambda *s: pltpu.VMEM(s, F32)
     scratch = [
-        vm(2, *ice), vm(3, *ice), vm(2, *ice), vm(*ice), vm(2, *ice), vm(*ice), vm(*ice), vm(*ice),
+        vm(2, *ice), vm(*ice), vm(2, *ice), vm(*ice), vm(*ice), vm(*ice),
         vm(2, 2, 8, 8, 128), vm(2, 2, 8, 8, 128), vm(2, 3, 4, 8, 128), vm(2, 3, 4, 8, 128),
         vm(2, G, 3, 8, 128), vm(2, 2, 3, 8, 128), vm(2, 2, 2, 8, 128), vm(2, 2, 2, 8, 128),
-        vm(2, 8, 128), vm(2, 8, 128), vm(2, 2, OR, 128),
+        vm(2, 8, 128), vm(2, 8, 128), vm(2, 2, OR, 128), vm(2, LT, 8, 128),
         *[vm(*ocean) for _ in range(13)],
         pltpu.VMEM((3, 3, 2, 8, 64), jnp.int32), pltpu.VMEM((3, 3, 32, 64), jnp.int32),
         vm(2, LT, IR, 128), vm(2, 2, 8, 128),
         vm(G, LT, IR, 128), vm(G, 2, 8, 128), vm(LT, 8, 128), vm(2, 8, 128),
-        vm(8, 8, 128), vm(T // 2, 8, 128), vm(LT, OR, 128), vm(DUMMY, 128),
+        vm(8, 8, 128), vm(T // 2, 8, 128), vm(6, 8, 128), vm(DUMMY, 128),
         pltpu.SemaphoreType.DMA((N_R,)), pltpu.SemaphoreType.DMA((N_S,)), pltpu.SemaphoreType.DMA((N_L,)),
     ]
     hbm = pl.BlockSpec(memory_space=pltpu.HBM)
+    vmem = pl.BlockSpec(memory_space=pltpu.VMEM)
+    worked = pl.pallas_call(
+        functools.partial(kernel, T),
+        out_shape=(vm(2, *ice), vm(3, *ice), vm(LT, OR, 128)),
+        in_specs=[hbm] * 10,
+        out_specs=(vmem, vmem, vmem),
+        scratch_shapes=scratch,
+        compiler_params=pltpu.CompilerParams(
+            collective_id=0, has_side_effects=True, vmem_limit_bytes=60 * 1024 * 1024),
+    )(*args)
     return pl.pallas_call(
-        functools.partial(kernel, T),
+        deliver,
         out_shape=(
             jax.ShapeDtypeStruct((OR, 128 * LT), F32),
             jax.ShapeDtypeStruct((2, 2, IR, 128 * LT), F32),
             jax.ShapeDtypeStruct((3, 2, IR, 128 * LT), F32),
         ),
-        in_specs=[hbm] * 10,
+        in_specs=[vmem] * 3,
         out_specs=(hbm, hbm, hbm),
-        scratch_shapes=scratch,
-        compiler_params=pltpu.CompilerParams(
-            collective_id=0, has_side_effects=True, vmem_limit_bytes=60 * 1024 * 1024),
-    )(*args)
+        scratch_shapes=[pltpu.SemaphoreType.DMA((3, LT))],
+        compiler_params=pltpu.CompilerParams(vmem_limit_bytes=1024 * 1024),
+    )(*worked)
+
+
+def deliver(V, S, OUT, o_ssh, o_vel, o_str, sem):
+    copies = []
+    for j in range(LT):
+        to = pl.ds(128 * j, 128)
+        copies += [
+            pltpu.make_async_copy(S.at[:, :, j, pl.ds(16, IR), :], o_str.at[:, :, :, to], sem.at[0, j]),
+            pltpu.make_async_copy(V.at[:, :, j, pl.ds(16, IR), :], o_vel.at[:, :, :, to], sem.at[1, j]),
+            pltpu.make_async_copy(OUT.at[j], o_ssh.at[:, to], sem.at[2, j]),
+        ]
+    for c in copies:
+        c.start()
+    for c in copies:
+        c.wait()
 
 
 def solution(mesh):

time: 63.9 us -> 55.8 us (0.87)
  local copies, waits for them, and re-layouts: 4.69 us -> 0 us
  Pallas kernels: 58.3 us -> 55 us
    unnamed x5 -> x0, local copies, waits for them, and re-layouts: 4.69 us -> none
    pallas_call x1 -> x2, Pallas kernels: 58.3 us -> 55 us  [the longest x1 53.7 us: shards(): pl.pallas_call(functools.partial(kernel, T), out_shape=(vm(2, *ice), vm(3...]
where the time goes in v3:
time: 55.8 us; the launch traced here: 55.7 us
  Pallas kernels  55 us (99%)
  between operations  0.64 us (1%)
    pallas_call x1, Pallas kernels, shards(): pl.pallas_call(functools.partial(kernel, T), out_shape=(vm(2, *ice), vm(3...  53.7 us
    pallas_call x1, Pallas kernels, shards(): pl.pallas_call(deliver, out_shape=(jax.ShapeDtypeStruct((OR, 128 * LT), F...  1.32 us

profile of v3, /device:TPU:1, one launch (start us, length us, event | category | flops | bytes accessed | tf_op | source)
XLA Modules:
  0.0 55.7 jit_solution(14302215903314195256)
XLA Ops:
  0.6 53.7 %shard_map.121 = (f32[2,2,5,104,128]{4,3,2,1,0:T(8,128)S(1)}, f32[3,2,5,104,128]{4,3,2,1,0:T(8,128)S(1)}, f32[4,256,128]{2,1,0:T(8,128)S(1)}) custom-call(f32[256,512]{1,0:T(8,128)} %base.1, f32[256,512]{1,0:T(8,128)} %depth.1, f32[256,512]{1,0:T(8,128)} %ssh.1, f32[2,256,512]{2,1,0:T(8,128)} %cur.1, s32[32,64]{1,0:T(8,128)} %land.1, f32[2,64,512]{2,1,0:T(8,128)} %thick.1, ...), custom_call_target="tpu_custom_call" | custom-call | tf_op jit(solution)/shard_map/pallas_call | solution.py:976
  54.4 1.3 %shard_map.122 = (f32[256,512]{1,0:T(8,128)}, f32[2,2,64,512]{3,2,1,0:T(8,128)}, f32[3,2,64,512]{3,2,1,0:T(8,128)}) custom-call(f32[2,2,5,104,128]{4,3,2,1,0:T(8,128)S(1)} %get-tuple-element.6.V, f32[3,2,5,104,128]{4,3,2,1,0:T(8,128)S(1)} %get-tuple-element.7.S, f32[4,256,128]{2,1,0:T(8,128)S(1)} %get-tuple-element.8.OUT), custom_call_target="tpu_custom_call" | custom-call | tf_op jit(solution)/shard_map/pallas_call | solution.py:985

commit v4 on v3

--- a/solution.py
+++ b/solution.py
@@ -68,7 +68,7 @@
     W, TH, FL, CV, C1, C2,
     PI, LI, PC, LC, PF, LF, PH, LH, PHO, LHO, CE, FE,
     B, D, X, Z, Y0, Y1, Y2, H, WID, DG, WET, V1, V2,
-    BI, BO, SPB, XB, RSP, RX, RH, RXH, L1, L2, MOM, DUM,
+    BI, BO, PB, LB, SPB, XB, RSP, RX, RH, RXH, L1, L2, MOM, DUM,
     rs, ss, ls,
 ):
     g = lax.axis_index("grp")
@@ -144,8 +144,8 @@
         pl.semaphore_signal(barrier, inc=1, device_id=dev, device_id_type=MESH)
 
     phase("loads")
-    local(iblk, BI.at[1, 1], L_BLK)
-    local(land, BO.at[1, 1], L_BLK)
+    local(iblk, BI.at[1], L_BLK)
+    local(land, BO.at[1], L_BLK)
     for j in range(LT):
         local(ivel.at[:, :, :, cols(j)], V.at[:, :, j, pl.ds(16, IR), :], L_ICE)
         local(istr.at[:, :, :, cols(j)], S.at[:, :, j, pl.ds(16, IR), :], L_ICE)
@@ -160,6 +160,14 @@
         local(cur.at[:, :, cols(0)], CE.at[0], L_ED)
         local(cur.at[:, :, cols(LT - 1)], CE.at[1], L_ED)
 
+    pltpu.make_async_copy(iblk, BI.at[1], ls.at[L_BLK]).wait()
+    pltpu.make_async_copy(land, BO.at[1], ls.at[L_BLK]).wait()
+    line = lax.broadcasted_iota(jnp.int32, (8, 64), 0)
+    for e, i, o in ((0, 0, 0), (1, 7, 7)):
+        ends = [BI[1, 0][i:i + 1], BI[1, 1][i:i + 1], BO[1, 24 * e:24 * e + 8][o:o + 1]]
+        ends = [jnp.broadcast_to(x, (8, 64)) for x in ends]
+        PB[e] = jnp.where(line == 0, ends[0], jnp.where(line == 1, ends[1], ends[2]))
+
     phase("barrier")
     wide = 1 + jnp.minimum(t, 1) + jnp.minimum(T - 1 - t, 1)
     pl.semaphore_wait(barrier, G * wide - 1 + len(peers2))
@@ -171,9 +179,12 @@
         @pl.when(cond)
         def _(dy=dy, dx=dx, k=k):
             dev = (g + dy, t + dx)
-            send(iblk, BI.at[1 - dy, 1 - dx], S_BI + k, R_BI + k, dev)
-            rows = pl.ds(0, OR // BS) if dy == 0 else pl.ds(0 if dy < 0 else OR // BS - 8, 8)
-            send(land.at[rows], BO.at[1 - dy, 1 - dx, rows], S_BO + k, R_BO + k, dev)
+            if dy == 0:
+                send(iblk, BI.at[1 - dx], S_BI + k, R_BI + k, dev)
+                send(land, BO.at[1 - dx], S_BO + k, R_BO + k, dev)
+            else:
+                e = 0 if dy < 0 else 1
+                send(PB.at[e], LB.at[1 - e, 1 - dx], S_BI + k, R_BI + k, dev)
 
     def flow_rows(c, d):
         lo = IR * d if d == 0 or top_summed(c, d) else IR * d - 8
@@ -226,7 +237,7 @@
     halo_turn(0)
 
     phase("zeros")
-    for cond, row, orow, by in ((g == 0, 8, 8, 0), (g == G - 1, IR + 16, OR + 16, 2)):
+    for cond, row, orow, by in ((g == 0, 8, 8, 0), (g == G - 1, IR + 16, OR + 16, 1)):
         @pl.when(cond)
         def _(row=row, orow=orow, by=by):
             for c in range(2):
@@ -243,9 +254,7 @@
                 D[j, pl.ds(orow, 8), :] = zero
                 X[j, pl.ds(orow, 8), :] = zero
             for x in range(3):
-                for c in range(2):
-                    BI[by, x, c] = jnp.zeros((8, 64), jnp.int32)
-                BO[by, x] = jnp.zeros((32, 64), jnp.int32)
+                LB[by, x] = jnp.zeros((8, 64), jnp.int32)
 
     for d in (1, 2):
         @pl.when(g == d)
@@ -268,10 +277,10 @@
             for k in range(3):
                 for v in range(4):
                     LC[side, k, v] = zero
-            for y in range(3):
-                for c in range(2):
-                    BI[y, bx, c] = jnp.zeros((8, 64), jnp.int32)
-                BO[y, bx] = jnp.zeros((32, 64), jnp.int32)
+            for y in range(2):
+                LB[y, bx] = jnp.zeros((8, 64), jnp.int32)
+                BI[bx, y] = jnp.zeros((8, 64), jnp.int32)
+            BO[bx] = jnp.zeros((32, 64), jnp.int32)
 
     phase("pack")
     slot_of = lane // 16
@@ -398,16 +407,17 @@
         def _(own=own, c=c):
             send_flow(c, dests[own][2])
     halo_turn(1)
-    for dev, cond, at, to, s, r in (
-        (up, has_u, 0, OR + 16, S_U, R_OD),
-        (down, has_d, OR - 8, 8, S_D, R_OU),
-    ):
-        @pl.when(cond)
-        def _(dev=dev, at=at, to=to, s=s, r=r):
-            for j in range(LT):
-                send(base.at[pl.ds(at, 8), cols(j)], B.at[j, pl.ds(to, 8), :], s, r, dev)
-                send(depth.at[pl.ds(at, 8), cols(j)], D.at[j, pl.ds(to, 8), :], s, r, dev)
-                send(ssh.at[pl.ds(at, 8), cols(j)], X.at[j, pl.ds(to, 8), :], s, r, dev)
+    def ocean_ends():
+        for dev, cond, at, to, s, r in (
+            (up, has_u, 0, OR + 16, S_U, R_OD),
+            (down, has_d, OR - 8, 8, S_D, R_OU),
+        ):
+            @pl.when(cond)
+            def _(dev=dev, at=at, to=to, s=s, r=r):
+                for j in range(LT):
+                    send(base.at[pl.ds(at, 8), cols(j)], B.at[j, pl.ds(to, 8), :], s, r, dev)
+                    send(depth.at[pl.ds(at, 8), cols(j)], D.at[j, pl.ds(to, 8), :], s, r, dev)
+                    send(ssh.at[pl.ds(at, 8), cols(j)], X.at[j, pl.ds(to, 8), :], s, r, dev)
 
     phase("mergeoc")
     @pl.when(has_l)
@@ -434,20 +444,21 @@
             send(PHO.at[e], LHO.at[1 - e], s, r, dev)
 
     phase("masks")
-    pltpu.make_async_copy(iblk, BI.at[1, 1], ls.at[L_BLK]).wait()
-    pltpu.make_async_copy(land, BO.at[1, 1], ls.at[L_BLK]).wait()
+    def block_pairs(dy, x, e):
+        if dy == 0:
+            return [(iblk, BI.at[x], S_BI, R_BI), (land, BO.at[x], S_BO, R_BO)]
+        return [(PB.at[e], LB.at[1 - e, x], S_BI, R_BI)]
+
     for dy, dx, cond in nbrs:
         k = 3 * (1 + dy) + (1 + dx)
         @pl.when(cond)
         def _(dy=dy, dx=dx, k=k):
             dev = (g + dy, t + dx)
-            pltpu.make_async_remote_copy(
-                src_ref=iblk, dst_ref=BI.at[1 + dy, 1 + dx], send_sem=ss.at[S_BI + k],
-                recv_sem=rs.at[R_BI + k], device_id=dev, device_id_type=MESH).wait_recv()
-            rows = pl.ds(0, OR // BS) if dy == 0 else pl.ds(OR // BS - 8 if dy < 0 else 0, 8)
-            pltpu.make_async_remote_copy(
-                src_ref=land.at[rows], dst_ref=BO.at[1 + dy, 1 + dx, rows], send_sem=ss.at[S_BO + k],
-                recv_sem=rs.at[R_BO + k], device_id=dev, device_id_type=MESH).wait_recv()
+            pairs = block_pairs(dy, 1 + dx, 1 if dy < 0 else 0)
+            for src, dst, s, r in pairs:
+                pltpu.make_async_remote_copy(
+                    src_ref=src, dst_ref=dst, send_sem=ss.at[s + k], recv_sem=rs.at[r + k],
+                    device_id=dev, device_id_type=MESH).wait_recv()
 
     def selection(width, first, start):
         block = lax.broadcasted_iota(jnp.int32, (64, width), 0)
@@ -474,26 +485,26 @@
             ref[j, pl.ds(row, 8), :] = jnp.broadcast_to(wide[b:b + 1, 128 * j:128 * j + 128], (8, 128))
         ref[LT, pl.ds(row, 8), :] = jnp.broadcast_to(last[b:b + 1, :], (8, 128))
 
+    ends = [spread_rows([LB[y, x] for x in range(3)]) for y in range(2)]
     for c in range(2):
         cov = CV.at[c]
-        paint(cov, 8, spread_rows([BI[0, x, c] for x in range(3)]), 7)
-        mid = spread_rows([BI[1, x, c] for x in range(3)])
+        paint(cov, 8, ends[0], c)
+        mid = spread_rows([BI[x, c] for x in range(3)])
         for b in range(8):
             paint(cov, 16 + 8 * b, mid, b)
-        paint(cov, IR + 16, spread_rows([BI[2, x, c] for x in range(3)]), 0)
-    paint(WET, 8, spread_rows([BO[0, x, 24:32] for x in range(3)]), 7)
+        paint(cov, IR + 16, ends[1], c)
+    paint(WET, 8, ends[0], 2)
     for q in range(4):
-        mid = spread_rows([BO[1, x, 8 * q:8 * q + 8] for x in range(3)])
+        mid = spread_rows([BO[x, 8 * q:8 * q + 8] for x in range(3)])
         for b in range(8):
             paint(WET, 16 + 64 * q + 8 * b, mid, b)
-    paint(WET, OR + 16, spread_rows([BO[2, x, 0:8] for x in range(3)]), 0)
-
-    phase("")
+    paint(WET, OR + 16, ends[1], 2)
+
     def pass_on(c, row, to, dev, r):
         for j in range(LT):
             send(W.at[:, c, j, pl.ds(row, 8), :], W.at[:, c, j, pl.ds(to, 8), :], S_FW, r + c, dev)
 
-    def cap(c):
+    def cap(c, turn):
         phase = Phases()
         phase("capwait")
 
@@ -575,6 +586,10 @@
             pass_on(1, 16, IR + 16, up, R_FD)
 
         phase("subcycles")
+        @pl.when(turn == 1)
+        def _():
+            ocean_ends()
+
         keep = 1.0 / (1.0 + RELAX)
 
         def group(r):
@@ -597,23 +612,29 @@
                 S[0, c, j, rr, :] = s0[j]
                 S[1, c, j, rr, :] = s1[j]
                 S[2, c, j, rr, :] = s2[j]
+
+        def push(r):
+            rr, above = pl.ds(r, 8), pl.ds(r - 1, 8)
+            s0 = [S[0, c, j, rr, :] for j in range(NT)]
+            s1 = [S[1, c, j, rr, :] for j in range(NT)]
+            s2 = [S[2, c, j, rr, :] for j in range(NT)]
             dif = [s0[j] - s1[j] for j in range(NT)]
             dw, sw = west(dif, lane), west(s2, lane)
-            above = pl.ds(r - 1, 8)
             for j in range(NT):
                 tot_up = S[0, c, j, above, :] + S[1, c, j, above, :]
                 f0 = 0.5 * ((s0[j] + s1[j]) - tot_up) + (s2[j] - sw[j])
                 f1 = 0.5 * (dif[j] - dw[j]) + (s2[j] - S[2, c, j, above, :])
                 c1, c2 = C1[c, j, rr, :], C2[c, j, rr, :]
-                V[0, c, j, rr, :] = c1 * u[j] + c2 * (f0 + W[0, c, j, rr, :])
-                V[1, c, j, rr, :] = c1 * v[j] + c2 * (f1 + W[1, c, j, rr, :])
+                V[0, c, j, rr, :] = c1 * V[0, c, j, rr, :] + c2 * (f0 + W[0, c, j, rr, :])
+                V[1, c, j, rr, :] = c1 * V[1, c, j, rr, :] + c2 * (f1 + W[1, c, j, rr, :])
 
         def subcycle(n, carry):
-            for _ in range(2):
-                for i in range(IR // 8 + 2):
-                    group(8 + 8 * i)
+            for i in range(IR // 8 + 2):
+                group(8 + 8 * i)
+            for i in range(IR // 8 + 2):
+                push(8 + 8 * i)
             return carry
-        lax.fori_loop(0, NSUB // 2, subcycle, 0)
+        lax.fori_loop(0, NSUB, subcycle, 0)
 
         phase("diverge")
         prev = [zero] * NT
@@ -664,7 +685,7 @@
         phase(None)
 
     def caps(turn, carry):
-        cap(jnp.where(turn == 0, first_cap, 1 - first_cap))
+        cap(jnp.where(turn == 0, first_cap, 1 - first_cap), turn)
         return carry
 
     def ocean_rows(body, carry, unroll=4):
@@ -945,13 +966,10 @@
         @pl.when(cond)
         def _(dy=dy, dx=dx, k=k):
             dev = (g + dy, t + dx)
-            pltpu.make_async_remote_copy(
-                src_ref=iblk, dst_ref=BI.at[1 - dy, 1 - dx], send_sem=ss.at[S_BI + k],
-                recv_sem=rs.at[R_BI + k], device_id=dev, device_id_type=MESH).wait_send()
-            rows = pl.ds(0, OR // BS) if dy == 0 else pl.ds(0 if dy < 0 else OR // BS - 8, 8)
-            pltpu.make_async_remote_copy(
-                src_ref=land.at[rows], dst_ref=BO.at[1 - dy, 1 - dx, rows], send_sem=ss.at[S_BO + k],
-                recv_sem=rs.at[R_BO + k], device_id=dev, device_id_type=MESH).wait_send()
+            for src, dst, s, r in block_pairs(dy, 1 - dx, 0 if dy < 0 else 1):
+                pltpu.make_async_remote_copy(
+                    src_ref=src, dst_ref=dst, send_sem=ss.at[s + k], recv_sem=rs.at[r + k],
+                    device_id=dev, device_id_type=MESH).wait_send()
     phase(None)
 
 
@@ -965,7 +983,8 @@
         vm(2, G, 3, 8, 128), vm(2, 2, 3, 8, 128), vm(2, 2, 2, 8, 128), vm(2, 2, 2, 8, 128),
         vm(2, 8, 128), vm(2, 8, 128), vm(2, 2, OR, 128), vm(2, LT, 8, 128),
         *[vm(*ocean) for _ in range(13)],
-        pltpu.VMEM((3, 3, 2, 8, 64), jnp.int32), pltpu.VMEM((3, 3, 32, 64), jnp.int32),
+        pltpu.VMEM((3, 2, 8, 64), jnp.int32), pltpu.VMEM((3, 32, 64), jnp.int32),
+        pltpu.VMEM((2, 8, 64), jnp.int32), pltpu.VMEM((2, 3, 8, 64), jnp.int32),
         vm(2, LT, IR, 128), vm(2, 2, 8, 128),
         vm(G, LT, IR, 128), vm(G, 2, 8, 128), vm(LT, 8, 128), vm(2, 8, 128),
         vm(8, 8, 128), vm(T // 2, 8, 128), vm(6, 8, 128), vm(DUMMY, 128),

time: 55.8 us -> 51.9 us (0.930)
  Pallas kernels: 55 us -> 51.2 us
    pallas_call x1, Pallas kernels: 53.7 us -> 49.8 us  [shards(): pl.pallas_call(functools.partial(kernel, T), out_shape=(vm(2, *ice), vm(3...]
where the time goes in v4:
time: 51.9 us; the launch traced here: 51.8 us
  Pallas kernels  51.2 us (99%)
  between operations  0.64 us (1%)
    pallas_call x1, Pallas kernels, shards(): pl.pallas_call(functools.partial(kernel, T), out_shape=(vm(2, *ice), vm(3...  49.8 us
    pallas_call x1, Pallas kernels, shards(): pl.pallas_call(deliver, out_shape=(jax.ShapeDtypeStruct((OR, 128 * LT), F...  1.32 us

profile of v4, /device:TPU:1, one launch (start us, length us, event | category | flops | bytes accessed | tf_op | source)
XLA Modules:
  0.0 51.8 jit_solution(2258610278333444507)
XLA Ops:
  0.6 49.8 %shard_map.121 = (f32[2,2,5,104,128]{4,3,2,1,0:T(8,128)S(1)}, f32[3,2,5,104,128]{4,3,2,1,0:T(8,128)S(1)}, f32[4,256,128]{2,1,0:T(8,128)S(1)}) custom-call(f32[256,512]{1,0:T(8,128)} %base.1, f32[256,512]{1,0:T(8,128)} %depth.1, f32[256,512]{1,0:T(8,128)} %ssh.1, f32[2,256,512]{2,1,0:T(8,128)} %cur.1, s32[32,64]{1,0:T(8,128)} %land.1, f32[2,64,512]{2,1,0:T(8,128)} %thick.1, ...), custom_call_target="tpu_custom_call" | custom-call | tf_op jit(solution)/shard_map/pallas_call | solution.py:995
  50.5 1.3 %shard_map.122 = (f32[256,512]{1,0:T(8,128)}, f32[2,2,64,512]{3,2,1,0:T(8,128)}, f32[3,2,64,512]{3,2,1,0:T(8,128)}) custom-call(f32[2,2,5,104,128]{4,3,2,1,0:T(8,128)S(1)} %get-tuple-element.6.V, f32[3,2,5,104,128]{4,3,2,1,0:T(8,128)S(1)} %get-tuple-element.7.S, f32[4,256,128]{2,1,0:T(8,128)S(1)} %get-tuple-element.8.OUT), custom_call_target="tpu_custom_call" | custom-call | tf_op jit(solution)/shard_map/pallas_call | solution.py:1004

commit v5 on v4

--- a/solution.py
+++ b/solution.py
@@ -272,7 +272,7 @@
             for c in range(2):
                 for k in range(8):
                     LI[side, c, k] = zero
-                for v in range(3):
+                for v in range(2):
                     LF[side, c, v] = zero
             for k in range(3):
                 for v in range(4):
@@ -292,6 +292,16 @@
     def take(from_right, from_left, at):
         both = jnp.where(slot_of == at, from_right, from_left)
         return pltpu.roll(both, 128 - 16 * at, 1) if at else both
+
+    thin_of, thin_before = lane // 12, lax.rem(lane + 12, 128) // 12
+
+    def put_thin(pack, e, at, x):
+        moved = pltpu.roll(x, 12 * at, 1) if at else x
+        return jnp.where((thin_before if e else thin_of) == at, moved, pack)
+
+    def take_thin(from_right, from_left, at):
+        both = jnp.where(thin_of == at, from_right, from_left)
+        return pltpu.roll(both, 128 - 12 * at, 1) if at else both
 
     wait_rows(ls.at[L_ICE], 8 * 2 * IR * LT)
 
@@ -326,15 +336,13 @@
             wait_rows(ls.at[L_ED], 2 * 2 * OR)
             for e in range(2):
                 for d in range(G):
-                    packs = [zero] * 3
                     for k in range(2):
+                        pack = zero
                         for s in range(10):
                             q = 8 * d - 1 + s
                             if 0 <= q < OR // 8:
-                                m = 10 * k + s
-                                packs[m // 8] = put(packs[m // 8], e, m % 8, CE[e, k, pl.ds(8 * q, 8), :])
-                    for v in range(3):
-                        PF[e, d, v] = packs[v]
+                                pack = put_thin(pack, e, s, CE[e, k, pl.ds(8 * q, 8), :])
+                        PF[e, d, k] = pack
 
     wait_rows(ls.at[L_OC], 3 * OR * LT)
     for e, j in ((0, 0), (1, LT - 1)):
@@ -500,6 +508,22 @@
             paint(WET, 16 + 64 * q + 8 * b, mid, b)
     paint(WET, OR + 16, ends[1], 2)
 
+    def static(c, r):
+        rr = pl.ds(r, 8)
+        for j in range(NT):
+            cov = CV[c, j, rr, :]
+            thc = TH[c, j, rr, :] * cov
+            scale = cov / (thc + (1.0 + STEP * DRAG))
+            C1[c, j, rr, :] = scale * (thc + 1.0)
+            C2[c, j, rr, :] = scale * STEP
+            TH[c, j, rr, :] = thc * (RELAX * STRENGTH / (1.0 + RELAX))
+
+    for c in range(2):
+        def own_static(i, carry, c=c):
+            static(c, pl.multiple_of(8 * i + 16, 8))
+            return carry
+        lax.fori_loop(0, IR // 8, own_static, 0)
+
     def pass_on(c, row, to, dev, r):
         for j in range(LT):
             send(W.at[:, c, j, pl.ds(row, 8), :], W.at[:, c, j, pl.ds(to, 8), :], S_FW, r + c, dev)
@@ -528,16 +552,15 @@
 
         @pl.when(has_l)
         def _():
-            wait_rows(rs.at[R_PL + c], 24)
+            wait_rows(rs.at[R_PL + c], 16)
 
         @pl.when(has_r)
         def _():
-            wait_rows(rs.at[R_PR + c], 24)
+            wait_rows(rs.at[R_PR + c], 16)
 
         for k in range(2):
             for s in range(10):
-                m = 10 * k + s
-                FL[k, c, LT, pl.ds(8 + 8 * s, 8), :] = take(LF[1, c, m // 8], LF[0, c, m // 8], m % 8)
+                FL[k, c, LT, pl.ds(8 + 8 * s, 8), :] = take_thin(LF[1, c, k], LF[0, c, k], s)
 
         mine = jnp.logical_and(is_owner, c == owner_cap)
         at_end = jnp.logical_or(jnp.logical_and(c == 0, g == G - 1), jnp.logical_and(c == 1, g == 0))
@@ -555,15 +578,12 @@
                 wait_rows(rs.at[R_F + c], 2 * (IR + 8) * LT)
 
         phase("prepare")
+        static(c, 8)
+        static(c, IR + 16)
+
         def prepare(i, carry):
             r = pl.ds(pl.multiple_of(8 * i + 8, 8), 8)
             for j in range(NT):
-                cov = CV[c, j, r, :]
-                thc = TH[c, j, r, :] * cov
-                scale = cov / (thc + (1.0 + STEP * DRAG))
-                C1[c, j, r, :] = scale * (thc + 1.0)
-                C2[c, j, r, :] = scale * STEP
-                TH[c, j, r, :] = thc * (RELAX * STRENGTH / (1.0 + RELAX))
                 for k in range(2):
                     W[k, c, j, r, :] = W[k, c, j, r, :] + FL[k, c, j, r, :] * DRAG
             return carry
@@ -848,15 +868,25 @@
         body(row_of(start), None)
         body(row_of(end - 1), None)
 
-        def four(i, acc, first, body=body):
-            for m in range(4):
-                acc = body(row_of(first + 4 * i + m), acc)
+        def some(i, acc, first, count, body=body):
+            for m in range(count):
+                acc = body(row_of(first + count * i + m), acc)
             return acc
-        acc = (zero,) * len(into)
-        acc = lax.fori_loop(0, (start - 1) // 4, functools.partial(four, first=1), acc)
-        acc = lax.fori_loop(0, (33 - end) // 4, functools.partial(four, first=end), acc)
-        for k, m in zip(into, acc):
-            MOM[k] = m
+
+        @pl.when(is_owner)
+        def _(some=some, into=into):
+            acc = (zero,) * len(into)
+            acc = lax.fori_loop(0, (start - 1) // 4, functools.partial(some, first=1, count=4), acc)
+            acc = lax.fori_loop(0, (33 - end) // 4, functools.partial(some, first=end, count=4), acc)
+            for k, m in zip(into, acc):
+                MOM[k] = m
+
+        @pl.when(jnp.logical_not(is_owner))
+        def _(some=some, into=into):
+            acc = lax.fori_loop(
+                0, 2, functools.partial(some, first=1, count=16), (zero,) * len(into))
+            for k, m in zip(into, acc):
+                MOM[k] = m
 
     phase("late")
     for own, last_in in late_block.items():
@@ -930,7 +960,7 @@
     for s, cond in ((S_FL, jnp.logical_and(is_owner, has_l)), (S_FR, jnp.logical_and(is_owner, has_r))):
         @pl.when(cond)
         def _(s=s):
-            wait_rows(ss.at[s], G * 24)
+            wait_rows(ss.at[s], G * 16)
     for s, cond in ((S_L, has_l), (S_R, has_r)):
         @pl.when(cond)
         def _(s=s):
@@ -980,7 +1010,7 @@
     scratch = [
         vm(2, *ice), vm(*ice), vm(2, *ice), vm(*ice), vm(*ice), vm(*ice),
         vm(2, 2, 8, 8, 128), vm(2, 2, 8, 8, 128), vm(2, 3, 4, 8, 128), vm(2, 3, 4, 8, 128),
-        vm(2, G, 3, 8, 128), vm(2, 2, 3, 8, 128), vm(2, 2, 2, 8, 128), vm(2, 2, 2, 8, 128),
+        vm(2, G, 2, 8, 128), vm(2, 2, 2, 8, 128), vm(2, 2, 2, 8, 128), vm(2, 2, 2, 8, 128),
         vm(2, 8, 128), vm(2, 8, 128), vm(2, 2, OR, 128), vm(2, LT, 8, 128),
         *[vm(*ocean) for _ in range(13)],
         pltpu.VMEM((3, 2, 8, 64), jnp.int32), pltpu.VMEM((3, 32, 64), jnp.int32),

time: 51.9 us -> 51.6 us (level)
  no operation moved by 1% of the time
where the time goes in v5:
time: 51.6 us; the launch traced here: 51.5 us
  Pallas kernels  50.9 us (99%)
  between operations  0.64 us (1%)
    pallas_call x1, Pallas kernels, shards(): pl.pallas_call(functools.partial(kernel, T), out_shape=(vm(2, *ice), vm(3...  49.5 us
    pallas_call x1, Pallas kernels, shards(): pl.pallas_call(deliver, out_shape=(jax.ShapeDtypeStruct((OR, 128 * LT), F...  1.32 us

profile of v5, /device:TPU:1, one launch (start us, length us, event | category | flops | bytes accessed | tf_op | source)
XLA Modules:
  0.0 51.5 jit_solution(12955264011613962138)
XLA Ops:
  0.6 49.5 %shard_map.121 = (f32[2,2,5,104,128]{4,3,2,1,0:T(8,128)S(1)}, f32[3,2,5,104,128]{4,3,2,1,0:T(8,128)S(1)}, f32[4,256,128]{2,1,0:T(8,128)S(1)}) custom-call(f32[256,512]{1,0:T(8,128)} %base.1, f32[256,512]{1,0:T(8,128)} %depth.1, f32[256,512]{1,0:T(8,128)} %ssh.1, f32[2,256,512]{2,1,0:T(8,128)} %cur.1, s32[32,64]{1,0:T(8,128)} %land.1, f32[2,64,512]{2,1,0:T(8,128)} %thick.1, ...), custom_call_target="tpu_custom_call" | custom-call | tf_op jit(solution)/shard_map/pallas_call | solution.py:1025
  50.2 1.3 %shard_map.122 = (f32[256,512]{1,0:T(8,128)}, f32[2,2,64,512]{3,2,1,0:T(8,128)}, f32[3,2,64,512]{3,2,1,0:T(8,128)}) custom-call(f32[2,2,5,104,128]{4,3,2,1,0:T(8,128)S(1)} %get-tuple-element.6.V, f32[3,2,5,104,128]{4,3,2,1,0:T(8,128)S(1)} %get-tuple-element.7.S, f32[4,256,128]{2,1,0:T(8,128)S(1)} %get-tuple-element.8.OUT), custom_call_target="tpu_custom_call" | custom-call | tf_op jit(solution)/shard_map/pallas_call | solution.py:1034

commit v6 on v5

--- a/solution.py
+++ b/solution.py
@@ -69,7 +69,7 @@
     PI, LI, PC, LC, PF, LF, PH, LH, PHO, LHO, CE, FE,
     B, D, X, Z, Y0, Y1, Y2, H, WID, DG, WET, V1, V2,
     BI, BO, PB, LB, SPB, XB, RSP, RX, RH, RXH, L1, L2, MOM, DUM,
-    rs, ss, ls,
+    rs, ss, ls, far,
 ):
     g = lax.axis_index("grp")
     t = lax.axis_index("tile")
@@ -140,8 +140,18 @@
                     pl.semaphore_signal(barrier, inc=1, device_id=dev, device_id_type=MESH)
             elif dg:
                 pl.semaphore_signal(barrier, inc=1, device_id=dev, device_id_type=MESH)
-    for dev in peers2:
-        pl.semaphore_signal(barrier, inc=1, device_id=dev, device_id_type=MESH)
+
+    def tell(n):
+        for dt in (-(2 << n), 2 << n):
+            @pl.when(jnp.logical_and(t + dt >= 0, t + dt < T))
+            def _(dt=dt):
+                pl.semaphore_signal(far.at[n], inc=1, device_id=(g, t + dt), device_id_type=MESH)
+
+    def hear(n):
+        d = 2 << n
+        before = jnp.minimum(jnp.maximum(t - d + 1, 0), 1)
+        after = jnp.minimum(jnp.maximum(T - t - d, 0), 1)
+        pl.semaphore_wait(far.at[n], before + after)
 
     phase("loads")
     local(iblk, BI.at[1], L_BLK)
@@ -170,7 +180,7 @@
 
     phase("barrier")
     wide = 1 + jnp.minimum(t, 1) + jnp.minimum(T - 1 - t, 1)
-    pl.semaphore_wait(barrier, G * wide - 1 + len(peers2))
+    pl.semaphore_wait(barrier, G * wide - 1)
 
     phase("sends")
     left, right, up, down = (g, t - 1), (g, t + 1), (g - 1, t), (g + 1, t)
@@ -379,6 +389,7 @@
     def _():
         wait_rows(rs.at[R_IR], 2 * 8 * 8)
 
+    tell(0)
     quarter = lane // 32
     for c in range(2):
         ends = [[zero, zero], [zero, zero]]
@@ -508,6 +519,9 @@
             paint(WET, 16 + 64 * q + 8 * b, mid, b)
     paint(WET, OR + 16, ends[1], 2)
 
+    hear(0)
+    tell(1)
+
     def static(c, r):
         rr = pl.ds(r, 8)
         for j in range(NT):
@@ -578,6 +592,10 @@
                 wait_rows(rs.at[R_F + c], 2 * (IR + 8) * LT)
 
         phase("prepare")
+        @pl.when(turn == 0)
+        def _():
+            hear(1)
+            tell(2)
         static(c, 8)
         static(c, IR + 16)
 
@@ -657,6 +675,10 @@
         lax.fori_loop(0, NSUB, subcycle, 0)
 
         phase("diverge")
+        @pl.when(turn == 0)
+        def _():
+            hear(2)
+            tell(3)
         prev = [zero] * NT
         pack = zero
         for i in range(IR // 8):
@@ -921,6 +943,7 @@
     for k in range(1, 8):
         tile = tile + L1[k]
     phase("red2")
+    hear(3)
     L2[mine2] = tile
     for dev in peers2:
         send(L2.at[mine2], L2.at[mine2], S_2, R_2, dev)
@@ -1019,6 +1042,7 @@
         vm(G, LT, IR, 128), vm(G, 2, 8, 128), vm(LT, 8, 128), vm(2, 8, 128),
         vm(8, 8, 128), vm(T // 2, 8, 128), vm(6, 8, 128), vm(DUMMY, 128),
         pltpu.SemaphoreType.DMA((N_R,)), pltpu.SemaphoreType.DMA((N_S,)), pltpu.SemaphoreType.DMA((N_L,)),
+        pltpu.SemaphoreType.REGULAR((4,)),
     ]
     hbm = pl.BlockSpec(memory_space=pltpu.HBM)
     vmem = pl.BlockSpec(memory_space=pltpu.VMEM)

time: 51.6 us -> 51.7 us (level)
  no operation moved by 1% of the time
where the time goes in v6:
time: 51.7 us; the launch traced here: 51.6 us
  Pallas kernels  50.9 us (98%)
  between operations  0.64 us (1%)
    pallas_call x1, Pallas kernels, shards(): pl.pallas_call(functools.partial(kernel, T), out_shape=(vm(2, *ice), vm(3...  49.6 us
    pallas_call x1, Pallas kernels, shards(): pl.pallas_call(deliver, out_shape=(jax.ShapeDtypeStruct((OR, 128 * LT), F...  1.32 us

profile of v6, /device:TPU:1, one launch (start us, length us, event | category | flops | bytes accessed | tf_op | source)
XLA Modules:
  0.0 51.6 jit_solution(14525730968191346207)
XLA Ops:
  0.6 49.6 %shard_map.121 = (f32[2,2,5,104,128]{4,3,2,1,0:T(8,128)S(1)}, f32[3,2,5,104,128]{4,3,2,1,0:T(8,128)S(1)}, f32[4,256,128]{2,1,0:T(8,128)S(1)}) custom-call(f32[256,512]{1,0:T(8,128)} %base.1, f32[256,512]{1,0:T(8,128)} %depth.1, f32[256,512]{1,0:T(8,128)} %ssh.1, f32[2,256,512]{2,1,0:T(8,128)} %cur.1, s32[32,64]{1,0:T(8,128)} %land.1, f32[2,64,512]{2,1,0:T(8,128)} %thick.1, ...), custom_call_target="tpu_custom_call" | custom-call | tf_op jit(solution)/shard_map/pallas_call | solution.py:1049
  50.2 1.3 %shard_map.122 = (f32[256,512]{1,0:T(8,128)}, f32[2,2,64,512]{3,2,1,0:T(8,128)}, f32[3,2,64,512]{3,2,1,0:T(8,128)}) custom-call(f32[2,2,5,104,128]{4,3,2,1,0:T(8,128)S(1)} %get-tuple-element.6.V, f32[3,2,5,104,128]{4,3,2,1,0:T(8,128)S(1)} %get-tuple-element.7.S, f32[4,256,128]{2,1,0:T(8,128)S(1)} %get-tuple-element.8.OUT), custom_call_target="tpu_custom_call" | custom-call | tf_op jit(solution)/shard_map/pallas_call | solution.py:1058

commit v7 on v5

--- a/solution.py
+++ b/solution.py
@@ -856,8 +856,8 @@
         (functools.partial(krylov, Y1, Y2, V2), (3, 4)),
         (krylov3, (5,)),
     )
-    start = jnp.where(g == 0, 13, jnp.where(g == G - 1, 5, 17))
-    end = jnp.where(g == 0, 29, jnp.where(g == G - 1, 21, 17))
+    start = jnp.where(g == 0, 15, jnp.where(g == G - 1, 7, 17))
+    end = jnp.where(g == 0, 27, jnp.where(g == G - 1, 19, 17))
 
     def row_of(group):
         return pl.multiple_of(8 * group + 8, 8)
@@ -876,8 +876,8 @@
         @pl.when(is_owner)
         def _(some=some, into=into):
             acc = (zero,) * len(into)
-            acc = lax.fori_loop(0, (start - 1) // 4, functools.partial(some, first=1, count=4), acc)
-            acc = lax.fori_loop(0, (33 - end) // 4, functools.partial(some, first=end, count=4), acc)
+            acc = lax.fori_loop(0, (start - 1) // 2, functools.partial(some, first=1, count=2), acc)
+            acc = lax.fori_loop(0, (33 - end) // 2, functools.partial(some, first=end, count=2), acc)
             for k, m in zip(into, acc):
                 MOM[k] = m
 
@@ -902,7 +902,7 @@
     def _():
         for body, into in sweeps:
             acc = (zero,) * len(into)
-            for m in range(16):
+            for m in range(12):
                 acc = body(row_of(start + m), acc)
             for k, m in zip(into, acc):
                 MOM[k] = MOM[k] + m

time: 51.6 us -> 51.5 us (level)
  no operation moved by 1% of the time
where the time goes in v7:
time: 51.5 us; the launch traced here: 51.4 us
  Pallas kernels  50.8 us (99%)
  between operations  0.64 us (1%)
    pallas_call x1, Pallas kernels, shards(): pl.pallas_call(functools.partial(kernel, T), out_shape=(vm(2, *ice), vm(3...  49.4 us
    pallas_call x1, Pallas kernels, shards(): pl.pallas_call(deliver, out_shape=(jax.ShapeDtypeStruct((OR, 128 * LT), F...  1.32 us

profile of v7, /device:TPU:1, one launch (start us, length us, event | category | flops | bytes accessed | tf_op | source)
XLA Modules:
  0.0 51.4 jit_solution(1349130048270452265)
XLA Ops:
  0.6 49.4 %shard_map.121 = (f32[2,2,5,104,128]{4,3,2,1,0:T(8,128)S(1)}, f32[3,2,5,104,128]{4,3,2,1,0:T(8,128)S(1)}, f32[4,256,128]{2,1,0:T(8,128)S(1)}) custom-call(f32[256,512]{1,0:T(8,128)} %base.1, f32[256,512]{1,0:T(8,128)} %depth.1, f32[256,512]{1,0:T(8,128)} %ssh.1, f32[2,256,512]{2,1,0:T(8,128)} %cur.1, s32[32,64]{1,0:T(8,128)} %land.1, f32[2,64,512]{2,1,0:T(8,128)} %thick.1, ...), custom_call_target="tpu_custom_call" | custom-call | tf_op jit(solution)/shard_map/pallas_call | solution.py:1025
  50.1 1.3 %shard_map.122 = (f32[256,512]{1,0:T(8,128)}, f32[2,2,64,512]{3,2,1,0:T(8,128)}, f32[3,2,64,512]{3,2,1,0:T(8,128)}) custom-call(f32[2,2,5,104,128]{4,3,2,1,0:T(8,128)S(1)} %get-tuple-element.6.V, f32[3,2,5,104,128]{4,3,2,1,0:T(8,128)S(1)} %get-tuple-element.7.S, f32[4,256,128]{2,1,0:T(8,128)S(1)} %get-tuple-element.8.OUT), custom_call_target="tpu_custom_call" | custom-call | tf_op jit(solution)/shard_map/pallas_call | solution.py:1034
